TPU v7x, 32 devices: a whole 2x2x4 slice. The times are simulated.
32 devices in a mesh: dp: 8 (over y, x, core), mp: 4 (over z).
Axes of the slice: x: 2, y: 2, z: 4, core: 2. Of those that a mesh axis runs over, the one named last changes fastest.
Arguments:
- tokens: bfloat16 [5120, 768], P('dp'), may hold values from -6 to 6
- segment_ids: int32 [8, 640], P('dp'), may hold values from 0 to 3, never falling along the last dimension, each value on 1 to 320 neighbouring positions
- token_types: int32 [8, 640], P('dp'), may hold values 0 or 1
- q_weight: bfloat16 [4, 768, 768], P(None, None, 'mp'), may hold values from -0.21875 to 0.21875
- k_weight: bfloat16 [768, 768], P(None, 'mp'), may hold values from -0.21875 to 0.21875
- v_weight: bfloat16 [768, 768], P(None, 'mp'), may hold values from -0.21875 to 0.21875
- o_weight: bfloat16 [768, 768], P('mp'), may hold values from -2.5 to 2.5
- o_bias: float32 [768], replicated, may hold values from -1.5 to 1.5
- norm1_gain: float32 [768], replicated, may hold values from 0.25 to 1.75
- norm1_shift: float32 [768], replicated, may hold values from -1.5 to 1.5
- in_weight: bfloat16 [768, 3072], P(None, 'mp'), may hold values from -0.21875 to 0.21875
- in_bias: float32 [3072], P('mp'), may hold values from -1.5 to 1.5
- out_weight: bfloat16 [3072, 768], P('mp'), may hold values from -0.109375 to 0.109375
- out_bias: float32 [768], replicated, may hold values from -1.5 to 1.5
- norm2_gain: float32 [768], replicated, may hold values from 0.25 to 1.75
- norm2_shift: float32 [768], replicated, may hold values from -1.5 to 1.5
- cotangent: bfloat16 [5120, 768], P('dp'), may hold values from -6 to 6
Outputs:
- layer_out: bfloat16 [5120, 768], P('dp')
- tokens_grad: bfloat16 [5120, 768], P('dp')
- q_grad: float32 [4, 768, 768], P(None, 'dp', 'mp')
- k_grad: float32 [768, 768], P('dp', 'mp')
- v_grad: float32 [768, 768], P('dp', 'mp')
- o_grad: float32 [768, 768], P('mp', 'dp')
- o_bias_grad: float32 [768], replicated
- norm1_gain_grad: float32 [768], replicated
- norm1_shift_grad: float32 [768], replicated
- in_grad: float32 [768, 3072], P('dp', 'mp')
- in_bias_grad: float32 [3072], P('mp')
- out_grad: float32 [3072, 768], P('mp', 'dp')
- out_bias_grad: float32 [768], replicated
- norm2_gain_grad: float32 [768], replicated
- norm2_shift_grad: float32 [768], replicated
Inputs may be any that keep to these rules, and one draw needn't show every extreme that they name: `segment_ids`: a sequence's rows with equal ids form one run.
All inputs are finite; a program needn't handle non-finite values. No bound on the sum of `token_types` on one device may be relied on, other than what follows from the above.
Results may differ from a plain program's by a relative error of at most 0.019.
Values may be sent and summed in bfloat16 or wider, within the bound.
A program may use at most 128 MiB of HBM per device.

v0:
```python
import jax
import jax.numpy as jnp
from jax import lax
from jax.sharding import PartitionSpec as P

HD = 64


norm_epsilon = 1e-05


def layer_norm(inputs, gain, shift):
    average = jnp.mean(inputs, axis=-1, keepdims=True)
    centred = inputs - average
    spread = jnp.mean(centred * centred, axis=-1, keepdims=True)
    return centred * lax.rsqrt(spread + norm_epsilon) * gain + shift


def gelu_exact(inputs):
    return jax.nn.gelu(inputs, approximate=False)


def matmul(left, right):
    return jnp.dot(left, right, preferred_element_type=jnp.float32)


def local(
    tokens,
    segment_ids,
    token_types,
    q_weight,
    k_weight,
    v_weight,
    o_weight,
    o_bias,
    norm1_gain,
    norm1_shift,
    in_weight,
    in_bias,
    out_weight,
    out_bias,
    norm2_gain,
    norm2_shift,
    cotangent,
):
    row_count = tokens.shape[0]
    groups, length = segment_ids.shape
    local_width = k_weight.shape[1]
    head_count = local_width // HD
    score_scale = HD ** (-0.5)
    entity = token_types == 1
    chooser = entity[:, :, None, None]
    key_entity = entity[:, None, None, :]
    same_doc = (segment_ids[:, :, None] == segment_ids[:, None, :])[:, None]
    share_rows = row_count // lax.axis_size("mp")
    row_offset = lax.axis_index("mp") * share_rows
    queries = jnp.einsum(
        "rd,tdc->trc", tokens, q_weight, preferred_element_type=jnp.float32
    ).astype(jnp.bfloat16)
    keys = matmul(tokens, k_weight).astype(jnp.bfloat16)
    values = matmul(tokens, v_weight).astype(jnp.bfloat16)
    query_four = queries.reshape(4, groups, length, head_count, HD)
    query_word = jnp.where(chooser, query_four[2], query_four[0])
    query_ent = jnp.where(chooser, query_four[3], query_four[1])
    key_heads = keys.reshape(groups, length, head_count, HD)
    value_heads = values.reshape(groups, length, head_count, HD)

    def scores_now():
        raw_word = jnp.einsum(
            "gqhc,gkhc->ghqk", query_word, key_heads, preferred_element_type=jnp.float32
        )
        raw_ent = jnp.einsum(
            "gqhc,gkhc->ghqk", query_ent, key_heads, preferred_element_type=jnp.float32
        )
        raw_all = jnp.where(key_entity, raw_ent, raw_word)
        return jnp.where(same_doc, raw_all * score_scale, -1000000000.0)

    scores = scores_now()
    highest = jnp.max(scores, axis=-1, keepdims=True)
    log_total = highest + jnp.log(jnp.sum(jnp.exp(scores - highest), axis=-1, keepdims=True))
    attention_low = jnp.exp(scores - log_total).astype(jnp.bfloat16)
    mixed = jnp.einsum(
        "ghqk,gkhc->gqhc", attention_low, value_heads, preferred_element_type=jnp.float32
    )
    mixed = mixed.reshape(row_count, local_width).astype(jnp.bfloat16)
    token_wide = tokens.astype(jnp.float32)
    branch = lax.psum(matmul(mixed, o_weight), "mp") + o_bias
    hidden, norm1_pull = jax.vjp(layer_norm, token_wide + branch, norm1_gain, norm1_shift)
    hidden_low = hidden.astype(jnp.bfloat16)
    inner_pre = matmul(hidden_low, in_weight) + in_bias
    activated, gelu_pull = jax.vjp(gelu_exact, inner_pre)
    activated_low = activated.astype(jnp.bfloat16)
    ffn_out = (
        lax.psum(matmul(activated_low, out_weight).astype(jnp.bfloat16), "mp").astype(jnp.float32)
        + out_bias
    )
    result, norm2_pull = jax.vjp(layer_norm, hidden + ffn_out, norm2_gain, norm2_shift)
    layer_out = result.astype(jnp.bfloat16)
    d_res2, d_gain2, d_shift2 = norm2_pull(cotangent.astype(jnp.float32))
    d_out_bias = jnp.sum(d_res2, axis=0)
    grad_ffn = d_res2.astype(jnp.bfloat16)
    d_out_weight = matmul(activated_low.T, grad_ffn)
    (d_inner,) = gelu_pull(matmul(grad_ffn, out_weight.T))
    d_in_bias = jnp.sum(d_inner, axis=0)
    inner_low = d_inner.astype(jnp.bfloat16)
    d_in_weight = matmul(hidden_low.T, inner_low)
    d_hidden = d_res2 + lax.psum(matmul(inner_low, in_weight.T).astype(jnp.bfloat16), "mp").astype(
        jnp.float32
    )
    d_res1, d_gain1, d_shift1 = norm1_pull(d_hidden)
    d_o_bias = jnp.sum(d_res1, axis=0)
    grad_branch = d_res1.astype(jnp.bfloat16)
    d_o_weight = matmul(mixed.T, grad_branch)
    d_mixed = matmul(grad_branch, o_weight.T).astype(jnp.bfloat16)
    mixed_heads = d_mixed.reshape(groups, length, head_count, HD)
    attention = jnp.exp(scores_now() - log_total)
    d_probs = jnp.einsum(
        "gqhc,gkhc->ghqk", mixed_heads, value_heads, preferred_element_type=jnp.float32
    )
    d_values = jnp.einsum(
        "ghqk,gqhc->gkhc",
        attention.astype(jnp.bfloat16),
        mixed_heads,
        preferred_element_type=jnp.float32,
    )
    row_delta = jnp.sum(attention * d_probs, axis=-1, keepdims=True)
    d_raw = (attention * (d_probs - row_delta) * score_scale).astype(jnp.bfloat16)
    nothing = jnp.zeros_like(d_raw)
    raw_word = jnp.where(key_entity, nothing, d_raw)
    raw_ent = jnp.where(key_entity, d_raw, nothing)
    d_query_word = jnp.einsum(
        "ghqk,gkhc->gqhc", raw_word, key_heads, preferred_element_type=jnp.float32
    )
    d_query_ent = jnp.einsum(
        "ghqk,gkhc->gqhc", raw_ent, key_heads, preferred_element_type=jnp.float32
    )
    d_keys = jnp.einsum(
        "ghqk,gqhc->gkhc", raw_word, query_word, preferred_element_type=jnp.float32
    ) + jnp.einsum("ghqk,gqhc->gkhc", raw_ent, query_ent, preferred_element_type=jnp.float32)
    empty_rows = jnp.zeros_like(d_query_word)
    d_queries = (
        jnp.stack(
            [
                jnp.where(chooser, empty_rows, d_query_word),
                jnp.where(chooser, empty_rows, d_query_ent),
                jnp.where(chooser, d_query_word, empty_rows),
                jnp.where(chooser, d_query_ent, empty_rows),
            ]
        )
        .reshape(4, row_count, local_width)
        .astype(jnp.bfloat16)
    )
    d_keys_low = d_keys.reshape(row_count, local_width).astype(jnp.bfloat16)
    d_values_low = d_values.reshape(row_count, local_width).astype(jnp.bfloat16)
    d_q_weight = jnp.einsum("rd,trc->tdc", tokens, d_queries, preferred_element_type=jnp.float32)
    d_k_weight = matmul(tokens.T, d_keys_low)
    d_v_weight = matmul(tokens.T, d_values_low)
    res_rows = lax.dynamic_slice_in_dim(d_res1, row_offset, share_rows, 0)
    total = jnp.einsum("trc,tdc->rd", d_queries, q_weight, preferred_element_type=jnp.float32)
    grad_rows = (
        res_rows
        + lax.psum_scatter(
            (total + matmul(d_keys_low, k_weight.T) + matmul(d_values_low, v_weight.T)).astype(
                jnp.bfloat16
            ),
            "mp",
            scatter_dimension=0,
            tiled=True,
        ).astype(jnp.float32)
    ).astype(jnp.bfloat16)
    tokens_grad = lax.all_gather(grad_rows, "mp", axis=0, tiled=True)
    d_q_weight, d_k_weight, d_v_weight, d_o_weight, d_in_weight, d_out_weight = (
        lax.psum_scatter(d_q_weight, "dp", scatter_dimension=1, tiled=True),
        lax.psum_scatter(d_k_weight, "dp", scatter_dimension=0, tiled=True),
        lax.psum_scatter(d_v_weight, "dp", scatter_dimension=0, tiled=True),
        lax.psum_scatter(d_o_weight, "dp", scatter_dimension=1, tiled=True),
        lax.psum_scatter(d_in_weight, "dp", scatter_dimension=0, tiled=True),
        lax.psum_scatter(d_out_weight, "dp", scatter_dimension=1, tiled=True),
    )
    d_o_bias, d_gain1, d_shift1, d_in_bias, d_out_bias, d_gain2, d_shift2 = lax.psum(
        (d_o_bias, d_gain1, d_shift1, d_in_bias, d_out_bias, d_gain2, d_shift2), "dp"
    )
    return (
        layer_out,
        tokens_grad,
        d_q_weight,
        d_k_weight,
        d_v_weight,
        d_o_weight,
        d_o_bias,
        d_gain1,
        d_shift1,
        d_in_weight,
        d_in_bias,
        d_out_weight,
        d_out_bias,
        d_gain2,
        d_shift2,
    )


def solution(mesh):
    return jax.shard_map(
        local,
        mesh=mesh,
        in_specs=(
            P("dp", None),
            P("dp", None),
            P("dp", None),
            P(None, None, "mp"),
            P(None, "mp"),
            P(None, "mp"),
            P("mp", None),
            P(),
            P(),
            P(),
            P(None, "mp"),
            P("mp"),
            P("mp", None),
            P(),
            P(),
            P(),
            P("dp", None),
        ),
        out_specs=(
            P("dp", None),
            P("dp", None),
            P(None, "dp", "mp"),
            P("dp", "mp"),
            P("dp", "mp"),
            P("mp", "dp"),
            P(),
            P(),
            P(),
            P("dp", "mp"),
            P("mp"),
            P("mp", "dp"),
            P(),
            P(),
            P(),
        ),
        check_vma=False,
    )
```

profile of v0, /device:TPU:0, one launch (start us, length us, event | category | flops | bytes accessed | tf_op | source)
XLA Modules:
  0.0 547.3 jit_solution(5020968630286662695)
XLA Ops:
  12.0 2.4 fusion.19
  22.2 84.7 %all-reduce.5.cloned.1.call-done = f32[640,768]{1,0:T(8,128)} async-done(((f32[640,768]{1,0:T(8,128)}), f32[640,768]{1,0:T(8,128)}) %all-reduce.5.cloned.1.call-update) | async-done | bytes 1966096 | tf_op jit(solution)/shard_map/psum | solution.py:87
  106.9 2.1 fusion.75
  109.7 6.5 %multiply_convert_fusion.1 = (bf16[640,768]{1,0:T(8,128)(2,1)S(1)}, f32[640,768]{1,0:T(8,128)}, f32[640,768]{1,0:T(8,128)}) fusion(f32[768]{0:T(1024)S(1)} %copy-done.36, bf16[768,768]{1,0:T(8,128)(2,1)S(1)} %copy-done, f32[640,768]{1,0:T(8,128)S(1)} %get-tuple-element.70, f32[768]{0:T(1024)S(1)} %copy-done.31, f32[768]{0:T(1024)S(1)} %copy-done.27, ...), kind=kOutput, calls=%fused_computation.32 | convolution fusion | flops 789872640 | bytes 8075264 | tf_op jit(solution)/shard_map/dot_general | solution.py:24
  117.2 1.9 convolution_convert_fusion.1
  119.3 48.8 %all-reduce.7.cloned.1.call-done = bf16[640,768]{1,0:T(8,128)(2,1)} async-done(((bf16[640,768]{1,0:T(8,128)(2,1)}), bf16[640,768]{1,0:T(8,128)(2,1)}) %all-reduce.7.cloned.1.call-update) | async-done | bytes 983056 | tf_op jit(solution)/shard_map/psum | solution.py:94
  168.1 1.9 fusion.73
  177.6 1.9 convolution_convert_fusion
  179.6 49.1 %all-reduce.9.cloned.1.call-done = bf16[640,768]{1,0:T(8,128)(2,1)} async-done(((bf16[640,768]{1,0:T(8,128)(2,1)}), bf16[640,768]{1,0:T(8,128)(2,1)}) %all-reduce.9.cloned.1.call-update) | async-done | bytes 983056 | tf_op jit(solution)/shard_map/psum | solution.py:107
  228.7 3.1 multiply_reduce_fusion.1
  235.9 3.4 convolution_convert_fusion.3
  239.3 3.1 fusion.82
  242.4 9.7 %fusion.21 = f32[3,64,640]{2,1,0:T(8,128)} fusion(pred[640]{0:T(1024)(128)(4,1)S(1)} %compare_reduce_fusion, f32[3,640,640]{1,2,0:T(8,128)} %fusion.82, f32[3,640,640]{1,2,0:T(8,128)} %copy-done.2, f32[3,640]{1,0:T(4,128)S(1)} %log_add_fusion, bf16[640,3,64]{0,2,1:T(8,128)(2,1)S(1)} %bitcast.122, bf16[640,3,64]{0,2,1:T(8,128)(2,1)S(1)} %bitcast.120), kind=kOutput, calls=%fused_computation.69 | convolution fusion | flops 167242240 | bytes 10821760 | tf_op jit(solution)/shard_map/ghqk,gqhc->gkhc/dot_general | solution.py:137
  252.1 9.6 %convolution_bitcast_fusion.4 = bf16[1,3,64,640]{3,2,1,0:T(8,128)(2,1)} fusion(bf16[640,3,64]{0,2,1:T(8,128)(2,1)S(1)} %bitcast.104, pred[640]{0:T(1024)(128)(4,1)S(1)} %compare_reduce_fusion, f32[3,640,640]{1,2,0:T(8,128)} %fusion.82, f32[3,640,640]{1,2,0:T(8,128)} %copy-done.2, f32[3,640]{1,0:T(4,128)S(1)} %log_add_fusion), kind=kOutput, calls=%fused_computation.60 | convolution fusion | flops 167119360 | bytes 10330240 | tf_op jit(solution)/shard_map/ghqk,gkhc->gqhc/dot_general | solution.py:134
  263.7 9.3 %fusion.20 = bf16[3,64,640]{2,1,0:T(8,128)(2,1)S(1)} fusion(f32[3,64,640]{2,1,0:T(8,128)} %fusion.21, pred[640]{0:T(1024)(128)(4,1)S(1)} %compare_reduce_fusion, f32[3,640,640]{1,2,0:T(8,128)} %fusion.82, f32[3,640,640]{1,2,0:T(8,128)} %copy-done.2, f32[3,640]{1,0:T(4,128)S(1)} %log_add_fusion, bf16[640,3,64]{0,2,1:T(8,128)(2,1)} %bitcast.118, ...), kind=kOutput, calls=%fused_computation.63 | convolution fusion | flops 167488000 | bytes 11067520 | tf_op jit(solution)/shard_map/ghqk,gqhc->gkhc/dot_general | solution.py:139
  273.0 9.9 %select_convert_fusion.3 = (bf16[1,3,64,640]{3,2,1,0:T(8,128)(2,1)}, bf16[1,3,64,640]{3,2,1,0:T(8,128)(2,1)}, bf16[1,3,64,640]{3,2,1,0:T(8,128)(2,1)}, bf16[1,3,64,640]{3,2,1,0:T(8,128)(2,1)}) fusion(pred[640]{0:T(1024)(128)(4,1)S(1)} %compare_reduce_fusion, bf16[1,3,64,640]{3,2,1,0:T(8,128)(2,1)} %convolution_bitcast_fusion.4, ...), kind=kOutput, calls=%fused_computation.79 | convolution fusion | flops 167610880 | bytes 11313280 | tf_op jit(solution)/shard_map/ghqk,gkhc->gqhc/dot_general | solution.py:131
  284.5 3.6 fusion.12
  288.2 3.9 convolution_bitcast_fusion
  292.1 4.5 copy.56
  296.6 4.7 reshape.292
  302.6 2.2 copy.60
  304.9 2.2 convolution_bitcast_fusion.3
  307.1 2.4 copy.58
  309.6 4.2 fusion.64
  315.0 2.8 fusion.44
  317.8 24.7 %all-reduce = (f32[768]{0:T(1024)}, f32[768]{0:T(1024)}, f32[768]{0:T(1024)}, f32[768]{0:T(1024)}, f32[768]{0:T(1024)}, /*index=5*/f32[768]{0:T(1024)}, f32[768]{0:T(1024)}) all-reduce(f32[768]{0:T(1024)S(1)} %get-tuple-element.59, f32[768]{0:T(1024)S(1)} %get-tuple-element.45, ...), channel_id=1, replica_groups=mesh['dp'=8,'mp'=4] {'dp'}, use_global_device_ids=true, to_apply=%region_20.21 | all-reduce | flops 5376 | bytes 43008 | tf_op jit(solution)/shard_map/psum | solution.py:180
  345.4 19.8 %all_gather.3 = bf16[640,768]{1,0:T(8,128)(2,1)S(1)} all-gather(bf16[160,768]{1,0:T(8,128)(2,1)S(1)} %add_convert_fusion.2), channel_id=1, replica_groups=mesh['dp'=8,'mp'=4] {'mp'}, dimensions={0}, use_global_device_ids=true | all-gather | bytes 1228800 | tf_op jit(solution)/shard_map/all_gather | solution.py:171
  365.1 4.0 reduce-scatter.22.cloned.1.call-done
  371.2 36.6 %reduce-scatter.26.cloned.1.call-done = f32[96,192]{1,0:T(8,128)} async-done(((f32[768,192]{1,0:T(8,128)}), f32[96,192]{1,0:T(8,128)}) %reduce-scatter.26.cloned.1.call-update) | async-done | bytes 73744
  407.9 38.7 %reduce-scatter.24.cloned.1.call-done = f32[96,192]{1,0:T(8,128)} async-done(((f32[768,192]{1,0:T(8,128)}), f32[96,192]{1,0:T(8,128)}) %reduce-scatter.24.cloned.1.call-update) | async-done | bytes 73744
  446.6 46.3 %reduce-scatter.20.cloned.1.call-done = f32[768,96]{0,1:T(8,128)} async-done(((f32[768,768]{0,1:T(8,128)}), f32[768,96]{0,1:T(8,128)}) %reduce-scatter.20.cloned.1.call-update) | async-done | bytes 294928 | tf_op jit(solution)/shard_map/reduce_scatter | solution.py:178
  492.9 46.1 %reduce-scatter.18.cloned.1.call-done = f32[96,768]{1,0:T(8,128)} async-done(((f32[768,768]{1,0:T(8,128)}), f32[96,768]{1,0:T(8,128)}) %reduce-scatter.18.cloned.1.call-update) | async-done | bytes 294928 | tf_op jit(solution)/shard_map/reduce_scatter | solution.py:177
  (149 shorter events, 38.0 us)
Async XLA Ops:
  7.2 102.2 %copy-start = (bf16[768,768]{1,0:T(8,128)(2,1)S(1)}, bf16[768,768]{1,0:T(8,128)(2,1)}, u32[]{:S(2)}) copy-start(bf16[768,768]{1,0:T(8,128)(2,1)} %param.27) | copy-start | bytes 3538948
  7.2 4.8 copy-start.3
  7.2 4.5 copy-start.33
  7.2 99.6 %all-reduce.5.cloned.1.call-start = ((), (), s32[]{:S(2)}) async-start(), calls=%async_computation.7 | async-start | bytes 3932160 | tf_op jit(solution)/shard_map/psum | solution.py:87
  9.8 5.6 %copy-start.10 = (bf16[640,192]{0,1:T(8,128)(2,1)}, bf16[640,192]{0,1:T(8,128)(2,1)S(1)}, u32[]{:S(2)}) copy-start(bf16[640,192]{0,1:T(8,128)(2,1)S(1)} %convolution_convert_fusion.6) | copy-start | bytes 737284
  11.7 6.1 %copy-start.12 = (bf16[640,192]{0,1:T(8,128)(2,1)}, bf16[640,192]{0,1:T(8,128)(2,1)S(1)}, u32[]{:S(2)}) copy-start(bf16[640,192]{0,1:T(8,128)(2,1)S(1)} %convolution_convert_fusion.7) | copy-start | bytes 737284
  20.3 86.6 %copy-start.29 = (f32[768]{0:T(1024)S(1)}, f32[768]{0:T(1024)}, u32[]{:S(2)}) copy-start(f32[768]{0:T(1024)} %param.24) | copy-start | bytes 9220
  22.1 146.0 %all-reduce.7.cloned.1.call-start = ((), (), s32[]{:S(2)}) async-start(), calls=%async_computation.8 | async-start | bytes 1966080 | tf_op jit(solution)/shard_map/psum | solution.py:94
  109.7 7.5 %copy-start.34 = (bf16[768,768]{1,0:T(8,128)(2,1)S(1)}, bf16[768,768]{1,0:T(8,128)(2,1)}, u32[]{:S(2)}) copy-start(bf16[768,768]{1,0:T(8,128)(2,1)} %param.29) | copy-start | bytes 3538948
  117.2 50.9 %copy-start.30 = (f32[768]{0:T(1024)S(1)}, f32[768]{0:T(1024)}, u32[]{:S(2)}) copy-start(f32[768]{0:T(1024)} %param.30) | copy-start | bytes 9220
  119.1 109.6 %all-reduce.9.cloned.1.call-start = ((), (), s32[]{:S(2)}) async-start(), calls=%async_computation.9 | async-start | bytes 1966080 | tf_op jit(solution)/shard_map/psum | solution.py:107
  172.2 2.9 copy-start.44
  174.0 2.6 copy-start.6
  179.5 163.0 %reduce-scatter.28.cloned.1.call-start = ((), (), s32[]{:S(2)}) async-start(), calls=%async_computation.16 | async-start | bytes 884736
  228.7 3.1 copy-start.7
  228.7 3.1 copy-start.8
  235.9 3.4 copy-start.13
  239.3 3.1 copy-start.24
  239.3 3.1 copy-start.26
  242.4 9.7 %copy-start.11 = (bf16[640,192]{0,1:T(8,128)(2,1)S(1)}, bf16[640,192]{0,1:T(8,128)(2,1)}, u32[]{:S(2)}) copy-start(bf16[640,192]{0,1:T(8,128)(2,1)} %copy-done.10) | copy-start | bytes 737284
  252.1 9.9 %copy-start.17 = (bf16[768,192]{0,1:T(8,128)(2,1)S(1)}, bf16[768,192]{0,1:T(8,128)(2,1)}, u32[]{:S(2)}) copy-start(bf16[768,192]{0,1:T(8,128)(2,1)} %param.22) | copy-start | bytes 884740
  261.7 82.5 %reduce-scatter.16.cloned.1.call-start = ((), (), s32[]{:S(2)}) async-start(), calls=%async_computation.10 | async-start | bytes 1228800 | tf_op jit(solution)/shard_map/reduce_scatter | solution.py:162
  273.0 9.9 %copy-start.19 = (bf16[3,64,640]{2,1,0:T(8,128)(2,1)}, bf16[3,64,640]{2,1,0:T(8,128)(2,1)S(1)}, u32[]{:S(2)}) copy-start(bf16[3,64,640]{2,1,0:T(8,128)(2,1)S(1)} %fusion.20) | copy-start | bytes 737284
  273.0 9.9 %copy-start.18 = (bf16[768,192]{0,1:T(8,128)(2,1)S(1)}, bf16[768,192]{0,1:T(8,128)(2,1)}, u32[]{:S(2)}) copy-start(bf16[768,192]{0,1:T(8,128)(2,1)} %param.21) | copy-start | bytes 884740
  284.5 3.7 copy-start.4
  288.2 81.0 %reduce-scatter.22.cloned.1.call-start = ((), (), s32[]{:S(2)}) async-start(), calls=%async_computation.13 | async-start | bytes 2654208
  301.3 106.5 %reduce-scatter.26.cloned.1.call-start = ((), (), s32[]{:S(2)}) async-start(), calls=%async_computation.15 | async-start | bytes 884736
  304.9 141.7 %reduce-scatter.24.cloned.1.call-start = ((), (), s32[]{:S(2)}) async-start(), calls=%async_computation.14 | async-start | bytes 884736
  307.1 2.4 copy-start.40
  309.5 183.4 %reduce-scatter.20.cloned.1.call-start = ((), (), s32[]{:S(2)}) async-start(), calls=%async_computation.12 | async-start | bytes 2654208 | tf_op jit(solution)/shard_map/reduce_scatter | solution.py:178
  313.8 225.2 %reduce-scatter.18.cloned.1.call-start = ((), (), s32[]{:S(2)}) async-start(), calls=%async_computation.11 | async-start | bytes 2654208 | tf_op jit(solution)/shard_map/reduce_scatter | solution.py:177
  345.4 194.6 %copy-start.1 = (bf16[768,768]{1,0:T(8,128)(2,1)S(1)}, bf16[768,768]{1,0:T(8,128)(2,1)}, u32[]{:S(2)}) copy-start(bf16[768,768]{1,0:T(8,128)(2,1)} %param.27) | copy-start | bytes 3538948
  (23 other events, 29.0 us)
Sparse Core Ops, SparseCore 0:
  22.2 84.5 all-reduce.4
  119.2 48.8 all-reduce.6
  179.6 49.0 all-reduce.8
  261.8 34.1 reduce-scatter.27
  298.7 26.2 reduce-scatter.15
  328.2 40.9 reduce-scatter.21
  372.9 34.9 reduce-scatter.25
  411.6 34.9 reduce-scatter.23
  450.5 42.3 reduce-scatter.19
  496.7 42.3 reduce-scatter.17
where the time goes:
time: 555 us; the launch traced here: 547 us
  waiting for transfers between devices  355 us (64%)
  matrix products  90 us (16%)
  blocking collectives  44.5 us (8%)
  local copies, waits for them, and re-layouts  27.2 us (5%)
  between operations  15.1 us (3%)
  other arithmetic  14.8 us (3%)
    psum x1, waiting for transfers between devices, local(): branch = lax.psum(matmul(mixed, o_weight), 'mp') + o_bias  84.7 us
    unnamed x14, waiting for transfers between devices  79.5 us
    psum x1, waiting for transfers between devices, local(): lax.psum(matmul(inner_low, in_weight.T).astype(jnp.bfloat16), 'mp')  49.1 us
    psum x1, waiting for transfers between devices, local(): lax.psum(matmul(activated_low, out_weight).astype(jnp.bfloat16), 'mp')  48.8 us
    reduce_scatter x1, waiting for transfers between devices, local(): lax.psum_scatter(d_out_weight, 'dp', scatter_dimension=1, tiled=True)  46.3 us
    reduce_scatter x1, waiting for transfers between devices, local(): lax.psum_scatter(d_in_weight, 'dp', scatter_dimension=0, tiled=True)  46.1 us
    dot_general x14, matrix products, matmul(): return jnp.dot(left, right, preferred_element_type=jnp.float32)  30.4 us
    unnamed x98, local copies, waits for them, and re-layouts  27.1 us
  transfers between devices with their start and end apart: 10, of which 8 were waited for; matrix products, arithmetic and copies ran while one was open for 11% of the time, Pallas kernels for 0%

commit v1 on v0

v1 whole, which is shorter than its diff:
```python
import functools
import math
import operator
import types

import jax
import jax.numpy as jnp
from jax import lax
from jax.experimental import pallas as pl
from jax.experimental.pallas import tpu as pltpu
from jax.sharding import PartitionSpec as P

HD = 64
LINE = 4
HALVES = 2
CHUNK = 32
VMEM_LIMIT = 67043328

norm_epsilon = 1e-05


def remote(src, dst, send_sem, recv_sem, **axes):
    return pltpu.make_async_remote_copy(
        src_ref=src,
        dst_ref=dst,
        send_sem=send_sem,
        recv_sem=recv_sem,
        device_id=axes,
        device_id_type=pl.DeviceIdType.MESH,
    )


class LineReduce:
    def __init__(self, part, carry, single, summed, out, send, recv):
        self.part, self.carry, self.single, self.summed, self.out = part, carry, single, summed, out
        me = lax.axis_index("mp")
        self.me = me
        left = me < 2
        self.is_mid = jnp.logical_or(me == 1, me == 2)
        self.is_end = jnp.logical_not(self.is_mid)
        self.mid = jnp.where(left, 1, 2)
        self.end = jnp.where(left, 0, 3)
        self.far_mid = 3 - self.mid
        self.far_end = 3 - self.end
        self.send, self.recv = send, recv

    def end_sends(self):
        return (
            remote(self.part.at[self.far_end], self.carry.at[0], self.send.at[0], self.recv.at[2], mp=self.mid),
            remote(self.part.at[self.far_mid], self.carry.at[1], self.send.at[1], self.recv.at[3], mp=self.mid),
            remote(self.part.at[self.mid], self.single, self.send.at[2], self.recv.at[0], mp=self.mid),
        )

    def mid_sends(self):
        return (
            remote(self.part.at[self.end], self.single, self.send.at[0], self.recv.at[0], mp=self.end),
            remote(self.carry.at[0], self.summed, self.send.at[1], self.recv.at[1], mp=self.far_end),
            remote(self.carry.at[1], self.summed, self.send.at[2], self.recv.at[1], mp=self.far_mid),
        )

    def gather(self, block, slot, target):
        return remote(self.out.at[block], self.out.at[block], self.send.at[slot], self.recv.at[4 + block], mp=target)

    def start(self):
        @pl.when(self.is_end)
        def _():
            for copy in self.end_sends():
                copy.start()

        @pl.when(self.is_mid)
        def _():
            self.mid_sends()[0].start()

    def forward(self):
        @pl.when(self.is_mid)
        def _():
            sends = self.mid_sends()
            for i, block in ((0, self.far_end), (1, self.far_mid)):
                remote(self.carry.at[i], self.carry.at[i], self.send.at[0], self.recv.at[2 + i], mp=self.end).wait_recv()
                total = self.carry[i].astype(jnp.float32) + self.part[block].astype(jnp.float32)
                self.carry[i] = total.astype(jnp.bfloat16)
                sends[1 + i].start()

    def total(self):
        remote(self.single, self.single, self.send.at[0], self.recv.at[0], mp=self.mid).wait_recv()
        remote(self.summed, self.summed, self.send.at[0], self.recv.at[1], mp=self.mid).wait_recv()
        return (
            self.part[self.me].astype(jnp.float32)
            + self.single[...].astype(jnp.float32)
            + self.summed[...].astype(jnp.float32)
        )

    def spread(self):
        @pl.when(self.is_end)
        def _():
            self.gather(self.me, 3, self.mid).start()

        @pl.when(self.is_mid)
        def _():
            self.gather(self.me, 3, self.end).start()
            self.gather(self.me, 4, self.far_mid).start()

    def wait_block(self, block):
        self.gather(block, 3, self.mid).wait_recv()

    def relay(self):
        @pl.when(self.is_mid)
        def _():
            self.wait_block(self.end)
            self.gather(self.end, 5, self.far_mid).start()
            self.wait_block(self.far_mid)
            self.gather(self.far_mid, 6, self.end).start()
            self.wait_block(self.far_end)
            self.gather(self.far_end, 7, self.end).start()

    def arrive(self):
        @pl.when(self.is_end)
        def _():
            self.wait_block(self.mid)
            self.wait_block(self.far_mid)
            self.wait_block(self.far_end)

    def drain(self):
        @pl.when(self.is_end)
        def _():
            for copy in self.end_sends():
                copy.wait_send()
            self.gather(self.me, 3, self.mid).wait_send()

        @pl.when(self.is_mid)
        def _():
            for copy in self.mid_sends():
                copy.wait_send()
            for slot in range(3, 8):
                self.gather(self.me, slot, self.end).wait_send()


def line_scratch(rows, width):
    block = pltpu.VMEM((HALVES, rows, width), jnp.bfloat16)
    return [
        pltpu.VMEM((HALVES, LINE, rows, width), jnp.bfloat16),
        pltpu.VMEM((HALVES, 2, rows, width), jnp.bfloat16),
        block,
        block,
        pltpu.SemaphoreType.DMA((HALVES, 8)),
        pltpu.SemaphoreType.DMA((HALVES, 8)),
    ]


class LineGather:
    def __init__(self, place, send, recv, out):
        self.place, self.send, self.recv, self.out = place, send, recv, out

    def copy(self, block, slot, target):
        return remote(self.out(block), self.out(block), self.send.at[slot], self.recv.at[block], mp=target)

    def spread(self):
        at = self.place

        @pl.when(at.is_end)
        def _():
            self.copy(at.me, 0, at.mid).start()

        @pl.when(at.is_mid)
        def _():
            self.copy(at.me, 0, at.end).start()
            self.copy(at.me, 1, at.far_mid).start()

    def relay(self):
        at = self.place

        @pl.when(at.is_mid)
        def _():
            self.copy(at.end, 2, at.far_mid).wait_recv()
            self.copy(at.end, 2, at.far_mid).start()
            self.copy(at.far_mid, 3, at.end).wait_recv()
            self.copy(at.far_mid, 3, at.end).start()
            self.copy(at.far_end, 4, at.end).wait_recv()
            self.copy(at.far_end, 4, at.end).start()

    def arrive(self):
        at = self.place

        @pl.when(at.is_end)
        def _():
            self.copy(at.mid, 0, at.mid).wait_recv()
            self.copy(at.far_mid, 0, at.mid).wait_recv()
            self.copy(at.far_end, 0, at.mid).wait_recv()

    def drain(self):
        at = self.place

        @pl.when(at.is_end)
        def _():
            self.copy(at.me, 0, at.mid).wait_send()

        @pl.when(at.is_mid)
        def _():
            for slot in range(5):
                self.copy(at.me, slot, at.end).wait_send()


class Place:
    def __init__(self):
        me = lax.axis_index("mp")
        self.me = me
        self.is_mid = jnp.logical_or(me == 1, me == 2)
        self.is_end = jnp.logical_not(self.is_mid)
        left = me < 2
        self.mid = jnp.where(left, 1, 2)
        self.end = jnp.where(left, 0, 3)
        self.far_mid = 3 - self.mid
        self.far_end = 3 - self.end


class PlaneReduce:
    def __init__(self, grads, r1, sums, mid2, r2a, r2b, s3a, s3b, r3a, r3b, send, recv):
        self.grads, self.r1, self.sums, self.mid2 = grads, r1, sums, mid2
        self.r2a, self.r2b, self.s3a, self.s3b, self.r3a, self.r3b = r2a, r2b, s3a, s3b, r3a, r3b
        dp = lax.axis_index("dp")
        self.core, self.x, self.y = lax.rem(dp, 2), lax.rem(dp // 2, 2), dp // 4
        across = dp + 1 - 2 * self.core
        over_x = dp + 2 - 4 * self.x
        over_y = dp + 4 - 8 * self.y
        half = r2a.shape[2]
        self.low, self.high = pl.ds(0, half), pl.ds(half, grads.shape[2] - half)
        self.first = [
            remote(grads.at[2 * k + 1 - self.core], r1.at[k], send.at[k], recv.at[k], dp=across) for k in range(4)
        ]
        self.second = [
            remote(mid2.at[2 * j + 1 - self.x, :, self.low], r2a.at[j], send.at[4 + j], recv.at[4 + j], dp=over_x)
            for j in range(2)
        ] + [
            remote(mid2.at[2 * (1 - self.y) + j, :, self.high], r2b.at[j], send.at[6 + j], recv.at[6 + j], dp=over_y)
            for j in range(2)
        ]
        self.third = [
            remote(s3a, r3a, send.at[8], recv.at[8], dp=over_y),
            remote(s3b, r3b, send.at[9], recv.at[9], dp=over_x),
        ]

    def start(self):
        for copy in self.first:
            copy.start()

    def step_one(self):
        for copy in self.first:
            copy.wait_recv()

        def body(k, carry):
            total = self.grads[2 * k + self.core].astype(jnp.float32) + self.r1[k].astype(jnp.float32)
            self.sums[k] = total
            self.mid2[k] = total.astype(jnp.bfloat16)
            return carry

        lax.fori_loop(0, 4, body, 0)
        for copy in self.second:
            copy.start()

    def step_two(self):
        for copy in self.second:
            copy.wait_recv()
        x, y = self.x, self.y
        self.s3a[...] = (
            self.sums[2 * (1 - y) + x, :, self.low] + self.r2a[1 - y].astype(jnp.float32)
        ).astype(jnp.bfloat16)
        self.third[0].start()
        self.s3b[...] = (
            self.sums[2 * y + 1 - x, :, self.high] + self.r2b[1 - x].astype(jnp.float32)
        ).astype(jnp.bfloat16)
        self.third[1].start()

    def finish(self):
        x, y = self.x, self.y
        for copy in self.third:
            copy.wait_recv()
        own = self.sums.at[2 * y + x]
        own[:, self.low] = own[:, self.low] + self.r2a[y].astype(jnp.float32) + self.r3a[...].astype(jnp.float32)
        own[:, self.high] = own[:, self.high] + self.r2b[x].astype(jnp.float32) + self.r3b[...].astype(jnp.float32)
        for copy in self.first + self.second + self.third:
            copy.wait_send()
        return own


def plane_scratch(rows, width):
    half = (width // 128 + 1) // 2 * 128
    rest = width - half
    low = jnp.bfloat16
    return [
        pltpu.VMEM((4, rows, width), low),
        pltpu.VMEM((4, rows, width), jnp.float32),
        pltpu.VMEM((4, rows, width), low),
        pltpu.VMEM((2, rows, half), low),
        pltpu.VMEM((2, rows, rest), low),
        pltpu.VMEM((rows, half), low),
        pltpu.VMEM((rows, rest), low),
        pltpu.VMEM((rows, half), low),
        pltpu.VMEM((rows, rest), low),
        pltpu.SemaphoreType.DMA((10,)),
        pltpu.SemaphoreType.DMA((10,)),
    ]


def dot(left, right, left_dim=1, right_dim=0):
    return lax.dot_general(
        left, right, (((left_dim,), (right_dim,)), ((), ())), preferred_element_type=jnp.float32
    )


def rows_loop(start, count, body):
    def step(i, carry):
        body(pl.ds(pl.multiple_of(start + i * CHUNK, CHUNK), CHUNK))
        return carry

    lax.fori_loop(0, count // CHUNK, step, 0)


def fold(value):
    return jnp.sum(value.reshape(value.shape[0] // 8, 8, value.shape[1]), axis=0)


def row_mean(value):
    return jnp.mean(value, axis=-1, keepdims=True)


def layer_kernel(planar, layout, *refs):
    r = types.SimpleNamespace(**functools.reduce(operator.or_, jax.tree.unflatten(layout, refs)))
    tokens, rows, width = r.tokens, r.tokens.shape[0], r.tokens.shape[1]
    local_width = r.k_weight.shape[0]
    heads = local_width // HD
    pair = 2 * HD
    hidden_width = r.in_weight.shape[1]
    half_rows = rows // HALVES
    block_rows = half_rows // LINE
    low, wide = jnp.bfloat16, jnp.float32
    at = Place()
    me = at.me
    dp = lax.axis_index("dp")
    core = lax.rem(dp, 2)
    across = dp + 1 - 2 * core

    barrier = pltpu.get_barrier_semaphore()
    peers = [{"mp": lax.rem(me + step, LINE)} for step in range(1, LINE)] + [{"dp": across}]
    if planar:
        x, y = lax.rem(dp // 2, 2), dp // 4
        over_x, over_y = dp + 2 - 4 * x, dp + 4 - 8 * y
        peers += [{"dp": over_x}, {"dp": over_y}]
    for peer in peers:
        pl.semaphore_signal(barrier, inc=1, device_id=peer, device_id_type=pl.DeviceIdType.MESH)
    pl.semaphore_wait(barrier, len(peers))

    ow, ow_send, ow_recv = r.ow, r.ow_send, r.ow_recv
    share = local_width // 2
    mine, other = pl.ds(core * share, share), pl.ds((1 - core) * share, share)
    ow_line = []
    for step in range(1, LINE):
        ow_line.append(
            remote(
                r.o_weight.at[mine],
                ow.at[me, mine],
                ow_send.at[step - 1],
                ow_recv.at[step - 1],
                mp=lax.rem(me + step, LINE),
            )
        )
    for copy in ow_line:
        copy.start()
    ow_swap = []
    for step in range(1, LINE):
        source = lax.rem(me + LINE - step, LINE)
        ow_swap.append(
            remote(ow.at[source, mine], ow.at[source, mine], ow_send.at[2 + step], ow_recv.at[2 + step], dp=across)
        )

    wa, wb, wk = r.wa, r.wb, r.wk
    for h in range(heads):
        cols = slice(h * HD, (h + 1) * HD)
        both = slice(h * pair, (h + 1) * pair)
        wa[both, :] = jnp.concatenate([r.q_weight[0, cols, :], r.q_weight[1, cols, :]], axis=0)
        wb[both, :] = jnp.concatenate([r.q_weight[2, cols, :], r.q_weight[3, cols, :]], axis=0)
        key_part = r.k_weight[cols, :]
        wk[both, :] = jnp.concatenate([key_part, key_part], axis=0)
    kind_wide, seg_wide = r.kind_wide, r.seg_wide
    kind_wide[...] = jnp.broadcast_to(r.kind_col[...], kind_wide.shape)
    seg_wide[...] = jnp.broadcast_to(r.seg_col[...], seg_wide.shape)
    qcat, kcat, vt = r.qcat, r.kcat, r.vt
    tok = tokens[...]
    q_plain = dot(tok, wa[...], 1, 1)
    q_entity = dot(tok, wb[...], 1, 1)
    entity = kind_wide[...] == 1
    upper = lax.broadcasted_iota(jnp.int32, (rows, pair), 1) >= HD
    for h in range(heads):
        both = slice(h * pair, (h + 1) * pair)
        qcat[:, both] = jnp.where(entity, q_entity[:, both], q_plain[:, both]).astype(low)
    keys = dot(tok, wk[...], 1, 1)
    for h in range(heads):
        both = slice(h * pair, (h + 1) * pair)
        kcat[:, both] = jnp.where(entity == upper, keys[:, both], 0.0).astype(low)
    vt[...] = dot(r.v_weight[...], tok, 1, 1).astype(low)

    st, pt, mx = r.st, r.pt, r.mx
    gathers = []
    scale = HD ** (-0.5)
    lane_tiles = rows // 128
    for h in range(heads):
        both = slice(h * pair, (h + 1) * pair)
        st[...] = dot(kcat[:, both], qcat[:, both], 1, 1)

        def soften(i, carry, h=h):
            cols = pl.ds(pl.multiple_of(i * 128, 128), 128)
            scores = jnp.where(seg_wide[...] == r.seg_row[:, cols], st[:, cols] * scale, -1000000000.0)
            shifted = jnp.exp(scores - jnp.max(scores, axis=0, keepdims=True))
            total = jnp.sum(shifted, axis=0, keepdims=True)
            pt[h, :, cols] = (shifted * (1.0 / total)).astype(low)
            return carry

        lax.fori_loop(0, lane_tiles, soften, 0)
        mx[me, h] = dot(vt[h * HD : (h + 1) * HD, :], pt[h]).astype(low)
        gather = LineGather(at, r.mx_send.at[h], r.mx_recv.at[h], lambda block, h=h: mx.at[block, h])
        gathers.append(gather)
        gather.spread()
        if h:
            gathers[h - 1].relay()
    for copy in ow_line:
        copy.wait_recv()
    for copy in ow_swap:
        copy.start()
    ow[me] = r.o_weight[...]
    tok_t = r.tok_t
    tok_t[...] = tokens[...].T
    gathers[-1].relay()
    for gather in gathers:
        gather.arrive()
    for copy in ow_swap:
        copy.wait_recv()

    xh1, rstd1, hl = r.xh1, r.rstd1, r.hl
    xh1[...] = dot(mx[...].reshape(LINE * local_width, rows), ow[...].reshape(LINE * local_width, width), 0, 0)

    def first_norm(at_rows):
        value = xh1[at_rows, :] + tokens[at_rows, :].astype(wide) + r.o_bias[...]
        centred = value - row_mean(value)
        scaled = lax.rsqrt(row_mean(centred * centred) + norm_epsilon)
        normal = centred * scaled
        xh1[at_rows, :] = normal
        rstd1[at_rows, :] = jnp.broadcast_to(scaled, (CHUNK, 128))
        hl[at_rows, :] = (normal * r.gain1[...] + r.shift1[...]).astype(low)

    act, gp, dr2, gf, il, tmp = r.act, r.gp, r.dr2, r.gf, r.il, r.tmp
    acc = r.acc
    acc[...] = jnp.zeros_like(acc)

    def make_lines(parts, out):
        part, carry, single, summed, send, recv = parts
        return [
            LineReduce(part.at[h], carry.at[h], single.at[h], summed.at[h], out.at[h], send.at[h], recv.at[h])
            for h in range(HALVES)
        ]

    ffn = make_lines(r.ffn, r.ffn_out)
    back = make_lines(r.back, r.back_out)
    grad = make_lines(r.grad, r.tokens_grad)

    def put_part(line, value):
        line.part[...] = value.astype(low).reshape(line.part.shape)

    root_half = math.sqrt(0.5)
    density = 1.0 / math.sqrt(2.0 * math.pi)

    def forward_half(h):
        here = pl.ds(h * half_rows, half_rows)
        rows_loop(h * half_rows, half_rows, first_norm)
        gp[here, :] = dot(hl[here, :], r.in_weight[...])

        def activate(at_rows):
            inner = gp[at_rows, :] + r.in_bias[...]
            gate = 0.5 + 0.5 * lax.erf(inner * root_half)
            act[at_rows, :] = (inner * gate).astype(low)
            gp[at_rows, :] = gate + inner * (density * jnp.exp(-0.5 * inner * inner))

        rows_loop(h * half_rows, half_rows, activate)
        put_part(ffn[h], dot(act[here, :], r.out_weight[...]))
        ffn[h].start()

    def settle(line):
        line.forward()
        line.out[me] = line.total().astype(low)
        line.spread()

    def backward_half(h):
        here = pl.ds(h * half_rows, half_rows)
        start = h * half_rows

        def second_norm(at_rows, from_rows):
            value = xh1[at_rows, :] * r.gain1[...] + r.shift1[...]
            value = value + tmp[from_rows, :] + r.out_bias[...]
            centred = value - row_mean(value)
            scaled = lax.rsqrt(row_mean(centred * centred) + norm_epsilon)
            normal = centred * scaled
            r.layer_out[at_rows, :] = (normal * r.gain2[...] + r.shift2[...]).astype(low)
            cot = r.cotangent[at_rows, :].astype(wide)
            acc[6] += fold(cot)
            acc[5] += fold(cot * normal)
            inside = cot * r.gain2[...]
            grad_in = scaled * (inside - row_mean(inside) - normal * row_mean(inside * normal))
            acc[4] += fold(grad_in)
            dr2[at_rows, :] = grad_in
            gf[at_rows, :] = grad_in.astype(low)

        def norm_step(i, carry):
            at_rows = pl.ds(pl.multiple_of(start + i * CHUNK, CHUNK), CHUNK)
            from_rows = pl.ds(pl.multiple_of(i * CHUNK, CHUNK), CHUNK)
            second_norm(at_rows, from_rows)
            return carry

        tmp[...] = ffn[h].out[...].reshape(half_rows, width).astype(wide)
        lax.fori_loop(0, half_rows // CHUNK, norm_step, 0)
        tmp[...] = dot(gf[here, :], r.out_weight[...], 1, 1)

        def inner_step(i, carry):
            at_rows = pl.ds(pl.multiple_of(start + i * CHUNK, CHUNK), CHUNK)
            from_rows = pl.ds(pl.multiple_of(i * CHUNK, CHUNK), CHUNK)
            d_inner = tmp[from_rows, :] * gp[at_rows, :]
            acc[3] += fold(d_inner)
            il[at_rows, :] = d_inner.astype(low)
            return carry

        lax.fori_loop(0, half_rows // CHUNK, inner_step, 0)
        put_part(back[h], dot(il[here, :], r.in_weight[...], 1, 1))
        back[h].start()

    gb = r.gb

    def last_norm(h):
        start = h * half_rows

        def step(i, carry):
            at_rows = pl.ds(pl.multiple_of(start + i * CHUNK, CHUNK), CHUNK)
            from_rows = pl.ds(pl.multiple_of(i * CHUNK, CHUNK), CHUNK)
            d_hidden = dr2[at_rows, :] + tmp[from_rows, :]
            normal = xh1[at_rows, :]
            acc[2] += fold(d_hidden)
            acc[1] += fold(d_hidden * normal)
            inside = d_hidden * r.gain1[...]
            grad_in = rstd1[at_rows, 0:1] * (inside - row_mean(inside) - normal * row_mean(inside * normal))
            acc[0] += fold(grad_in)
            dr2[at_rows, :] = grad_in
            gb[at_rows, :] = grad_in.astype(low)
            return carry

        tmp[...] = back[h].out[...].reshape(half_rows, width).astype(wide)
        lax.fori_loop(0, half_rows // CHUNK, step, 0)

    gfeed, gattn = r.gfeed, r.gattn
    blocks, per_block = gfeed.shape[0], gfeed.shape[1]

    def put_grad(packed, start, value):
        packed[:, :, start : start + value.shape[1]] = value.astype(low).reshape(blocks, per_block, value.shape[1])

    forward_half(0)
    forward_half(1)
    settle(ffn[0])
    settle(ffn[1])
    ffn[0].relay()
    ffn[0].arrive()
    backward_half(0)
    ffn[1].relay()
    ffn[1].arrive()
    backward_half(1)
    settle(back[0])
    put_grad(gfeed, hidden_width, dot(gf[...], act[...], 0, 0))
    settle(back[1])
    back[0].relay()
    put_grad(gfeed, 0, dot(hl[...], il[...], 0, 0))
    if planar:
        feed = PlaneReduce(gfeed, *r.feed)
        feed.start()
    back[0].arrive()
    last_norm(0)
    back[1].relay()
    back[1].arrive()
    last_norm(1)

    small = r.small
    for i in range(8):
        small[i : i + 1, :] = jnp.sum(acc[i], axis=0, keepdims=True)
    if planar:
        small_in, partners = r.small_in, (across, over_x, over_y)
        small_sum = r.small_sum
        tiny = [
            remote(
                small if s == 0 else small_sum.at[s - 1],
                small_in.at[s],
                r.small_send.at[s],
                r.small_recv.at[s],
                dp=partners[s],
            )
            for s in range(3)
        ]
        tiny[0].start()
        feed.step_one()

    dmt, ds = r.dmt, r.ds
    dqa, dqb, dkv = r.dqa, r.dqb, r.dkv
    dmt[...] = dot(r.o_weight[...], gb[...], 1, 1).astype(low)
    d_keys, d_values = [], []
    for h in range(heads):
        both = slice(h * pair, (h + 1) * pair)
        those = slice(h * HD, (h + 1) * HD)
        st[...] = dot(vt[those, :], dmt[those, :], 0, 0)

        def harden(i, carry, h=h):
            cols = pl.ds(pl.multiple_of(i * 128, 128), 128)
            prob = pt[h, :, cols].astype(wide)
            d_prob = st[:, cols]
            delta = jnp.sum(prob * d_prob, axis=0, keepdims=True)
            ds[:, cols] = (prob * (d_prob - delta) * scale).astype(low)
            return carry

        lax.fori_loop(0, lane_tiles, harden, 0)
        d_values.append(dot(pt[h], dmt[those, :], 1, 1).astype(low))
        d_key = dot(ds[...], qcat[:, both])
        d_keys.append(jnp.where(kind_wide[:, :HD] == 1, d_key[:, HD:], d_key[:, :HD]).astype(low))
        d_query = dot(kcat[:, both], ds[...], 0, 0).T
        dqa[:, both] = jnp.where(kind_wide[...] == 1, 0.0, d_query).astype(low)
        dqb[:, both] = jnp.where(kind_wide[...] == 1, d_query, 0.0).astype(low)
        if planar and h == 0:
            tiny[0].wait_recv()
            small_sum[0] = small[...] + small_in[0]
            tiny[1].start()
            feed.step_two()
        if planar and h == 1:
            tiny[1].wait_recv()
            small_sum[1] = small_sum[0] + small_in[1]
            tiny[2].start()
    dkv[...] = jnp.concatenate(d_keys + d_values, axis=1)
    wkv = jnp.concatenate([r.k_weight[...], r.v_weight[...]], axis=0)
    total = dot(dqa[...], wa[...]) + dot(dqb[...], wb[...]) + dot(dkv[...], wkv)
    total = total.astype(low).reshape(HALVES, LINE, block_rows, width)
    for h in range(HALVES):
        grad[h].part[...] = total[h]
        grad[h].start()
    put_grad(gattn, 0, dot(tok_t[...], dqa[...]))
    put_grad(gattn, 2 * local_width, dot(tok_t[...], dqb[...]))
    put_grad(gattn, 4 * local_width, dot(tok_t[...], dkv[...]))
    o_grad = dot(gb[...], mx[me].reshape(local_width, rows), 0, 1)
    pad = gattn.shape[2] - 7 * local_width
    put_grad(gattn, 6 * local_width, jnp.concatenate([o_grad, jnp.zeros((width, pad), wide)], axis=1))
    if planar:
        attn = PlaneReduce(gattn, *r.attn)
        attn.start()

    def settle_grad(h):
        line = grad[h]
        line.forward()
        own = pl.ds(pl.multiple_of(h * half_rows + me * block_rows, 16), block_rows)
        line.out[me] = (line.total() + dr2[own, :]).astype(low)
        line.spread()

    settle_grad(0)
    if planar:
        tiny[2].wait_recv()
        r.small_out[...] = small_sum[1] + small_in[2]
        feed_sum = feed.finish()
        r.in_grad[...] = feed_sum[:, :hidden_width]
        r.out_grad[...] = feed_sum[:, hidden_width:]
        attn.step_one()
    settle_grad(1)
    grad[0].relay()
    if planar:
        attn.step_two()
    grad[1].relay()
    if planar:
        attn_sum = attn.finish()
        for part in range(4):
            base = (part // 2) * 2 * local_width + (part % 2) * HD
            r.q_grad[part] = jnp.concatenate(
                [attn_sum[:, base + h * pair : base + h * pair + HD] for h in range(heads)], axis=1
            )
        both_grads = attn_sum[:, 4 * local_width : 6 * local_width]
        r.k_grad[...] = both_grads[:, :local_width]
        r.v_grad[...] = both_grads[:, local_width:]
        r.o_grad[...] = attn_sum[:, 6 * local_width : 7 * local_width].T
    else:
        r.small_out[...] = small[...]
        r.feed_out[...] = gfeed[...]
        r.attn_out[...] = gattn[...]
    for line in grad:
        line.arrive()
    for line in ffn + back + grad:
        line.drain()
    for gather in gathers:
        gather.drain()
    for copy in ow_line + ow_swap:
        copy.wait_send()
    if planar:
        for copy in tiny:
            copy.wait_send()


def local(
    tokens,
    segment_ids,
    token_types,
    q_weight,
    k_weight,
    v_weight,
    o_weight,
    o_bias,
    norm1_gain,
    norm1_shift,
    in_weight,
    in_bias,
    out_weight,
    out_bias,
    norm2_gain,
    norm2_shift,
    cotangent,
):
    rows, width = tokens.shape
    local_width = k_weight.shape[1]
    heads = local_width // HD
    hidden_width = in_weight.shape[1]
    n_dp = lax.axis_size("dp")
    planar = n_dp == 8
    blocks = 8
    per_block = width // blocks
    half_rows = rows // HALVES
    block_rows = half_rows // LINE
    low, wide = jnp.bfloat16, jnp.float32
    attn_width = -(-7 * local_width // 128) * 128
    args = dict(
        tokens=tokens,
        seg_col=segment_ids.reshape(rows, 1),
        seg_row=segment_ids.reshape(1, rows),
        kind_col=token_types.reshape(rows, 1),
        q_weight=q_weight.swapaxes(1, 2),
        k_weight=k_weight.T,
        v_weight=v_weight.T,
        o_weight=o_weight,
        o_bias=o_bias[None],
        gain1=norm1_gain[None],
        shift1=norm1_shift[None],
        in_weight=in_weight,
        in_bias=in_bias[None],
        out_weight=out_weight,
        out_bias=out_bias[None],
        gain2=norm2_gain[None],
        shift2=norm2_shift[None],
        cotangent=cotangent,
    )
    shaped = jax.ShapeDtypeStruct
    outs = dict(
        layer_out=shaped((rows, width), low),
        tokens_grad=shaped((HALVES, LINE, block_rows, width), low),
        small_out=shaped((8, width), wide),
    )
    if planar:
        outs |= dict(
            q_grad=shaped((4, per_block, local_width), wide),
            k_grad=shaped((per_block, local_width), wide),
            v_grad=shaped((per_block, local_width), wide),
            o_grad=shaped((local_width, per_block), wide),
            in_grad=shaped((per_block, hidden_width), wide),
            out_grad=shaped((per_block, hidden_width), wide),
        )
    else:
        outs |= dict(
            feed_out=shaped((blocks, per_block, 2 * hidden_width), low),
            attn_out=shaped((blocks, per_block, attn_width), low),
        )
    dma = pltpu.SemaphoreType.DMA
    scratch = dict(
        ow=pltpu.VMEM((LINE, local_width, width), low),
        ow_send=dma((6,)),
        ow_recv=dma((6,)),
        wa=pltpu.VMEM((2 * local_width, width), low),
        wb=pltpu.VMEM((2 * local_width, width), low),
        wk=pltpu.VMEM((2 * local_width, width), low),
        kind_wide=pltpu.VMEM((rows, 2 * HD), jnp.int32),
        seg_wide=pltpu.VMEM((rows, 2 * HD), jnp.int32),
        qcat=pltpu.VMEM((rows, 2 * local_width), low),
        kcat=pltpu.VMEM((rows, 2 * local_width), low),
        vt=pltpu.VMEM((local_width, rows), low),
        st=pltpu.VMEM((rows, rows), wide),
        pt=pltpu.VMEM((heads, rows, rows), low),
        mx=pltpu.VMEM((LINE, heads, HD, rows), low),
        mx_send=dma((heads, 5)),
        mx_recv=dma((heads, LINE)),
        tok_t=pltpu.VMEM((width, rows), low),
        xh1=pltpu.VMEM((rows, width), wide),
        rstd1=pltpu.VMEM((rows, 128), wide),
        hl=pltpu.VMEM((rows, width), low),
        act=pltpu.VMEM((rows, hidden_width), low),
        gp=pltpu.VMEM((rows, hidden_width), wide),
        dr2=pltpu.VMEM((rows, width), wide),
        gf=pltpu.VMEM((rows, width), low),
        il=pltpu.VMEM((rows, hidden_width), low),
        tmp=pltpu.VMEM((half_rows, width), wide),
        acc=pltpu.VMEM((8, 8, width), wide),
        gb=pltpu.VMEM((rows, width), low),
        ffn_out=pltpu.VMEM((HALVES, LINE, block_rows, width), low),
        back_out=pltpu.VMEM((HALVES, LINE, block_rows, width), low),
        gfeed=pltpu.VMEM((blocks, per_block, 2 * hidden_width), low),
        gattn=pltpu.VMEM((blocks, per_block, attn_width), low),
        small=pltpu.VMEM((8, width), wide),
        dmt=pltpu.VMEM((local_width, rows), low),
        ds=pltpu.VMEM((rows, rows), low),
        dqa=pltpu.VMEM((rows, 2 * local_width), low),
        dqb=pltpu.VMEM((rows, 2 * local_width), low),
        dkv=pltpu.VMEM((rows, 2 * local_width), low),
    )
    for name in ("ffn", "back", "grad"):
        scratch[name] = line_scratch(block_rows, width)
    if planar:
        scratch |= dict(
            feed=plane_scratch(per_block, 2 * hidden_width),
            attn=plane_scratch(per_block, attn_width),
            small_in=pltpu.VMEM((3, 8, width), wide),
            small_sum=pltpu.VMEM((2, 8, width), wide),
            small_send=dma((3,)),
            small_recv=dma((3,)),
        )
    layout = jax.tree.structure((args, outs, scratch))
    vm = pl.BlockSpec(memory_space=pltpu.VMEM)
    results = pl.pallas_call(
        functools.partial(layer_kernel, planar, layout),
        out_shape=jax.tree.leaves(outs),
        in_specs=[vm] * len(args),
        out_specs=[vm] * len(outs),
        scratch_shapes=jax.tree.leaves(scratch),
        compiler_params=pltpu.CompilerParams(
            collective_id=0, has_side_effects=True, vmem_limit_bytes=VMEM_LIMIT
        ),
    )(*jax.tree.leaves(args))
    res = types.SimpleNamespace(**jax.tree.unflatten(jax.tree.structure(outs), results))
    small = res.small_out
    if planar:
        grads = (res.q_grad, res.k_grad, res.v_grad, res.o_grad, res.in_grad, res.out_grad.T)
    else:
        feed = res.feed_out.astype(wide).reshape(width, 2 * hidden_width)
        attn = res.attn_out.astype(wide).reshape(width, attn_width)
        feed = lax.psum_scatter(feed, "dp", scatter_dimension=0, tiled=True)
        attn = lax.psum_scatter(attn, "dp", scatter_dimension=0, tiled=True)
        small = lax.psum(small, "dp")
        per = feed.shape[0]
        queries = attn[:, : 4 * local_width].reshape(per, 2, heads, 2, HD)
        queries = queries.transpose(1, 3, 0, 2, 4).reshape(4, per, local_width)
        grads = (
            queries,
            attn[:, 4 * local_width : 5 * local_width],
            attn[:, 5 * local_width : 6 * local_width],
            attn[:, 6 * local_width : 7 * local_width].T,
            feed[:, :hidden_width],
            feed[:, hidden_width:].T,
        )
    d_q, d_k, d_v, d_o, d_in, d_out = grads
    return (
        res.layer_out,
        res.tokens_grad.reshape(rows, width),
        d_q,
        d_k,
        d_v,
        d_o,
        small[0],
        small[1],
        small[2],
        d_in,
        small[3],
        d_out,
        small[4],
        small[5],
        small[6],
    )


def solution(mesh):
    return jax.shard_map(
        local,
        mesh=mesh,
        in_specs=(
            P("dp", None),
            P("dp", None),
            P("dp", None),
            P(None, None, "mp"),
            P(None, "mp"),
            P(None, "mp"),
            P("mp", None),
            P(),
            P(),
            P(),
            P(None, "mp"),
            P("mp"),
            P("mp", None),
            P(),
            P(),
            P(),
            P("dp", None),
        ),
        out_specs=(
            P("dp", None),
            P("dp", None),
            P(None, "dp", "mp"),
            P("dp", "mp"),
            P("dp", "mp"),
            P("mp", "dp"),
            P(),
            P(),
            P(),
            P("dp", "mp"),
            P("mp"),
            P("mp", "dp"),
            P(),
            P(),
            P(),
        ),
        check_vma=False,
    )
```

time: 555 us -> 194 us (0.35); the launches traced: 547 us -> 194 us
  waiting for transfers between devices: 355 us -> 0 us
  Pallas kernels: 0 us -> 172 us
  matrix products: 90 us -> 0 us
  blocking collectives: 44.5 us -> 0 us
  other arithmetic: 14.8 us -> 0 us
  between operations: 15.1 us -> 0.69 us
  local copies, waits for them, and re-layouts: 27.2 us -> 21.2 us
    psum x3 -> x0, waiting for transfers between devices: 183 us -> none  [the longest x1 84.7 us: local(): branch = lax.psum(matmul(mixed, o_weight), 'mp') + o_bias]
    pallas_call x0 -> x1, Pallas kernels: none -> 172 us  [local(): pl.pallas_call(functools.partial(layer_kernel, planar, layout), out_shape...]
    reduce_scatter x3 -> x0, waiting for transfers between devices: 92.4 us -> none  [the longest x1 46.3 us: local(): lax.psum_scatter(d_out_weight, 'dp', scatter_dimension=1, tiled=True)]
    dot_general x26 -> x0, matrix products: 88.5 us -> none  [the longest x14 30.4 us: matmul(): return jnp.dot(left, right, preferred_element_type=jnp.float32)]
    unnamed x14 -> x0, waiting for transfers between devices: 79.5 us -> none
    psum x1 -> x0, blocking collectives: 24.7 us -> none  [local(): lax.psum((d_o_bias, d_gain1, d_shift1, d_in_bias, d_out_bias, d_gain2, d_...]
    all_gather x1 -> x0, blocking collectives: 19.8 us -> none  [local(): tokens_grad = lax.all_gather(grad_rows, 'mp', axis=0, tiled=True)]
    unnamed x98 -> x22, local copies, waits for them, and re-layouts: 27.1 us -> 7.49 us
  transfers between devices with their start and end apart: 10 -> 0, of which waited for: 8 -> 0; matrix products, arithmetic and copies ran while one was open for 11% -> 0% of each run, Pallas kernels for 0% -> 0%
where the time goes in v1:
time: 194 us
  Pallas kernels  172 us (89%)
  local copies, waits for them, and re-layouts  21.2 us (11%)
    pallas_call x1, Pallas kernels, local(): pl.pallas_call(functools.partial(layer_kernel, planar, layout), out_shape...  172 us
    unnamed x22, local copies, waits for them, and re-layouts  7.49 us

profile of v1, /device:TPU:0, one launch (start us, length us, event | category | flops | bytes accessed | tf_op | source)
XLA Modules:
  0.0 193.6 jit_solution(2262092249047233949)
XLA Ops:
  0.6 1.3 broadcast_in_dim.24.refs_7_
  1.9 1.3 broadcast_in_dim.21.refs_1_
  3.2 1.3 broadcast_in_dim.26.refs_14_
  4.4 1.3 broadcast_in_dim.23.refs_3_
  5.7 1.3 broadcast_in_dim.25.refs_9_
  7.0 1.3 broadcast_in_dim.22.refs_2_
  8.2 1.3 broadcast_in_dim.27.refs_15_
  9.5 1.6 copy.32.refs_6_
  11.1 1.6 copy.33.refs_12_
  12.7 171.7 %shard_map.280 = (f32[96,768]{1,0:T(8,128)}, f32[96,192]{1,0:T(8,128)}, bf16[640,768]{1,0:T(8,128)(2,1)}, f32[192,96]{1,0:T(8,128)}, f32[96,768]{1,0:T(8,128)}, ...) custom-call(bf16[640,768]{1,0:T(8,128)(2,1)} %refs_0_.1, ...), custom_call_target="tpu_custom_call" | custom-call | tf_op jit(solution)/shard_map/pallas_call | solution.py:826
  184.4 0.0 copy-start
  184.4 1.7 slice_reduce_fusion
  186.1 2.2 %copy.42 = bf16[640,768]{1,0:T(8,128)(2,1)} copy(bf16[640,768]{1,0:T(8,128)(2,1)} %get-tuple-element.55) | data formatting | bytes 1966080
  188.3 0.0 copy-done
  188.3 0.0 copy-start.1
  188.3 0.0 copy-start.6
  188.3 0.0 copy-start.5
  188.3 0.0 copy-start.4
  188.3 0.9 copy.43
  189.3 0.2 copy-done.1
  189.5 0.0 copy-start.3
  189.5 0.7 copy.44
  190.3 0.0 copy-done.6
  190.3 0.6 copy.45
  190.9 0.0 copy-done.5
  190.9 0.6 copy.46
  191.6 0.0 copy-done.4
  191.6 0.6 copy.47
  192.2 0.0 copy-done.3
  192.2 0.7 copy.48
  192.9 0.0 copy-done.2
  192.9 0.7 copy.49
  (1 shorter events, 0.0 us)
Async XLA Ops:
  184.4 3.9 %copy-start = (bf16[2,4,80,768]{3,2,1,0:T(8,128)(2,1)S(1)}, bf16[2,4,80,768]{3,2,1,0:T(8,128)(2,1)}, u32[]{:S(2)}) copy-start(bf16[2,4,80,768]{3,2,1,0:T(8,128)(2,1)} %get-tuple-element.25) | copy-start | bytes 2949124
  188.3 1.2 copy-start.1
  188.3 1.9 %copy-start.6 = (f32[96,192]{1,0:T(8,128)S(1)}, f32[96,192]{1,0:T(8,128)}, u32[]{:S(2)}) copy-start(f32[96,192]{1,0:T(8,128)} %get-tuple-element.58) | copy-start | bytes 221188
  188.3 2.6 %copy-start.5 = (f32[96,192]{1,0:T(8,128)S(1)}, f32[96,192]{1,0:T(8,128)}, u32[]{:S(2)}) copy-start(f32[96,192]{1,0:T(8,128)} %get-tuple-element.59) | copy-start | bytes 221188
  188.3 3.2 %copy-start.4 = (f32[192,96]{1,0:T(8,128)S(1)}, f32[192,96]{1,0:T(8,128)}, u32[]{:S(2)}) copy-start(f32[192,96]{1,0:T(8,128)} %get-tuple-element.60) | copy-start | bytes 221188
  189.5 2.7 %copy-start.3 = (f32[96,768]{1,0:T(8,128)S(1)}, f32[96,768]{1,0:T(8,128)}, u32[]{:S(2)}) copy-start(f32[96,768]{1,0:T(8,128)} %get-tuple-element.64) | copy-start | bytes 884740
  189.5 3.4 %copy-start.2 = (f32[96,768]{1,0:T(8,128)S(1)}, f32[96,768]{1,0:T(8,128)}, u32[]{:S(2)}) copy-start(f32[96,768]{1,0:T(8,128)} %get-tuple-element.32) | copy-start | bytes 884740

commit v2 on v1

--- a/solution.py
+++ b/solution.py
@@ -12,7 +12,7 @@
 
 HD = 64
 LINE = 4
-HALVES = 2
+TILE = 128
 CHUNK = 32
 VMEM_LIMIT = 67043328
 
@@ -135,15 +135,15 @@
                 self.gather(self.me, slot, self.end).wait_send()
 
 
-def line_scratch(rows, width):
-    block = pltpu.VMEM((HALVES, rows, width), jnp.bfloat16)
+def line_scratch(tiles, rows, width):
+    block = pltpu.VMEM((tiles, rows, width), jnp.bfloat16)
     return [
-        pltpu.VMEM((HALVES, LINE, rows, width), jnp.bfloat16),
-        pltpu.VMEM((HALVES, 2, rows, width), jnp.bfloat16),
+        pltpu.VMEM((tiles, LINE, rows, width), jnp.bfloat16),
+        pltpu.VMEM((tiles, 2, rows, width), jnp.bfloat16),
         block,
         block,
-        pltpu.SemaphoreType.DMA((HALVES, 8)),
-        pltpu.SemaphoreType.DMA((HALVES, 8)),
+        pltpu.SemaphoreType.DMA((tiles, 8)),
+        pltpu.SemaphoreType.DMA((tiles, 8)),
     ]
 
 
@@ -309,7 +309,8 @@
 
 def rows_loop(start, count, body):
     def step(i, carry):
-        body(pl.ds(pl.multiple_of(start + i * CHUNK, CHUNK), CHUNK))
+        inside = pl.ds(pl.multiple_of(i * CHUNK, CHUNK), CHUNK)
+        body(pl.ds(pl.multiple_of(start + i * CHUNK, CHUNK), CHUNK), inside)
         return carry
 
     lax.fori_loop(0, count // CHUNK, step, 0)
@@ -330,8 +331,8 @@
     heads = local_width // HD
     pair = 2 * HD
     hidden_width = r.in_weight.shape[1]
-    half_rows = rows // HALVES
-    block_rows = half_rows // LINE
+    tiles = rows // TILE
+    block_rows = TILE // LINE
     low, wide = jnp.bfloat16, jnp.float32
     at = Place()
     me = at.me
@@ -351,18 +352,17 @@
 
     ow, ow_send, ow_recv = r.ow, r.ow_send, r.ow_recv
     share = local_width // 2
-    mine, other = pl.ds(core * share, share), pl.ds((1 - core) * share, share)
-    ow_line = []
-    for step in range(1, LINE):
-        ow_line.append(
-            remote(
-                r.o_weight.at[mine],
-                ow.at[me, mine],
-                ow_send.at[step - 1],
-                ow_recv.at[step - 1],
-                mp=lax.rem(me + step, LINE),
-            )
+    mine = pl.ds(core * share, share)
+    ow_line = [
+        remote(
+            r.o_weight.at[mine],
+            ow.at[me, mine],
+            ow_send.at[step - 1],
+            ow_recv.at[step - 1],
+            mp=lax.rem(me + step, LINE),
         )
+        for step in range(1, LINE)
+    ]
     for copy in ow_line:
         copy.start()
     ow_swap = []
@@ -372,6 +372,8 @@
             remote(ow.at[source, mine], ow.at[source, mine], ow_send.at[2 + step], ow_recv.at[2 + step], dp=across)
         )
 
+    vec = r.vec
+    o_bias, gain1, shift1, in_bias, out_bias, gain2, shift2 = (vec[i : i + 1, :] for i in range(7))
     wa, wb, wk = r.wa, r.wb, r.wk
     for h in range(heads):
         cols = slice(h * HD, (h + 1) * HD)
@@ -381,80 +383,77 @@
         key_part = r.k_weight[cols, :]
         wk[both, :] = jnp.concatenate([key_part, key_part], axis=0)
     kind_wide, seg_wide = r.kind_wide, r.seg_wide
-    kind_wide[...] = jnp.broadcast_to(r.kind_col[...], kind_wide.shape)
-    seg_wide[...] = jnp.broadcast_to(r.seg_col[...], seg_wide.shape)
+    kind_wide[...] = jnp.broadcast_to(r.kind_row[...], (pair, rows)).T
+    seg_wide[...] = jnp.broadcast_to(r.seg_row[...], (pair, rows)).T
     qcat, kcat, vt = r.qcat, r.kcat, r.vt
     tok = tokens[...]
-    q_plain = dot(tok, wa[...], 1, 1)
-    q_entity = dot(tok, wb[...], 1, 1)
     entity = kind_wide[...] == 1
     upper = lax.broadcasted_iota(jnp.int32, (rows, pair), 1) >= HD
-    for h in range(heads):
-        both = slice(h * pair, (h + 1) * pair)
-        qcat[:, both] = jnp.where(entity, q_entity[:, both], q_plain[:, both]).astype(low)
     keys = dot(tok, wk[...], 1, 1)
     for h in range(heads):
         both = slice(h * pair, (h + 1) * pair)
         kcat[:, both] = jnp.where(entity == upper, keys[:, both], 0.0).astype(low)
     vt[...] = dot(r.v_weight[...], tok, 1, 1).astype(low)
-
-    st, pt, mx = r.st, r.pt, r.mx
-    gathers = []
-    scale = HD ** (-0.5)
-    lane_tiles = rows // 128
+    q_plain = dot(tok, wa[...], 1, 1)
+    q_entity = dot(tok, wb[...], 1, 1)
     for h in range(heads):
         both = slice(h * pair, (h + 1) * pair)
-        st[...] = dot(kcat[:, both], qcat[:, both], 1, 1)
-
-        def soften(i, carry, h=h):
-            cols = pl.ds(pl.multiple_of(i * 128, 128), 128)
-            scores = jnp.where(seg_wide[...] == r.seg_row[:, cols], st[:, cols] * scale, -1000000000.0)
+        qcat[:, both] = jnp.where(entity, q_entity[:, both], q_plain[:, both]).astype(low)
+
+    pt, mx, mloc = r.pt, r.mx, r.mloc
+    scale = HD ** (-0.5)
+    gathers = [
+        LineGather(at, r.mx_send.at[q], r.mx_recv.at[q], lambda block, q=q: mx.at[block, q]) for q in range(tiles)
+    ]
+
+    def pair_of(h):
+        return pl.ds(pl.multiple_of(h * pair, pair), pair)
+
+    def head_of(h):
+        return pl.ds(pl.multiple_of(h * HD, HD), HD)
+
+    def attend(q):
+        span = slice(q * TILE, (q + 1) * TILE)
+
+        def head_step(h, carry):
+            raw = dot(kcat[:, pair_of(h)], qcat[span, pair_of(h)], 1, 1)
+            scores = jnp.where(seg_wide[...] == r.seg_row[:, span], raw * scale, -1000000000.0)
             shifted = jnp.exp(scores - jnp.max(scores, axis=0, keepdims=True))
             total = jnp.sum(shifted, axis=0, keepdims=True)
-            pt[h, :, cols] = (shifted * (1.0 / total)).astype(low)
+            prob = (shifted * (1.0 / total)).astype(low)
+            pt[h, :, span] = prob
+            mixed = dot(vt[head_of(h), :], prob).astype(low)
+            mx[me, q, head_of(h), :] = mixed
+            mloc[head_of(h), span] = mixed
             return carry
 
-        lax.fori_loop(0, lane_tiles, soften, 0)
-        mx[me, h] = dot(vt[h * HD : (h + 1) * HD, :], pt[h]).astype(low)
-        gather = LineGather(at, r.mx_send.at[h], r.mx_recv.at[h], lambda block, h=h: mx.at[block, h])
-        gathers.append(gather)
-        gather.spread()
-        if h:
-            gathers[h - 1].relay()
-    for copy in ow_line:
-        copy.wait_recv()
-    for copy in ow_swap:
-        copy.start()
-    ow[me] = r.o_weight[...]
-    tok_t = r.tok_t
-    tok_t[...] = tokens[...].T
-    gathers[-1].relay()
-    for gather in gathers:
-        gather.arrive()
-    for copy in ow_swap:
-        copy.wait_recv()
+        lax.fori_loop(0, heads, head_step, 0)
+        gathers[q].spread()
+
+    def swap_weights():
+        for copy in ow_line:
+            copy.wait_recv()
+        for copy in ow_swap:
+            copy.start()
+        ow[me] = r.o_weight[...]
+
+    tok_t, kct, vn = r.tok_t, r.kct, r.vn
+
+    def turn():
+        tok_t[...] = tokens[...].T
+        kct[...] = kcat[...].T
+        for h in range(heads):
+            vn[h] = vt[h * HD : (h + 1) * HD, :].T
 
     xh1, rstd1, hl = r.xh1, r.rstd1, r.hl
-    xh1[...] = dot(mx[...].reshape(LINE * local_width, rows), ow[...].reshape(LINE * local_width, width), 0, 0)
-
-    def first_norm(at_rows):
-        value = xh1[at_rows, :] + tokens[at_rows, :].astype(wide) + r.o_bias[...]
-        centred = value - row_mean(value)
-        scaled = lax.rsqrt(row_mean(centred * centred) + norm_epsilon)
-        normal = centred * scaled
-        xh1[at_rows, :] = normal
-        rstd1[at_rows, :] = jnp.broadcast_to(scaled, (CHUNK, 128))
-        hl[at_rows, :] = (normal * r.gain1[...] + r.shift1[...]).astype(low)
-
-    act, gp, dr2, gf, il, tmp = r.act, r.gp, r.dr2, r.gf, r.il, r.tmp
-    acc = r.acc
+    act, gp, dr2, gf, il, gb, tmp, acc = r.act, r.gp, r.dr2, r.gf, r.il, r.gb, r.tmp, r.acc
     acc[...] = jnp.zeros_like(acc)
 
     def make_lines(parts, out):
         part, carry, single, summed, send, recv = parts
         return [
-            LineReduce(part.at[h], carry.at[h], single.at[h], summed.at[h], out.at[h], send.at[h], recv.at[h])
-            for h in range(HALVES)
+            LineReduce(part.at[q], carry.at[q], single.at[q], summed.at[q], out.at[q], send.at[q], recv.at[q])
+            for q in range(tiles)
         ]
 
     ffn = make_lines(r.ffn, r.ffn_out)
@@ -463,93 +462,123 @@
 
     def put_part(line, value):
         line.part[...] = value.astype(low).reshape(line.part.shape)
-
-    root_half = math.sqrt(0.5)
-    density = 1.0 / math.sqrt(2.0 * math.pi)
-
-    def forward_half(h):
-        here = pl.ds(h * half_rows, half_rows)
-        rows_loop(h * half_rows, half_rows, first_norm)
-        gp[here, :] = dot(hl[here, :], r.in_weight[...])
-
-        def activate(at_rows):
-            inner = gp[at_rows, :] + r.in_bias[...]
-            gate = 0.5 + 0.5 * lax.erf(inner * root_half)
-            act[at_rows, :] = (inner * gate).astype(low)
-            gp[at_rows, :] = gate + inner * (density * jnp.exp(-0.5 * inner * inner))
-
-        rows_loop(h * half_rows, half_rows, activate)
-        put_part(ffn[h], dot(act[here, :], r.out_weight[...]))
-        ffn[h].start()
 
     def settle(line):
         line.forward()
         line.out[me] = line.total().astype(low)
         line.spread()
 
-    def backward_half(h):
-        here = pl.ds(h * half_rows, half_rows)
-        start = h * half_rows
-
-        def second_norm(at_rows, from_rows):
-            value = xh1[at_rows, :] * r.gain1[...] + r.shift1[...]
-            value = value + tmp[from_rows, :] + r.out_bias[...]
+    root_half = math.sqrt(0.5)
+    density = 1.0 / math.sqrt(2.0 * math.pi)
+
+    def forward(q):
+        gathers[q].arrive()
+        start = q * TILE
+        here = pl.ds(start, TILE)
+        tmp[...] = dot(mx[:, q].reshape(LINE * local_width, TILE), ow[...].reshape(LINE * local_width, width), 0, 0)
+
+        def first_norm(at_rows, inside):
+            value = tmp[inside, :] + tokens[at_rows, :].astype(wide) + o_bias
             centred = value - row_mean(value)
             scaled = lax.rsqrt(row_mean(centred * centred) + norm_epsilon)
             normal = centred * scaled
-            r.layer_out[at_rows, :] = (normal * r.gain2[...] + r.shift2[...]).astype(low)
+            xh1[at_rows, :] = normal
+            rstd1[at_rows, :] = jnp.broadcast_to(scaled, (CHUNK, 128))
+            hl[at_rows, :] = (normal * gain1 + shift1).astype(low)
+
+        rows_loop(start, TILE, first_norm)
+        tmp[...] = dot(hl[here, :], r.in_weight[...])
+
+        def activate(at_rows, inside):
+            inner = tmp[inside, :] + in_bias
+            gate = 0.5 + 0.5 * lax.erf(inner * root_half)
+            act[at_rows, :] = (inner * gate).astype(low)
+            gp[at_rows, :] = gate + inner * (density * jnp.exp(-0.5 * inner * inner))
+
+        rows_loop(start, TILE, activate)
+        put_part(ffn[q], dot(act[here, :], r.out_weight[...]))
+        ffn[q].start()
+
+    def backward(q):
+        ffn[q].arrive()
+        start = q * TILE
+        here = pl.ds(start, TILE)
+        tmp[...] = ffn[q].out[...].reshape(TILE, width).astype(wide)
+
+        def second_norm(at_rows, inside):
+            value = xh1[at_rows, :] * gain1 + shift1
+            value = value + tmp[inside, :] + out_bias
+            centred = value - row_mean(value)
+            scaled = lax.rsqrt(row_mean(centred * centred) + norm_epsilon)
+            normal = centred * scaled
+            r.layer_out[at_rows, :] = (normal * gain2 + shift2).astype(low)
             cot = r.cotangent[at_rows, :].astype(wide)
             acc[6] += fold(cot)
             acc[5] += fold(cot * normal)
-            inside = cot * r.gain2[...]
-            grad_in = scaled * (inside - row_mean(inside) - normal * row_mean(inside * normal))
+            grown = cot * gain2
+            grad_in = scaled * (grown - row_mean(grown) - normal * row_mean(grown * normal))
             acc[4] += fold(grad_in)
             dr2[at_rows, :] = grad_in
             gf[at_rows, :] = grad_in.astype(low)
 
-        def norm_step(i, carry):
-            at_rows = pl.ds(pl.multiple_of(start + i * CHUNK, CHUNK), CHUNK)
-            from_rows = pl.ds(pl.multiple_of(i * CHUNK, CHUNK), CHUNK)
-            second_norm(at_rows, from_rows)
-            return carry
-
-        tmp[...] = ffn[h].out[...].reshape(half_rows, width).astype(wide)
-        lax.fori_loop(0, half_rows // CHUNK, norm_step, 0)
+        rows_loop(start, TILE, second_norm)
         tmp[...] = dot(gf[here, :], r.out_weight[...], 1, 1)
 
-        def inner_step(i, carry):
-            at_rows = pl.ds(pl.multiple_of(start + i * CHUNK, CHUNK), CHUNK)
-            from_rows = pl.ds(pl.multiple_of(i * CHUNK, CHUNK), CHUNK)
-            d_inner = tmp[from_rows, :] * gp[at_rows, :]
+        def inner_step(at_rows, inside):
+            d_inner = tmp[inside, :] * gp[at_rows, :]
             acc[3] += fold(d_inner)
             il[at_rows, :] = d_inner.astype(low)
-            return carry
-
-        lax.fori_loop(0, half_rows // CHUNK, inner_step, 0)
-        put_part(back[h], dot(il[here, :], r.in_weight[...], 1, 1))
-        back[h].start()
-
-    gb = r.gb
-
-    def last_norm(h):
-        start = h * half_rows
-
-        def step(i, carry):
-            at_rows = pl.ds(pl.multiple_of(start + i * CHUNK, CHUNK), CHUNK)
-            from_rows = pl.ds(pl.multiple_of(i * CHUNK, CHUNK), CHUNK)
-            d_hidden = dr2[at_rows, :] + tmp[from_rows, :]
+
+        rows_loop(start, TILE, inner_step)
+        put_part(back[q], dot(il[here, :], r.in_weight[...], 1, 1))
+        back[q].start()
+
+    dqa, dqb, dkv, dk_sum, dv_sum = r.dqa, r.dqb, r.dkv, r.dk_sum, r.dv_sum
+    dmt = r.dmt
+
+    def finish_rows(q):
+        back[q].arrive()
+        start = q * TILE
+        here = pl.ds(start, TILE)
+        span = slice(start, start + TILE)
+        tmp[...] = back[q].out[...].reshape(TILE, width).astype(wide)
+
+        def last_norm(at_rows, inside):
+            d_hidden = dr2[at_rows, :] + tmp[inside, :]
             normal = xh1[at_rows, :]
             acc[2] += fold(d_hidden)
             acc[1] += fold(d_hidden * normal)
-            inside = d_hidden * r.gain1[...]
-            grad_in = rstd1[at_rows, 0:1] * (inside - row_mean(inside) - normal * row_mean(inside * normal))
+            grown = d_hidden * gain1
+            grad_in = rstd1[at_rows, 0:1] * (grown - row_mean(grown) - normal * row_mean(grown * normal))
             acc[0] += fold(grad_in)
             dr2[at_rows, :] = grad_in
             gb[at_rows, :] = grad_in.astype(low)
+
+        rows_loop(start, TILE, last_norm)
+        dmt[...] = dot(r.o_weight[...], gb[here, :], 1, 1).astype(low)
+        row_entity = kind_wide[span, :] == 1
+
+        def head_step(h, carry):
+            d_mixed = dmt[head_of(h), :]
+            d_prob = dot(vn[h], d_mixed)
+            prob_low = pt[h, :, span]
+            prob = prob_low.astype(wide)
+            delta = jnp.sum(prob * d_prob, axis=0, keepdims=True)
+            d_score = (prob * (d_prob - delta) * scale).astype(low)
+            d_value = dot(prob_low, d_mixed, 1, 1)
+            d_key = dot(d_score, qcat[span, pair_of(h)])
+            if q == 0:
+                dv_sum[h] = d_value
+                dk_sum[h] = d_key
+            else:
+                dv_sum[h] += d_value
+                dk_sum[h] += d_key
+            d_query = dot(kct[pair_of(h), :], d_score).T
+            dqa[span, pair_of(h)] = jnp.where(row_entity, 0.0, d_query).astype(low)
+            dqb[span, pair_of(h)] = jnp.where(row_entity, d_query, 0.0).astype(low)
             return carry
 
-        tmp[...] = back[h].out[...].reshape(half_rows, width).astype(wide)
-        lax.fori_loop(0, half_rows // CHUNK, step, 0)
+        lax.fori_loop(0, heads, head_step, 0)
 
     gfeed, gattn = r.gfeed, r.gattn
     blocks, per_block = gfeed.shape[0], gfeed.shape[1]
@@ -557,29 +586,41 @@
     def put_grad(packed, start, value):
         packed[:, :, start : start + value.shape[1]] = value.astype(low).reshape(blocks, per_block, value.shape[1])
 
-    forward_half(0)
-    forward_half(1)
-    settle(ffn[0])
-    settle(ffn[1])
-    ffn[0].relay()
-    ffn[0].arrive()
-    backward_half(0)
-    ffn[1].relay()
-    ffn[1].arrive()
-    backward_half(1)
-    settle(back[0])
-    put_grad(gfeed, hidden_width, dot(gf[...], act[...], 0, 0))
-    settle(back[1])
-    back[0].relay()
-    put_grad(gfeed, 0, dot(hl[...], il[...], 0, 0))
     if planar:
         feed = PlaneReduce(gfeed, *r.feed)
-        feed.start()
-    back[0].arrive()
-    last_norm(0)
-    back[1].relay()
-    back[1].arrive()
-    last_norm(1)
+        attn = PlaneReduce(gattn, *r.attn)
+
+    def feed_grads():
+        put_grad(gfeed, hidden_width, dot(gf[...], act[...], 0, 0))
+        put_grad(gfeed, 0, dot(hl[...], il[...], 0, 0))
+        if planar:
+            feed.start()
+
+    stages = (
+        attend,
+        lambda q: gathers[q].relay(),
+        forward,
+        lambda q: settle(ffn[q]),
+        lambda q: ffn[q].relay(),
+        backward,
+        lambda q: settle(back[q]),
+        lambda q: back[q].relay(),
+        finish_rows,
+    )
+    lag = (0, 2, 3, 4, 5, 6, 7, 8, 9)
+    for tick in range(tiles + lag[-1]):
+        if tick == 3:
+            swap_weights()
+            for copy in ow_swap:
+                copy.wait_recv()
+        for stage, late in reversed(tuple(zip(stages, lag))):
+            q = tick - late
+            if 0 <= q < tiles:
+                stage(q)
+        if tick == lag[-1] - 1:
+            turn()
+        if tick == tiles - 1 + lag[6]:
+            feed_grads()
 
     small = r.small
     for i in range(8):
@@ -598,78 +639,60 @@
             for s in range(3)
         ]
         tiny[0].start()
+
+    d_keys = [
+        jnp.where(kind_wide[:, :HD] == 1, dk_sum[h, :, HD:], dk_sum[h, :, :HD]).astype(low) for h in range(heads)
+    ]
+    d_values = [dv_sum[h].astype(low) for h in range(heads)]
+    dkv[...] = jnp.concatenate(d_keys + d_values, axis=1)
+    wkv = jnp.concatenate([r.k_weight[...], r.v_weight[...]], axis=0)
+    for q in range(tiles):
+        span = slice(q * TILE, (q + 1) * TILE)
+        put_part(grad[q], dot(dqa[span, :], wa[...]) + dot(dqb[span, :], wb[...]) + dot(dkv[span, :], wkv))
+        grad[q].start()
+
+    def settle_grad(q):
+        line = grad[q]
+        line.forward()
+        own = pl.ds(pl.multiple_of(q * TILE + me * block_rows, block_rows), block_rows)
+        line.out[me] = (line.total() + dr2[own, :]).astype(low)
+        line.spread()
+
+    if planar:
         feed.step_one()
-
-    dmt, ds = r.dmt, r.ds
-    dqa, dqb, dkv = r.dqa, r.dqb, r.dkv
-    dmt[...] = dot(r.o_weight[...], gb[...], 1, 1).astype(low)
-    d_keys, d_values = [], []
-    for h in range(heads):
-        both = slice(h * pair, (h + 1) * pair)
-        those = slice(h * HD, (h + 1) * HD)
-        st[...] = dot(vt[those, :], dmt[those, :], 0, 0)
-
-        def harden(i, carry, h=h):
-            cols = pl.ds(pl.multiple_of(i * 128, 128), 128)
-            prob = pt[h, :, cols].astype(wide)
-            d_prob = st[:, cols]
-            delta = jnp.sum(prob * d_prob, axis=0, keepdims=True)
-            ds[:, cols] = (prob * (d_prob - delta) * scale).astype(low)
-            return carry
-
-        lax.fori_loop(0, lane_tiles, harden, 0)
-        d_values.append(dot(pt[h], dmt[those, :], 1, 1).astype(low))
-        d_key = dot(ds[...], qcat[:, both])
-        d_keys.append(jnp.where(kind_wide[:, :HD] == 1, d_key[:, HD:], d_key[:, :HD]).astype(low))
-        d_query = dot(kcat[:, both], ds[...], 0, 0).T
-        dqa[:, both] = jnp.where(kind_wide[...] == 1, 0.0, d_query).astype(low)
-        dqb[:, both] = jnp.where(kind_wide[...] == 1, d_query, 0.0).astype(low)
-        if planar and h == 0:
-            tiny[0].wait_recv()
-            small_sum[0] = small[...] + small_in[0]
-            tiny[1].start()
-            feed.step_two()
-        if planar and h == 1:
+    put_grad(gattn, 0, dot(tok_t[...], dqa[...]))
+    put_grad(gattn, 2 * local_width, dot(tok_t[...], dqb[...]))
+    settle_grad(0)
+    put_grad(gattn, 4 * local_width, dot(tok_t[...], dkv[...]))
+    o_grad = dot(gb[...], mloc[...], 0, 1)
+    pad = gattn.shape[2] - 7 * local_width
+    put_grad(gattn, 6 * local_width, jnp.concatenate([o_grad, jnp.zeros((width, pad), wide)], axis=1))
+    if planar:
+        attn.start()
+    settle_grad(1)
+    grad[0].relay()
+    if planar:
+        tiny[0].wait_recv()
+        small_sum[0] = small[...] + small_in[0]
+        tiny[1].start()
+        feed.step_two()
+        attn.step_one()
+    for q in range(2, tiles):
+        settle_grad(q)
+        grad[q - 1].relay()
+        if planar and q == 2:
             tiny[1].wait_recv()
             small_sum[1] = small_sum[0] + small_in[1]
             tiny[2].start()
-    dkv[...] = jnp.concatenate(d_keys + d_values, axis=1)
-    wkv = jnp.concatenate([r.k_weight[...], r.v_weight[...]], axis=0)
-    total = dot(dqa[...], wa[...]) + dot(dqb[...], wb[...]) + dot(dkv[...], wkv)
-    total = total.astype(low).reshape(HALVES, LINE, block_rows, width)
-    for h in range(HALVES):
-        grad[h].part[...] = total[h]
-        grad[h].start()
-    put_grad(gattn, 0, dot(tok_t[...], dqa[...]))
-    put_grad(gattn, 2 * local_width, dot(tok_t[...], dqb[...]))
-    put_grad(gattn, 4 * local_width, dot(tok_t[...], dkv[...]))
-    o_grad = dot(gb[...], mx[me].reshape(local_width, rows), 0, 1)
-    pad = gattn.shape[2] - 7 * local_width
-    put_grad(gattn, 6 * local_width, jnp.concatenate([o_grad, jnp.zeros((width, pad), wide)], axis=1))
-    if planar:
-        attn = PlaneReduce(gattn, *r.attn)
-        attn.start()
-
-    def settle_grad(h):
-        line = grad[h]
-        line.forward()
-        own = pl.ds(pl.multiple_of(h * half_rows + me * block_rows, 16), block_rows)
-        line.out[me] = (line.total() + dr2[own, :]).astype(low)
-        line.spread()
-
-    settle_grad(0)
+            feed_sum = feed.finish()
+            r.in_grad[...] = feed_sum[:, :hidden_width]
+            r.out_grad[...] = feed_sum[:, hidden_width:]
+        if planar and q == 3:
+            attn.step_two()
     if planar:
         tiny[2].wait_recv()
         r.small_out[...] = small_sum[1] + small_in[2]
-        feed_sum = feed.finish()
-        r.in_grad[...] = feed_sum[:, :hidden_width]
-        r.out_grad[...] = feed_sum[:, hidden_width:]
-        attn.step_one()
-    settle_grad(1)
-    grad[0].relay()
-    if planar:
-        attn.step_two()
-    grad[1].relay()
+    grad[tiles - 1].relay()
     if planar:
         attn_sum = attn.finish()
         for part in range(4):
@@ -696,6 +719,12 @@
     if planar:
         for copy in tiny:
             copy.wait_send()
+
+
+def hand_on(*refs):
+    count = len(refs) // 2
+    for source, target in zip(refs[:count], refs[count:]):
+        target[...] = source[...]
 
 
 def local(
@@ -725,34 +754,27 @@
     planar = n_dp == 8
     blocks = 8
     per_block = width // blocks
-    half_rows = rows // HALVES
-    block_rows = half_rows // LINE
+    tiles = rows // TILE
+    block_rows = TILE // LINE
     low, wide = jnp.bfloat16, jnp.float32
     attn_width = -(-7 * local_width // 128) * 128
     args = dict(
         tokens=tokens,
-        seg_col=segment_ids.reshape(rows, 1),
-        seg_row=segment_ids.reshape(1, rows),
-        kind_col=token_types.reshape(rows, 1),
+        seg_row=segment_ids,
+        kind_row=token_types,
         q_weight=q_weight.swapaxes(1, 2),
         k_weight=k_weight.T,
         v_weight=v_weight.T,
         o_weight=o_weight,
-        o_bias=o_bias[None],
-        gain1=norm1_gain[None],
-        shift1=norm1_shift[None],
+        vec=jnp.stack([o_bias, norm1_gain, norm1_shift, in_bias, out_bias, norm2_gain, norm2_shift, o_bias]),
         in_weight=in_weight,
-        in_bias=in_bias[None],
         out_weight=out_weight,
-        out_bias=out_bias[None],
-        gain2=norm2_gain[None],
-        shift2=norm2_shift[None],
         cotangent=cotangent,
     )
     shaped = jax.ShapeDtypeStruct
     outs = dict(
         layer_out=shaped((rows, width), low),
-        tokens_grad=shaped((HALVES, LINE, block_rows, width), low),
+        tokens_grad=shaped((tiles, LINE, block_rows, width), low),
         small_out=shaped((8, width), wide),
     )
     if planar:
@@ -782,11 +804,11 @@
         qcat=pltpu.VMEM((rows, 2 * local_width), low),
         kcat=pltpu.VMEM((rows, 2 * local_width), low),
         vt=pltpu.VMEM((local_width, rows), low),
-        st=pltpu.VMEM((rows, rows), wide),
         pt=pltpu.VMEM((heads, rows, rows), low),
-        mx=pltpu.VMEM((LINE, heads, HD, rows), low),
-        mx_send=dma((heads, 5)),
-        mx_recv=dma((heads, LINE)),
+        mx=pltpu.VMEM((LINE, tiles, local_width, TILE), low),
+        mloc=pltpu.VMEM((local_width, rows), low),
+        mx_send=dma((tiles, 5)),
+        mx_recv=dma((tiles, LINE)),
         tok_t=pltpu.VMEM((width, rows), low),
         xh1=pltpu.VMEM((rows, width), wide),
         rstd1=pltpu.VMEM((rows, 128), wide),
@@ -796,22 +818,25 @@
         dr2=pltpu.VMEM((rows, width), wide),
         gf=pltpu.VMEM((rows, width), low),
         il=pltpu.VMEM((rows, hidden_width), low),
-        tmp=pltpu.VMEM((half_rows, width), wide),
+        tmp=pltpu.VMEM((TILE, width), wide),
         acc=pltpu.VMEM((8, 8, width), wide),
         gb=pltpu.VMEM((rows, width), low),
-        ffn_out=pltpu.VMEM((HALVES, LINE, block_rows, width), low),
-        back_out=pltpu.VMEM((HALVES, LINE, block_rows, width), low),
+        ffn_out=pltpu.VMEM((tiles, LINE, block_rows, width), low),
+        back_out=pltpu.VMEM((tiles, LINE, block_rows, width), low),
         gfeed=pltpu.VMEM((blocks, per_block, 2 * hidden_width), low),
         gattn=pltpu.VMEM((blocks, per_block, attn_width), low),
         small=pltpu.VMEM((8, width), wide),
-        dmt=pltpu.VMEM((local_width, rows), low),
-        ds=pltpu.VMEM((rows, rows), low),
+        kct=pltpu.VMEM((2 * local_width, rows), low),
+        vn=pltpu.VMEM((heads, rows, HD), low),
+        dmt=pltpu.VMEM((local_width, TILE), low),
+        dk_sum=pltpu.VMEM((heads, rows, 2 * HD), wide),
+        dv_sum=pltpu.VMEM((heads, rows, HD), wide),
         dqa=pltpu.VMEM((rows, 2 * local_width), low),
         dqb=pltpu.VMEM((rows, 2 * local_width), low),
         dkv=pltpu.VMEM((rows, 2 * local_width), low),
     )
     for name in ("ffn", "back", "grad"):
-        scratch[name] = line_scratch(block_rows, width)
+        scratch[name] = line_scratch(tiles, block_rows, width)
     if planar:
         scratch |= dict(
             feed=plane_scratch(per_block, 2 * hidden_width),
@@ -833,7 +858,20 @@
             collective_id=0, has_side_effects=True, vmem_limit_bytes=VMEM_LIMIT
         ),
     )(*jax.tree.leaves(args))
-    res = types.SimpleNamespace(**jax.tree.unflatten(jax.tree.structure(outs), results))
+    results = dict(zip(sorted(outs), results))
+    if planar:
+        small = results.pop("small_out")
+        results["tokens_grad"] = results["tokens_grad"].reshape(rows, width)
+        flat, tree = jax.tree.flatten(results)
+        flat = pl.pallas_call(
+            hand_on,
+            out_shape=[shaped(a.shape, a.dtype) for a in flat],
+            in_specs=[vm] * len(flat),
+            out_specs=[vm] * len(flat),
+            compiler_params=pltpu.CompilerParams(vmem_limit_bytes=VMEM_LIMIT),
+        )(*flat)
+        results = jax.tree.unflatten(tree, flat) | {"small_out": small}
+    res = types.SimpleNamespace(**results)
     small = res.small_out
     if planar:
         grads = (res.q_grad, res.k_grad, res.v_grad, res.o_grad, res.in_grad, res.out_grad.T)

time: 194 us -> 220 us (1.13)
  Pallas kernels: 172 us -> 212 us
  local copies, waits for them, and re-layouts: 21.2 us -> 7.14 us
    pallas_call x1, Pallas kernels: 172 us -> 208 us  [local(): pl.pallas_call(functools.partial(layer_kernel, planar, layout), out_shape...]
    broadcast_in_dim x7 -> x0, local copies, waits for them, and re-layouts: 8.87 us -> none  [the longest x1 1.27 us: local(): o_bias[None]]
    unnamed x22 -> x0, local copies, waits for them, and re-layouts: 7.49 us -> none
    another operation x0 -> x8, local copies, waits for them, and re-layouts: none -> 5.47 us  [local(): jnp.stack([o_bias, norm1_gain, norm1_shift, in_bias, out_bias, norm2_gain...]
    pallas_call x0 -> x1, Pallas kernels: none -> 3.6 us  [local(): pl.pallas_call(hand_on, out_shape=[shaped(a.shape, a.dtype) for a in flat...]
    reshape x2 -> x0, local copies, waits for them, and re-layouts: 3.16 us -> none  [the longest x1 1.58 us: local(): token_types.reshape(rows, 1)]
where the time goes in v2:
time: 220 us; the launch traced here: 219 us
  Pallas kernels  212 us (96%)
  local copies, waits for them, and re-layouts  7.14 us (3%)
    pallas_call x1, Pallas kernels, local(): pl.pallas_call(functools.partial(layer_kernel, planar, layout), out_shape...  208 us
    another operation x8, local copies, waits for them, and re-layouts, local(): jnp.stack([o_bias, norm1_gain, norm1_shift, in_bias, out_bias, norm2_gain...  5.47 us

profile of v2, /device:TPU:0, one launch (start us, length us, event | category | flops | bytes accessed | tf_op | source)
XLA Modules:
  0.0 219.4 jit_solution(10617234678019423386)
XLA Ops:
  0.6 0.7 stack.25
  1.3 0.7 stack.26
  2.0 0.7 stack.27
  2.7 0.7 stack.28
  3.4 0.7 stack.29
  4.1 0.7 stack.30
  4.8 0.7 stack.31
  5.5 0.6 stack.32.refs_10_
  6.1 208.0 %shard_map.280 = (f32[96,768]{1,0:T(8,128)}, f32[96,192]{1,0:T(8,128)}, bf16[640,768]{1,0:T(8,128)(2,1)}, f32[192,96]{1,0:T(8,128)}, f32[96,768]{1,0:T(8,128)}, ...) custom-call(bf16[640,768]{1,0:T(8,128)(2,1)} %refs_0_.1, ...), custom_call_target="tpu_custom_call" | custom-call | tf_op jit(solution)/shard_map/pallas_call | solution.py:851
  214.1 3.6 %shard_map.281 = (f32[96,768]{1,0:T(8,128)}, f32[96,192]{1,0:T(8,128)}, bf16[640,768]{1,0:T(8,128)(2,1)}, f32[192,96]{1,0:T(8,128)}, f32[96,768]{1,0:T(8,128)}, ...) custom-call(f32[96,768]{1,0:T(8,128)} %get-tuple-element.32.refs_0_, ...), custom_call_target="tpu_custom_call" | custom-call | tf_op jit(solution)/shard_map/pallas_call | solution.py:866
  217.7 1.7 slice_reduce_fusion

commit v3 on v2

--- a/solution.py
+++ b/solution.py
@@ -12,7 +12,8 @@
 
 HD = 64
 LINE = 4
-TILE = 128
+PORTIONS = (2, 3)
+LANES = 128
 CHUNK = 32
 VMEM_LIMIT = 67043328
 
@@ -28,176 +29,6 @@
         device_id=axes,
         device_id_type=pl.DeviceIdType.MESH,
     )
-
-
-class LineReduce:
-    def __init__(self, part, carry, single, summed, out, send, recv):
-        self.part, self.carry, self.single, self.summed, self.out = part, carry, single, summed, out
-        me = lax.axis_index("mp")
-        self.me = me
-        left = me < 2
-        self.is_mid = jnp.logical_or(me == 1, me == 2)
-        self.is_end = jnp.logical_not(self.is_mid)
-        self.mid = jnp.where(left, 1, 2)
-        self.end = jnp.where(left, 0, 3)
-        self.far_mid = 3 - self.mid
-        self.far_end = 3 - self.end
-        self.send, self.recv = send, recv
-
-    def end_sends(self):
-        return (
-            remote(self.part.at[self.far_end], self.carry.at[0], self.send.at[0], self.recv.at[2], mp=self.mid),
-            remote(self.part.at[self.far_mid], self.carry.at[1], self.send.at[1], self.recv.at[3], mp=self.mid),
-            remote(self.part.at[self.mid], self.single, self.send.at[2], self.recv.at[0], mp=self.mid),
-        )
-
-    def mid_sends(self):
-        return (
-            remote(self.part.at[self.end], self.single, self.send.at[0], self.recv.at[0], mp=self.end),
-            remote(self.carry.at[0], self.summed, self.send.at[1], self.recv.at[1], mp=self.far_end),
-            remote(self.carry.at[1], self.summed, self.send.at[2], self.recv.at[1], mp=self.far_mid),
-        )
-
-    def gather(self, block, slot, target):
-        return remote(self.out.at[block], self.out.at[block], self.send.at[slot], self.recv.at[4 + block], mp=target)
-
-    def start(self):
-        @pl.when(self.is_end)
-        def _():
-            for copy in self.end_sends():
-                copy.start()
-
-        @pl.when(self.is_mid)
-        def _():
-            self.mid_sends()[0].start()
-
-    def forward(self):
-        @pl.when(self.is_mid)
-        def _():
-            sends = self.mid_sends()
-            for i, block in ((0, self.far_end), (1, self.far_mid)):
-                remote(self.carry.at[i], self.carry.at[i], self.send.at[0], self.recv.at[2 + i], mp=self.end).wait_recv()
-                total = self.carry[i].astype(jnp.float32) + self.part[block].astype(jnp.float32)
-                self.carry[i] = total.astype(jnp.bfloat16)
-                sends[1 + i].start()
-
-    def total(self):
-        remote(self.single, self.single, self.send.at[0], self.recv.at[0], mp=self.mid).wait_recv()
-        remote(self.summed, self.summed, self.send.at[0], self.recv.at[1], mp=self.mid).wait_recv()
-        return (
-            self.part[self.me].astype(jnp.float32)
-            + self.single[...].astype(jnp.float32)
-            + self.summed[...].astype(jnp.float32)
-        )
-
-    def spread(self):
-        @pl.when(self.is_end)
-        def _():
-            self.gather(self.me, 3, self.mid).start()
-
-        @pl.when(self.is_mid)
-        def _():
-            self.gather(self.me, 3, self.end).start()
-            self.gather(self.me, 4, self.far_mid).start()
-
-    def wait_block(self, block):
-        self.gather(block, 3, self.mid).wait_recv()
-
-    def relay(self):
-        @pl.when(self.is_mid)
-        def _():
-            self.wait_block(self.end)
-            self.gather(self.end, 5, self.far_mid).start()
-            self.wait_block(self.far_mid)
-            self.gather(self.far_mid, 6, self.end).start()
-            self.wait_block(self.far_end)
-            self.gather(self.far_end, 7, self.end).start()
-
-    def arrive(self):
-        @pl.when(self.is_end)
-        def _():
-            self.wait_block(self.mid)
-            self.wait_block(self.far_mid)
-            self.wait_block(self.far_end)
-
-    def drain(self):
-        @pl.when(self.is_end)
-        def _():
-            for copy in self.end_sends():
-                copy.wait_send()
-            self.gather(self.me, 3, self.mid).wait_send()
-
-        @pl.when(self.is_mid)
-        def _():
-            for copy in self.mid_sends():
-                copy.wait_send()
-            for slot in range(3, 8):
-                self.gather(self.me, slot, self.end).wait_send()
-
-
-def line_scratch(tiles, rows, width):
-    block = pltpu.VMEM((tiles, rows, width), jnp.bfloat16)
-    return [
-        pltpu.VMEM((tiles, LINE, rows, width), jnp.bfloat16),
-        pltpu.VMEM((tiles, 2, rows, width), jnp.bfloat16),
-        block,
-        block,
-        pltpu.SemaphoreType.DMA((tiles, 8)),
-        pltpu.SemaphoreType.DMA((tiles, 8)),
-    ]
-
-
-class LineGather:
-    def __init__(self, place, send, recv, out):
-        self.place, self.send, self.recv, self.out = place, send, recv, out
-
-    def copy(self, block, slot, target):
-        return remote(self.out(block), self.out(block), self.send.at[slot], self.recv.at[block], mp=target)
-
-    def spread(self):
-        at = self.place
-
-        @pl.when(at.is_end)
-        def _():
-            self.copy(at.me, 0, at.mid).start()
-
-        @pl.when(at.is_mid)
-        def _():
-            self.copy(at.me, 0, at.end).start()
-            self.copy(at.me, 1, at.far_mid).start()
-
-    def relay(self):
-        at = self.place
-
-        @pl.when(at.is_mid)
-        def _():
-            self.copy(at.end, 2, at.far_mid).wait_recv()
-            self.copy(at.end, 2, at.far_mid).start()
-            self.copy(at.far_mid, 3, at.end).wait_recv()
-            self.copy(at.far_mid, 3, at.end).start()
-            self.copy(at.far_end, 4, at.end).wait_recv()
-            self.copy(at.far_end, 4, at.end).start()
-
-    def arrive(self):
-        at = self.place
-
-        @pl.when(at.is_end)
-        def _():
-            self.copy(at.mid, 0, at.mid).wait_recv()
-            self.copy(at.far_mid, 0, at.mid).wait_recv()
-            self.copy(at.far_end, 0, at.mid).wait_recv()
-
-    def drain(self):
-        at = self.place
-
-        @pl.when(at.is_end)
-        def _():
-            self.copy(at.me, 0, at.mid).wait_send()
-
-        @pl.when(at.is_mid)
-        def _():
-            for slot in range(5):
-                self.copy(at.me, slot, at.end).wait_send()
 
 
 class Place:
@@ -211,6 +42,152 @@
         self.end = jnp.where(left, 0, 3)
         self.far_mid = 3 - self.mid
         self.far_end = 3 - self.end
+
+
+class LineGather:
+    def __init__(self, place, send, recv, out):
+        self.at, self.send, self.recv, self.out = place, send, recv, out
+
+    def copy(self, block, slot, target):
+        return remote(self.out(block), self.out(block), self.send.at[slot], self.recv.at[block], mp=target)
+
+    def spread(self):
+        at = self.at
+
+        @pl.when(at.is_end)
+        def _():
+            self.copy(at.me, 0, at.mid).start()
+
+        @pl.when(at.is_mid)
+        def _():
+            self.copy(at.me, 0, at.end).start()
+            self.copy(at.me, 1, at.far_mid).start()
+
+    def relay(self, step):
+        at = self.at
+        block = (at.end, at.far_mid, at.far_end)[step]
+        target = (at.far_mid, at.end, at.end)[step]
+
+        @pl.when(at.is_mid)
+        def _():
+            self.copy(block, 2 + step, target).wait_recv()
+            self.copy(block, 2 + step, target).start()
+
+    def arrive(self):
+        at = self.at
+
+        @pl.when(at.is_end)
+        def _():
+            self.copy(at.mid, 0, at.mid).wait_recv()
+            self.copy(at.far_mid, 0, at.mid).wait_recv()
+            self.copy(at.far_end, 0, at.mid).wait_recv()
+
+    def drain(self):
+        at = self.at
+
+        @pl.when(at.is_end)
+        def _():
+            self.copy(at.me, 0, at.mid).wait_send()
+
+        @pl.when(at.is_mid)
+        def _():
+            for slot in range(5):
+                self.copy(at.me, slot, at.end).wait_send()
+
+
+class LineReduce:
+    def __init__(self, place, part, carry, single, summed, send, recv, start, block_rows, out):
+        self.at, self.carry, self.single, self.summed = place, carry, single, summed
+        self.send, self.recv = send, recv
+
+        def rows_of(block):
+            return pl.ds(pl.multiple_of(start + block * block_rows, 16), block_rows)
+
+        self.rows_of, self.part_ref, self.out_ref = rows_of, part, out
+        self.gather = LineGather(place, send.at[1], recv.at[1], lambda block: out.at[rows_of(block)])
+
+    def part(self, block):
+        return self.part_ref.at[self.rows_of(block)]
+
+    def end_sends(self):
+        at, send, recv = self.at, self.send, self.recv
+        return (
+            remote(self.part(at.far_end), self.carry.at[0], send.at[0, 0], recv.at[0, 2], mp=at.mid),
+            remote(self.part(at.far_mid), self.carry.at[1], send.at[0, 1], recv.at[0, 3], mp=at.mid),
+            remote(self.part(at.mid), self.single, send.at[0, 2], recv.at[0, 0], mp=at.mid),
+        )
+
+    def mid_sends(self):
+        at, send, recv = self.at, self.send, self.recv
+        return (
+            remote(self.carry.at[0], self.summed, send.at[0, 1], recv.at[0, 1], mp=at.far_end),
+            remote(self.carry.at[1], self.summed, send.at[0, 2], recv.at[0, 1], mp=at.far_mid),
+            remote(self.part(at.end), self.single, send.at[0, 0], recv.at[0, 0], mp=at.end),
+        )
+
+    def start(self):
+        @pl.when(self.at.is_end)
+        def _():
+            for copy in self.end_sends():
+                copy.start()
+
+        @pl.when(self.at.is_mid)
+        def _():
+            self.mid_sends()[2].start()
+
+    def forward(self, step):
+        at = self.at
+
+        @pl.when(at.is_mid)
+        def _():
+            block = (at.far_end, at.far_mid)[step]
+            self.end_sends()[step].wait_recv()
+            total = self.carry[step].astype(jnp.float32) + self.part(block)[...].astype(jnp.float32)
+            self.carry[step] = total.astype(jnp.bfloat16)
+            self.mid_sends()[step].start()
+
+    def settle(self, extra=None):
+        at = self.at
+        self.end_sends()[2].wait_recv()
+        self.mid_sends()[0].wait_recv()
+        total = (
+            self.part(at.me)[...].astype(jnp.float32)
+            + self.single[...].astype(jnp.float32)
+            + self.summed[...].astype(jnp.float32)
+        )
+        if extra is not None:
+            total = total + extra[self.rows_of(at.me), :]
+        self.out_ref[self.rows_of(at.me), :] = total.astype(jnp.bfloat16)
+        self.gather.spread()
+
+    def relay(self, step):
+        self.gather.relay(step)
+
+    def arrive(self):
+        self.gather.arrive()
+
+    def drain(self):
+        @pl.when(self.at.is_end)
+        def _():
+            for copy in self.end_sends():
+                copy.wait_send()
+
+        @pl.when(self.at.is_mid)
+        def _():
+            for copy in self.mid_sends():
+                copy.wait_send()
+
+        self.gather.drain()
+
+
+def line_scratch(rows, width):
+    return [
+        pltpu.VMEM((2, rows, width), jnp.bfloat16),
+        pltpu.VMEM((rows, width), jnp.bfloat16),
+        pltpu.VMEM((rows, width), jnp.bfloat16),
+        pltpu.SemaphoreType.DMA((2, 5)),
+        pltpu.SemaphoreType.DMA((2, 4)),
+    ]
 
 
 class PlaneReduce:
@@ -324,6 +301,11 @@
     return jnp.mean(value, axis=-1, keepdims=True)
 
 
+def portions_of(rows):
+    unit = rows // sum(PORTIONS)
+    return [(unit * sum(PORTIONS[:i]), unit * size) for i, size in enumerate(PORTIONS)]
+
+
 def layer_kernel(planar, layout, *refs):
     r = types.SimpleNamespace(**functools.reduce(operator.or_, jax.tree.unflatten(layout, refs)))
     tokens, rows, width = r.tokens, r.tokens.shape[0], r.tokens.shape[1]
@@ -331,8 +313,7 @@
     heads = local_width // HD
     pair = 2 * HD
     hidden_width = r.in_weight.shape[1]
-    tiles = rows // TILE
-    block_rows = TILE // LINE
+    spans = portions_of(rows)
     low, wide = jnp.bfloat16, jnp.float32
     at = Place()
     me = at.me
@@ -373,6 +354,8 @@
         )
 
     vec = r.vec
+    for i, name in enumerate((r.o_bias, r.gain1, r.shift1, r.in_bias, r.out_bias, r.gain2, r.shift2)):
+        vec[i, :] = name[...]
     o_bias, gain1, shift1, in_bias, out_bias, gain2, shift2 = (vec[i : i + 1, :] for i in range(7))
     wa, wb, wk = r.wa, r.wb, r.wk
     for h in range(heads):
@@ -400,10 +383,11 @@
         both = slice(h * pair, (h + 1) * pair)
         qcat[:, both] = jnp.where(entity, q_entity[:, both], q_plain[:, both]).astype(low)
 
-    pt, mx, mloc = r.pt, r.mx, r.mloc
+    pt, mx, mloc, st = r.pt, r.mx, r.mloc, r.st
     scale = HD ** (-0.5)
     gathers = [
-        LineGather(at, r.mx_send.at[q], r.mx_recv.at[q], lambda block, q=q: mx.at[block, q]) for q in range(tiles)
+        LineGather(at, r.mx_send.at[q], r.mx_recv.at[q], lambda block, q=q: mx[q].at[block])
+        for q in range(len(spans))
     ]
 
     def pair_of(h):
@@ -413,18 +397,25 @@
         return pl.ds(pl.multiple_of(h * HD, HD), HD)
 
     def attend(q):
-        span = slice(q * TILE, (q + 1) * TILE)
+        start, size = spans[q]
+        here = pl.ds(start, size)
 
         def head_step(h, carry):
-            raw = dot(kcat[:, pair_of(h)], qcat[span, pair_of(h)], 1, 1)
-            scores = jnp.where(seg_wide[...] == r.seg_row[:, span], raw * scale, -1000000000.0)
-            shifted = jnp.exp(scores - jnp.max(scores, axis=0, keepdims=True))
-            total = jnp.sum(shifted, axis=0, keepdims=True)
-            prob = (shifted * (1.0 / total)).astype(low)
-            pt[h, :, span] = prob
-            mixed = dot(vt[head_of(h), :], prob).astype(low)
-            mx[me, q, head_of(h), :] = mixed
-            mloc[head_of(h), span] = mixed
+            st[:, :size] = dot(kcat[:, pair_of(h)], qcat[here, pair_of(h)], 1, 1)
+
+            def soften(i, carry):
+                cols = pl.ds(pl.multiple_of(i * LANES, LANES), LANES)
+                span = pl.ds(pl.multiple_of(start + i * LANES, LANES), LANES)
+                scores = jnp.where(seg_wide[...] == r.seg_row[:, span], st[:, cols] * scale, -1000000000.0)
+                shifted = jnp.exp(scores - jnp.max(scores, axis=0, keepdims=True))
+                total = jnp.sum(shifted, axis=0, keepdims=True)
+                pt[h, :, span] = (shifted * (1.0 / total)).astype(low)
+                return carry
+
+            lax.fori_loop(0, size // LANES, soften, 0)
+            mixed = dot(vt[head_of(h), :], pt[h, :, here]).astype(low)
+            mx[q][me, head_of(h), :] = mixed
+            mloc[head_of(h), here] = mixed
             return carry
 
         lax.fori_loop(0, heads, head_step, 0)
@@ -449,33 +440,24 @@
     act, gp, dr2, gf, il, gb, tmp, acc = r.act, r.gp, r.dr2, r.gf, r.il, r.gb, r.tmp, r.acc
     acc[...] = jnp.zeros_like(acc)
 
-    def make_lines(parts, out):
-        part, carry, single, summed, send, recv = parts
+    def make_lines(parts, part, out):
         return [
-            LineReduce(part.at[q], carry.at[q], single.at[q], summed.at[q], out.at[q], send.at[q], recv.at[q])
-            for q in range(tiles)
+            LineReduce(at, part, *parts[q], start, size // LINE, out) for q, (start, size) in enumerate(spans)
         ]
 
-    ffn = make_lines(r.ffn, r.ffn_out)
-    back = make_lines(r.back, r.back_out)
-    grad = make_lines(r.grad, r.tokens_grad)
-
-    def put_part(line, value):
-        line.part[...] = value.astype(low).reshape(line.part.shape)
-
-    def settle(line):
-        line.forward()
-        line.out[me] = line.total().astype(low)
-        line.spread()
+    ffn = make_lines(r.ffn, r.ffn_part, r.ffn_out)
+    back = make_lines(r.back, r.back_part, r.back_out)
+    grad = make_lines(r.grad, r.grad_part, r.tokens_grad)
 
     root_half = math.sqrt(0.5)
     density = 1.0 / math.sqrt(2.0 * math.pi)
 
     def forward(q):
         gathers[q].arrive()
-        start = q * TILE
-        here = pl.ds(start, TILE)
-        tmp[...] = dot(mx[:, q].reshape(LINE * local_width, TILE), ow[...].reshape(LINE * local_width, width), 0, 0)
+        start, size = spans[q]
+        here = pl.ds(start, size)
+        mixed = mx[q][...].reshape(LINE * local_width, size)
+        tmp[:size, :] = dot(mixed, ow[...].reshape(LINE * local_width, width), 0, 0)
 
         def first_norm(at_rows, inside):
             value = tmp[inside, :] + tokens[at_rows, :].astype(wide) + o_bias
@@ -486,8 +468,8 @@
             rstd1[at_rows, :] = jnp.broadcast_to(scaled, (CHUNK, 128))
             hl[at_rows, :] = (normal * gain1 + shift1).astype(low)
 
-        rows_loop(start, TILE, first_norm)
-        tmp[...] = dot(hl[here, :], r.in_weight[...])
+        rows_loop(start, size, first_norm)
+        tmp[:size, :] = dot(hl[here, :], r.in_weight[...])
 
         def activate(at_rows, inside):
             inner = tmp[inside, :] + in_bias
@@ -495,19 +477,18 @@
             act[at_rows, :] = (inner * gate).astype(low)
             gp[at_rows, :] = gate + inner * (density * jnp.exp(-0.5 * inner * inner))
 
-        rows_loop(start, TILE, activate)
-        put_part(ffn[q], dot(act[here, :], r.out_weight[...]))
+        rows_loop(start, size, activate)
+        r.ffn_part[here, :] = dot(act[here, :], r.out_weight[...]).astype(low)
         ffn[q].start()
 
     def backward(q):
         ffn[q].arrive()
-        start = q * TILE
-        here = pl.ds(start, TILE)
-        tmp[...] = ffn[q].out[...].reshape(TILE, width).astype(wide)
+        start, size = spans[q]
+        here = pl.ds(start, size)
 
         def second_norm(at_rows, inside):
             value = xh1[at_rows, :] * gain1 + shift1
-            value = value + tmp[inside, :] + out_bias
+            value = value + r.ffn_out[at_rows, :].astype(wide) + out_bias
             centred = value - row_mean(value)
             scaled = lax.rsqrt(row_mean(centred * centred) + norm_epsilon)
             normal = centred * scaled
@@ -521,30 +502,28 @@
             dr2[at_rows, :] = grad_in
             gf[at_rows, :] = grad_in.astype(low)
 
-        rows_loop(start, TILE, second_norm)
-        tmp[...] = dot(gf[here, :], r.out_weight[...], 1, 1)
+        rows_loop(start, size, second_norm)
+        tmp[:size, :] = dot(gf[here, :], r.out_weight[...], 1, 1)
 
         def inner_step(at_rows, inside):
             d_inner = tmp[inside, :] * gp[at_rows, :]
             acc[3] += fold(d_inner)
             il[at_rows, :] = d_inner.astype(low)
 
-        rows_loop(start, TILE, inner_step)
-        put_part(back[q], dot(il[here, :], r.in_weight[...], 1, 1))
+        rows_loop(start, size, inner_step)
+        r.back_part[here, :] = dot(il[here, :], r.in_weight[...], 1, 1).astype(low)
         back[q].start()
 
     dqa, dqb, dkv, dk_sum, dv_sum = r.dqa, r.dqb, r.dkv, r.dk_sum, r.dv_sum
-    dmt = r.dmt
+    dmt, ds = r.dmt, r.ds
 
     def finish_rows(q):
         back[q].arrive()
-        start = q * TILE
-        here = pl.ds(start, TILE)
-        span = slice(start, start + TILE)
-        tmp[...] = back[q].out[...].reshape(TILE, width).astype(wide)
+        start, size = spans[q]
+        here = pl.ds(start, size)
 
         def last_norm(at_rows, inside):
-            d_hidden = dr2[at_rows, :] + tmp[inside, :]
+            d_hidden = dr2[at_rows, :] + r.back_out[at_rows, :].astype(wide)
             normal = xh1[at_rows, :]
             acc[2] += fold(d_hidden)
             acc[1] += fold(d_hidden * normal)
@@ -554,19 +533,26 @@
             dr2[at_rows, :] = grad_in
             gb[at_rows, :] = grad_in.astype(low)
 
-        rows_loop(start, TILE, last_norm)
-        dmt[...] = dot(r.o_weight[...], gb[here, :], 1, 1).astype(low)
-        row_entity = kind_wide[span, :] == 1
+        rows_loop(start, size, last_norm)
+        dmt[:, here] = dot(r.o_weight[...], gb[here, :], 1, 1).astype(low)
 
         def head_step(h, carry):
-            d_mixed = dmt[head_of(h), :]
-            d_prob = dot(vn[h], d_mixed)
-            prob_low = pt[h, :, span]
-            prob = prob_low.astype(wide)
-            delta = jnp.sum(prob * d_prob, axis=0, keepdims=True)
-            d_score = (prob * (d_prob - delta) * scale).astype(low)
-            d_value = dot(prob_low, d_mixed, 1, 1)
-            d_key = dot(d_score, qcat[span, pair_of(h)])
+            d_mixed = dmt[head_of(h), here]
+            st[:, :size] = dot(vn[h], d_mixed)
+
+            def harden(i, carry):
+                cols = pl.ds(pl.multiple_of(i * LANES, LANES), LANES)
+                span = pl.ds(pl.multiple_of(start + i * LANES, LANES), LANES)
+                prob = pt[h, :, span].astype(wide)
+                d_prob = st[:, cols]
+                delta = jnp.sum(prob * d_prob, axis=0, keepdims=True)
+                ds[:, cols] = (prob * (d_prob - delta) * scale).astype(low)
+                return carry
+
+            lax.fori_loop(0, size // LANES, harden, 0)
+            d_score = ds[:, :size]
+            d_value = dot(pt[h, :, here], d_mixed, 1, 1)
+            d_key = dot(d_score, qcat[here, pair_of(h)])
             if q == 0:
                 dv_sum[h] = d_value
                 dk_sum[h] = d_key
@@ -574,8 +560,9 @@
                 dv_sum[h] += d_value
                 dk_sum[h] += d_key
             d_query = dot(kct[pair_of(h), :], d_score).T
-            dqa[span, pair_of(h)] = jnp.where(row_entity, 0.0, d_query).astype(low)
-            dqb[span, pair_of(h)] = jnp.where(row_entity, d_query, 0.0).astype(low)
+            row_entity = kind_wide[here, :] == 1
+            dqa[here, pair_of(h)] = jnp.where(row_entity, 0.0, d_query).astype(low)
+            dqb[here, pair_of(h)] = jnp.where(row_entity, d_query, 0.0).astype(low)
             return carry
 
         lax.fori_loop(0, heads, head_step, 0)
@@ -590,37 +577,52 @@
         feed = PlaneReduce(gfeed, *r.feed)
         attn = PlaneReduce(gattn, *r.attn)
 
-    def feed_grads():
-        put_grad(gfeed, hidden_width, dot(gf[...], act[...], 0, 0))
-        put_grad(gfeed, 0, dot(hl[...], il[...], 0, 0))
-        if planar:
-            feed.start()
-
-    stages = (
-        attend,
-        lambda q: gathers[q].relay(),
-        forward,
-        lambda q: settle(ffn[q]),
-        lambda q: ffn[q].relay(),
-        backward,
-        lambda q: settle(back[q]),
-        lambda q: back[q].relay(),
-        finish_rows,
-    )
-    lag = (0, 2, 3, 4, 5, 6, 7, 8, 9)
-    for tick in range(tiles + lag[-1]):
-        if tick == 3:
-            swap_weights()
-            for copy in ow_swap:
-                copy.wait_recv()
-        for stage, late in reversed(tuple(zip(stages, lag))):
-            q = tick - late
-            if 0 <= q < tiles:
-                stage(q)
-        if tick == lag[-1] - 1:
-            turn()
-        if tick == tiles - 1 + lag[6]:
-            feed_grads()
+    attend(0)
+    attend(1)
+    turn()
+    for step in range(3):
+        gathers[0].relay(step)
+    swap_weights()
+    gathers[1].relay(0)
+    for copy in ow_swap:
+        copy.wait_recv()
+    forward(0)
+    gathers[1].relay(1)
+    gathers[1].relay(2)
+    ffn[0].forward(0)
+    forward(1)
+    ffn[0].forward(1)
+    ffn[0].settle()
+    ffn[1].forward(0)
+    ffn[0].relay(0)
+    ffn[0].relay(1)
+    ffn[1].forward(1)
+    ffn[0].relay(2)
+    ffn[1].settle()
+    backward(0)
+    ffn[1].relay(0)
+    ffn[1].relay(1)
+    back[0].forward(0)
+    ffn[1].relay(2)
+    back[0].forward(1)
+    back[0].settle()
+    backward(1)
+    back[0].relay(0)
+    back[0].relay(1)
+    back[0].relay(2)
+    back[1].forward(0)
+    put_grad(gfeed, hidden_width, dot(gf[...], act[...], 0, 0))
+    back[1].forward(1)
+    finish_rows(0)
+    back[1].settle()
+    put_grad(gfeed, 0, dot(hl[...], il[...], 0, 0))
+    if planar:
+        feed.start()
+    for step in range(3):
+        back[1].relay(step)
+    if planar:
+        feed.step_one()
+    finish_rows(1)
 
     small = r.small
     for i in range(8):
@@ -646,53 +648,48 @@
     d_values = [dv_sum[h].astype(low) for h in range(heads)]
     dkv[...] = jnp.concatenate(d_keys + d_values, axis=1)
     wkv = jnp.concatenate([r.k_weight[...], r.v_weight[...]], axis=0)
-    for q in range(tiles):
-        span = slice(q * TILE, (q + 1) * TILE)
-        put_part(grad[q], dot(dqa[span, :], wa[...]) + dot(dqb[span, :], wb[...]) + dot(dkv[span, :], wkv))
+    for q, (start, size) in enumerate(spans):
+        here = pl.ds(start, size)
+        share = dot(dqa[here, :], wa[...]) + dot(dqb[here, :], wb[...]) + dot(dkv[here, :], wkv)
+        r.grad_part[here, :] = share.astype(low)
         grad[q].start()
-
-    def settle_grad(q):
-        line = grad[q]
-        line.forward()
-        own = pl.ds(pl.multiple_of(q * TILE + me * block_rows, block_rows), block_rows)
-        line.out[me] = (line.total() + dr2[own, :]).astype(low)
-        line.spread()
-
-    if planar:
-        feed.step_one()
     put_grad(gattn, 0, dot(tok_t[...], dqa[...]))
     put_grad(gattn, 2 * local_width, dot(tok_t[...], dqb[...]))
-    settle_grad(0)
+    grad[0].forward(0)
     put_grad(gattn, 4 * local_width, dot(tok_t[...], dkv[...]))
     o_grad = dot(gb[...], mloc[...], 0, 1)
     pad = gattn.shape[2] - 7 * local_width
     put_grad(gattn, 6 * local_width, jnp.concatenate([o_grad, jnp.zeros((width, pad), wide)], axis=1))
+    grad[0].forward(1)
     if planar:
         attn.start()
-    settle_grad(1)
-    grad[0].relay()
-    if planar:
         tiny[0].wait_recv()
         small_sum[0] = small[...] + small_in[0]
         tiny[1].start()
         feed.step_two()
+    grad[0].settle(dr2)
+    grad[1].forward(0)
+    grad[0].relay(0)
+    grad[0].relay(1)
+    grad[1].forward(1)
+    if planar:
         attn.step_one()
-    for q in range(2, tiles):
-        settle_grad(q)
-        grad[q - 1].relay()
-        if planar and q == 2:
-            tiny[1].wait_recv()
-            small_sum[1] = small_sum[0] + small_in[1]
-            tiny[2].start()
-            feed_sum = feed.finish()
-            r.in_grad[...] = feed_sum[:, :hidden_width]
-            r.out_grad[...] = feed_sum[:, hidden_width:]
-        if planar and q == 3:
-            attn.step_two()
+        tiny[1].wait_recv()
+        small_sum[1] = small_sum[0] + small_in[1]
+        tiny[2].start()
+    grad[0].relay(2)
+    grad[1].settle(dr2)
+    if planar:
+        feed_sum = feed.finish()
+        r.in_grad[...] = feed_sum[:, :hidden_width]
+        r.out_grad[...] = feed_sum[:, hidden_width:]
+        attn.step_two()
+    grad[1].relay(0)
+    grad[1].relay(1)
     if planar:
         tiny[2].wait_recv()
         r.small_out[...] = small_sum[1] + small_in[2]
-    grad[tiles - 1].relay()
+    grad[1].relay(2)
     if planar:
         attn_sum = attn.finish()
         for part in range(4):
@@ -754,8 +751,8 @@
     planar = n_dp == 8
     blocks = 8
     per_block = width // blocks
-    tiles = rows // TILE
-    block_rows = TILE // LINE
+    spans = portions_of(rows)
+    largest = max(size for _, size in spans)
     low, wide = jnp.bfloat16, jnp.float32
     attn_width = -(-7 * local_width // 128) * 128
     args = dict(
@@ -766,7 +763,13 @@
         k_weight=k_weight.T,
         v_weight=v_weight.T,
         o_weight=o_weight,
-        vec=jnp.stack([o_bias, norm1_gain, norm1_shift, in_bias, out_bias, norm2_gain, norm2_shift, o_bias]),
+        o_bias=o_bias,
+        gain1=norm1_gain,
+        shift1=norm1_shift,
+        in_bias=in_bias,
+        out_bias=out_bias,
+        gain2=norm2_gain,
+        shift2=norm2_shift,
         in_weight=in_weight,
         out_weight=out_weight,
         cotangent=cotangent,
@@ -774,7 +777,7 @@
     shaped = jax.ShapeDtypeStruct
     outs = dict(
         layer_out=shaped((rows, width), low),
-        tokens_grad=shaped((tiles, LINE, block_rows, width), low),
+        tokens_grad=shaped((rows, width), low),
         small_out=shaped((8, width), wide),
     )
     if planar:
@@ -805,10 +808,12 @@
         kcat=pltpu.VMEM((rows, 2 * local_width), low),
         vt=pltpu.VMEM((local_width, rows), low),
         pt=pltpu.VMEM((heads, rows, rows), low),
-        mx=pltpu.VMEM((LINE, tiles, local_width, TILE), low),
+        mx=[pltpu.VMEM((LINE, local_width, size), low) for _, size in spans],
+        st=pltpu.VMEM((rows, largest), wide),
+        ds=pltpu.VMEM((rows, largest), low),
         mloc=pltpu.VMEM((local_width, rows), low),
-        mx_send=dma((tiles, 5)),
-        mx_recv=dma((tiles, LINE)),
+        mx_send=dma((len(spans), 5)),
+        mx_recv=dma((len(spans), LINE)),
         tok_t=pltpu.VMEM((width, rows), low),
         xh1=pltpu.VMEM((rows, width), wide),
         rstd1=pltpu.VMEM((rows, 128), wide),
@@ -818,17 +823,21 @@
         dr2=pltpu.VMEM((rows, width), wide),
         gf=pltpu.VMEM((rows, width), low),
         il=pltpu.VMEM((rows, hidden_width), low),
-        tmp=pltpu.VMEM((TILE, width), wide),
+        tmp=pltpu.VMEM((largest, width), wide),
+        vec=pltpu.VMEM((8, width), wide),
         acc=pltpu.VMEM((8, 8, width), wide),
         gb=pltpu.VMEM((rows, width), low),
-        ffn_out=pltpu.VMEM((tiles, LINE, block_rows, width), low),
-        back_out=pltpu.VMEM((tiles, LINE, block_rows, width), low),
+        ffn_part=pltpu.VMEM((rows, width), low),
+        back_part=pltpu.VMEM((rows, width), low),
+        grad_part=pltpu.VMEM((rows, width), low),
+        ffn_out=pltpu.VMEM((rows, width), low),
+        back_out=pltpu.VMEM((rows, width), low),
         gfeed=pltpu.VMEM((blocks, per_block, 2 * hidden_width), low),
         gattn=pltpu.VMEM((blocks, per_block, attn_width), low),
         small=pltpu.VMEM((8, width), wide),
         kct=pltpu.VMEM((2 * local_width, rows), low),
         vn=pltpu.VMEM((heads, rows, HD), low),
-        dmt=pltpu.VMEM((local_width, TILE), low),
+        dmt=pltpu.VMEM((local_width, rows), low),
         dk_sum=pltpu.VMEM((heads, rows, 2 * HD), wide),
         dv_sum=pltpu.VMEM((heads, rows, HD), wide),
         dqa=pltpu.VMEM((rows, 2 * local_width), low),
@@ -836,7 +845,7 @@
         dkv=pltpu.VMEM((rows, 2 * local_width), low),
     )
     for name in ("ffn", "back", "grad"):
-        scratch[name] = line_scratch(tiles, block_rows, width)
+        scratch[name] = [line_scratch(size // LINE, width) for _, size in spans]
     if planar:
         scratch |= dict(
             feed=plane_scratch(per_block, 2 * hidden_width),
@@ -861,7 +870,6 @@
     results = dict(zip(sorted(outs), results))
     if planar:
         small = results.pop("small_out")
-        results["tokens_grad"] = results["tokens_grad"].reshape(rows, width)
         flat, tree = jax.tree.flatten(results)
         flat = pl.pallas_call(
             hand_on,
@@ -895,7 +903,7 @@
     d_q, d_k, d_v, d_o, d_in, d_out = grads
     return (
         res.layer_out,
-        res.tokens_grad.reshape(rows, width),
+        res.tokens_grad,
         d_q,
         d_k,
         d_v,

time: 220 us -> 168 us (0.76)
  Pallas kernels: 212 us -> 166 us
  local copies, waits for them, and re-layouts: 7.14 us -> 1.67 us
    pallas_call x1, Pallas kernels: 208 us -> 162 us  [local(): pl.pallas_call(functools.partial(layer_kernel, planar, layout), out_shape...]
    another operation x8 -> x0, local copies, waits for them, and re-layouts: 5.47 us -> none  [local(): jnp.stack([o_bias, norm1_gain, norm1_shift, in_bias, out_bias, norm2_gain...]
where the time goes in v3:
time: 168 us
  Pallas kernels  166 us (99%)
    pallas_call x1, Pallas kernels, local(): pl.pallas_call(functools.partial(layer_kernel, planar, layout), out_shape...  162 us
    pallas_call x1, Pallas kernels, local(): pl.pallas_call(hand_on, out_shape=[shaped(a.shape, a.dtype) for a in flat...  3.6 us

profile of v3, /device:TPU:0, one launch (start us, length us, event | category | flops | bytes accessed | tf_op | source)
XLA Modules:
  0.0 167.8 jit_solution(7334550902505727831)
XLA Ops:
  0.7 161.9 %shard_map.280 = (f32[96,768]{1,0:T(8,128)}, f32[96,192]{1,0:T(8,128)}, bf16[640,768]{1,0:T(8,128)(2,1)}, f32[192,96]{1,0:T(8,128)}, f32[96,768]{1,0:T(8,128)}, ...) custom-call(bf16[640,768]{1,0:T(8,128)(2,1)} %refs_0_.1, ...), custom_call_target="tpu_custom_call" | custom-call | tf_op jit(solution)/shard_map/pallas_call | solution.py:860
  162.6 3.6 %shard_map.281 = (f32[96,768]{1,0:T(8,128)}, f32[96,192]{1,0:T(8,128)}, bf16[640,768]{1,0:T(8,128)(2,1)}, f32[192,96]{1,0:T(8,128)}, f32[96,768]{1,0:T(8,128)}, ...) custom-call(f32[96,768]{1,0:T(8,128)} %get-tuple-element.32.refs_0_, ...), custom_call_target="tpu_custom_call" | custom-call | tf_op jit(solution)/shard_map/pallas_call | solution.py:874
  166.2 1.7 slice_reduce_fusion

commit v4 on v3

--- a/solution.py
+++ b/solution.py
@@ -12,7 +12,7 @@
 
 HD = 64
 LINE = 4
-PORTIONS = (2, 3)
+PORTIONS = (1, 1, 1, 1, 1)
 LANES = 128
 CHUNK = 32
 VMEM_LIMIT = 67043328
@@ -322,36 +322,23 @@
     across = dp + 1 - 2 * core
 
     barrier = pltpu.get_barrier_semaphore()
-    peers = [{"mp": lax.rem(me + step, LINE)} for step in range(1, LINE)] + [{"dp": across}]
+    near = lax.rem(dp // 2, 2)
+    over_x = dp + 2 - 4 * near
+    peers = [{"mp": lax.rem(me + step, LINE)} for step in range(1, LINE)] + [{"dp": across}, {"dp": over_x}]
     if planar:
-        x, y = lax.rem(dp // 2, 2), dp // 4
-        over_x, over_y = dp + 2 - 4 * x, dp + 4 - 8 * y
-        peers += [{"dp": over_x}, {"dp": over_y}]
+        over_y = dp + 4 - 8 * (dp // 4)
+        peers += [{"dp": over_y}]
     for peer in peers:
         pl.semaphore_signal(barrier, inc=1, device_id=peer, device_id_type=pl.DeviceIdType.MESH)
-    pl.semaphore_wait(barrier, len(peers))
-
-    ow, ow_send, ow_recv = r.ow, r.ow_send, r.ow_recv
-    share = local_width // 2
-    mine = pl.ds(core * share, share)
-    ow_line = [
-        remote(
-            r.o_weight.at[mine],
-            ow.at[me, mine],
-            ow_send.at[step - 1],
-            ow_recv.at[step - 1],
-            mp=lax.rem(me + step, LINE),
+
+    late = [
+        pltpu.make_async_copy(source, target, r.late_sem.at[i])
+        for i, (source, target) in enumerate(
+            ((r.in_weight, r.in_w), (r.out_weight, r.out_w), (r.cotangent, r.cot_in))
         )
-        for step in range(1, LINE)
     ]
-    for copy in ow_line:
+    for copy in late:
         copy.start()
-    ow_swap = []
-    for step in range(1, LINE):
-        source = lax.rem(me + LINE - step, LINE)
-        ow_swap.append(
-            remote(ow.at[source, mine], ow.at[source, mine], ow_send.at[2 + step], ow_recv.at[2 + step], dp=across)
-        )
 
     vec = r.vec
     for i, name in enumerate((r.o_bias, r.gain1, r.shift1, r.in_bias, r.out_bias, r.gain2, r.shift2)):
@@ -365,6 +352,27 @@
         wb[both, :] = jnp.concatenate([r.q_weight[2, cols, :], r.q_weight[3, cols, :]], axis=0)
         key_part = r.k_weight[cols, :]
         wk[both, :] = jnp.concatenate([key_part, key_part], axis=0)
+    pl.semaphore_wait(barrier, len(peers))
+
+    ow, ow_send, ow_recv = r.ow, r.ow_send, r.ow_recv
+    share = local_width // 4
+    quarter = pl.ds(pl.multiple_of((2 * core + near) * share, 16), share)
+    pairs = pl.ds(pl.multiple_of(2 * core * share, 16), 2 * share)
+    ow_line, ow_plane, ow_chip = [], [], []
+    for step in range(1, LINE):
+        source, i = lax.rem(me + LINE - step, LINE), step - 1
+        ow_line.append(
+            remote(
+                r.o_weight.at[quarter], ow.at[me, quarter], ow_send.at[i], ow_recv.at[i], mp=lax.rem(me + step, LINE)
+            )
+        )
+        held = ow.at[source, quarter]
+        ow_plane.append(remote(held, held, ow_send.at[3 + i], ow_recv.at[3 + i], dp=over_x))
+        held = ow.at[source, pairs]
+        ow_chip.append(remote(held, held, ow_send.at[6 + i], ow_recv.at[6 + i], dp=across))
+    for copy in ow_line:
+        copy.start()
+
     kind_wide, seg_wide = r.kind_wide, r.seg_wide
     kind_wide[...] = jnp.broadcast_to(r.kind_row[...], (pair, rows)).T
     seg_wide[...] = jnp.broadcast_to(r.seg_row[...], (pair, rows)).T
@@ -421,12 +429,24 @@
         lax.fori_loop(0, heads, head_step, 0)
         gathers[q].spread()
 
-    def swap_weights():
+    def swap_plane():
+        ow[me] = r.o_weight[...]
         for copy in ow_line:
             copy.wait_recv()
-        for copy in ow_swap:
+        for copy in ow_plane:
             copy.start()
-        ow[me] = r.o_weight[...]
+
+    def swap_chip():
+        for copy in ow_plane:
+            copy.wait_recv()
+        for copy in ow_chip:
+            copy.start()
+
+    def own_weights():
+        for copy in ow_chip:
+            copy.wait_recv()
+        late[0].wait()
+        late[1].wait()
 
     tok_t, kct, vn = r.tok_t, r.kct, r.vn
 
@@ -469,7 +489,7 @@
             hl[at_rows, :] = (normal * gain1 + shift1).astype(low)
 
         rows_loop(start, size, first_norm)
-        tmp[:size, :] = dot(hl[here, :], r.in_weight[...])
+        tmp[:size, :] = dot(hl[here, :], r.in_w[...])
 
         def activate(at_rows, inside):
             inner = tmp[inside, :] + in_bias
@@ -478,7 +498,7 @@
             gp[at_rows, :] = gate + inner * (density * jnp.exp(-0.5 * inner * inner))
 
         rows_loop(start, size, activate)
-        r.ffn_part[here, :] = dot(act[here, :], r.out_weight[...]).astype(low)
+        r.ffn_part[here, :] = dot(act[here, :], r.out_w[...]).astype(low)
         ffn[q].start()
 
     def backward(q):
@@ -493,7 +513,7 @@
             scaled = lax.rsqrt(row_mean(centred * centred) + norm_epsilon)
             normal = centred * scaled
             r.layer_out[at_rows, :] = (normal * gain2 + shift2).astype(low)
-            cot = r.cotangent[at_rows, :].astype(wide)
+            cot = r.cot_in[at_rows, :].astype(wide)
             acc[6] += fold(cot)
             acc[5] += fold(cot * normal)
             grown = cot * gain2
@@ -503,7 +523,7 @@
             gf[at_rows, :] = grad_in.astype(low)
 
         rows_loop(start, size, second_norm)
-        tmp[:size, :] = dot(gf[here, :], r.out_weight[...], 1, 1)
+        tmp[:size, :] = dot(gf[here, :], r.out_w[...], 1, 1)
 
         def inner_step(at_rows, inside):
             d_inner = tmp[inside, :] * gp[at_rows, :]
@@ -511,7 +531,7 @@
             il[at_rows, :] = d_inner.astype(low)
 
         rows_loop(start, size, inner_step)
-        r.back_part[here, :] = dot(il[here, :], r.in_weight[...], 1, 1).astype(low)
+        r.back_part[here, :] = dot(il[here, :], r.in_w[...], 1, 1).astype(low)
         back[q].start()
 
     dqa, dqb, dkv, dk_sum, dv_sum = r.dqa, r.dqb, r.dkv, r.dk_sum, r.dv_sum
@@ -577,119 +597,229 @@
         feed = PlaneReduce(gfeed, *r.feed)
         attn = PlaneReduce(gattn, *r.attn)
 
-    attend(0)
-    attend(1)
-    turn()
-    for step in range(3):
-        gathers[0].relay(step)
-    swap_weights()
-    gathers[1].relay(0)
-    for copy in ow_swap:
-        copy.wait_recv()
-    forward(0)
-    gathers[1].relay(1)
-    gathers[1].relay(2)
-    ffn[0].forward(0)
-    forward(1)
-    ffn[0].forward(1)
-    ffn[0].settle()
-    ffn[1].forward(0)
-    ffn[0].relay(0)
-    ffn[0].relay(1)
-    ffn[1].forward(1)
-    ffn[0].relay(2)
-    ffn[1].settle()
-    backward(0)
-    ffn[1].relay(0)
-    ffn[1].relay(1)
-    back[0].forward(0)
-    ffn[1].relay(2)
-    back[0].forward(1)
-    back[0].settle()
-    backward(1)
-    back[0].relay(0)
-    back[0].relay(1)
-    back[0].relay(2)
-    back[1].forward(0)
-    put_grad(gfeed, hidden_width, dot(gf[...], act[...], 0, 0))
-    back[1].forward(1)
-    finish_rows(0)
-    back[1].settle()
-    put_grad(gfeed, 0, dot(hl[...], il[...], 0, 0))
+    small = r.small
     if planar:
-        feed.start()
-    for step in range(3):
-        back[1].relay(step)
-    if planar:
-        feed.step_one()
-    finish_rows(1)
-
-    small = r.small
-    for i in range(8):
-        small[i : i + 1, :] = jnp.sum(acc[i], axis=0, keepdims=True)
-    if planar:
-        small_in, partners = r.small_in, (across, over_x, over_y)
         small_sum = r.small_sum
         tiny = [
             remote(
                 small if s == 0 else small_sum.at[s - 1],
-                small_in.at[s],
+                r.small_in.at[s],
                 r.small_send.at[s],
                 r.small_recv.at[s],
-                dp=partners[s],
+                dp=(across, over_x, over_y)[s],
             )
             for s in range(3)
         ]
-        tiny[0].start()
-
-    d_keys = [
-        jnp.where(kind_wide[:, :HD] == 1, dk_sum[h, :, HD:], dk_sum[h, :, :HD]).astype(low) for h in range(heads)
-    ]
-    d_values = [dv_sum[h].astype(low) for h in range(heads)]
-    dkv[...] = jnp.concatenate(d_keys + d_values, axis=1)
-    wkv = jnp.concatenate([r.k_weight[...], r.v_weight[...]], axis=0)
-    for q, (start, size) in enumerate(spans):
+
+    def tiny_step(s):
+        if planar:
+            tiny[s].wait_recv()
+            small_sum[s] = (small if s == 0 else small_sum.at[s - 1])[...] + r.small_in[s]
+            if s < 2:
+                tiny[s + 1].start()
+
+    def feed_step(i):
+        if i == 0:
+            put_grad(gfeed, hidden_width, dot(gf[...], act[...], 0, 0))
+        elif i == 1:
+            put_grad(gfeed, 0, dot(hl[...], il[...], 0, 0))
+        elif planar and i == 2:
+            feed.start()
+        elif planar and i == 3:
+            feed.step_one()
+        elif planar and i == 4:
+            feed.step_two()
+        elif planar and i == 5:
+            feed_sum = feed.finish()
+            r.in_grad[...] = feed_sum[:, :hidden_width]
+            r.out_grad[...] = feed_sum[:, hidden_width:]
+
+    def key_grads():
+        for i in range(8):
+            small[i : i + 1, :] = jnp.sum(acc[i], axis=0, keepdims=True)
+        if planar:
+            tiny[0].start()
+        d_keys = [
+            jnp.where(kind_wide[:, :HD] == 1, dk_sum[h, :, HD:], dk_sum[h, :, :HD]).astype(low)
+            for h in range(heads)
+        ]
+        d_values = [dv_sum[h].astype(low) for h in range(heads)]
+        dkv[...] = jnp.concatenate(d_keys + d_values, axis=1)
+
+    def input_share(q):
+        start, size = spans[q]
         here = pl.ds(start, size)
-        share = dot(dqa[here, :], wa[...]) + dot(dqb[here, :], wb[...]) + dot(dkv[here, :], wkv)
+        share = dot(dqa[here, :], wa[...]) + dot(dqb[here, :], wb[...])
+        share = share + dot(dkv[here, :local_width], r.k_weight[...]) + dot(dkv[here, local_width:], r.v_weight[...])
         r.grad_part[here, :] = share.astype(low)
         grad[q].start()
-    put_grad(gattn, 0, dot(tok_t[...], dqa[...]))
-    put_grad(gattn, 2 * local_width, dot(tok_t[...], dqb[...]))
+
+    def attn_step(i):
+        if i == 0:
+            put_grad(gattn, 0, dot(tok_t[...], dqa[...]))
+            put_grad(gattn, 2 * local_width, dot(tok_t[...], dqb[...]))
+        elif i == 1:
+            put_grad(gattn, 4 * local_width, dot(tok_t[...], dkv[...]))
+            o_grad = dot(gb[...], mloc[...], 0, 1)
+            pad = gattn.shape[2] - 7 * local_width
+            put_grad(gattn, 6 * local_width, jnp.concatenate([o_grad, jnp.zeros((width, pad), wide)], axis=1))
+        elif planar and i == 2:
+            attn.start()
+            tiny_step(0)
+        elif planar and i == 3:
+            attn.step_one()
+            tiny_step(1)
+        elif planar and i == 4:
+            attn.step_two()
+            tiny_step(2)
+
+    attend(0)
+    attend(1)
+    gathers[0].relay(0)
+    gathers[0].relay(1)
+    swap_plane()
+    attend(2)
+    gathers[1].relay(0)
+    gathers[0].relay(2)
+    attend(3)
+    gathers[3].relay(0)
+    gathers[1].relay(1)
+    gathers[1].relay(2)
+    attend(4)
+    gathers[4].relay(0)
+    swap_chip()
+    gathers[3].relay(1)
+    gathers[3].relay(2)
+    gathers[2].relay(0)
+    gathers[4].relay(1)
+    gathers[4].relay(2)
+    gathers[2].relay(1)
+    own_weights()
+    forward(0)
+    ffn[0].forward(0)
+    ffn[0].forward(1)
+    gathers[2].relay(2)
+    forward(1)
+    ffn[1].forward(0)
+    forward(3)
+    ffn[3].forward(0)
+    ffn[1].forward(1)
+    forward(4)
+    ffn[0].settle()
+    ffn[3].forward(1)
+    ffn[4].forward(0)
+    forward(2)
+    ffn[0].relay(0)
+    ffn[1].settle()
+    ffn[2].forward(0)
+    ffn[2].forward(1)
+    ffn[0].relay(1)
+    ffn[0].relay(2)
+    ffn[1].relay(0)
+    ffn[3].settle()
+    ffn[1].relay(1)
+    ffn[4].forward(1)
+    ffn[3].relay(0)
+    ffn[1].relay(2)
+    ffn[2].settle()
+    ffn[2].relay(0)
+    ffn[3].relay(1)
+    ffn[3].relay(2)
+    ffn[4].settle()
+    ffn[4].relay(0)
+    ffn[2].relay(1)
+    late[2].wait()
+    backward(0)
+    back[0].forward(0)
+    ffn[2].relay(2)
+    back[0].forward(1)
+    backward(1)
+    ffn[4].relay(1)
+    back[1].forward(0)
+    backward(3)
+    back[1].forward(1)
+    ffn[4].relay(2)
+    back[3].forward(0)
+    back[0].settle()
+    backward(2)
+    back[0].relay(0)
+    back[3].forward(1)
+    back[1].settle()
+    back[2].forward(0)
+    back[2].forward(1)
+    back[0].relay(1)
+    backward(4)
+    back[1].relay(0)
+    back[3].settle()
+    feed_step(0)
+    back[4].forward(0)
+    back[1].relay(1)
+    back[4].forward(1)
+    back[0].relay(2)
+    back[2].settle()
+    turn()
+    back[1].relay(2)
+    back[3].relay(0)
+    back[2].relay(0)
+    back[4].settle()
+    back[2].relay(1)
+    feed_step(1)
+    back[2].relay(2)
+    back[3].relay(1)
+    back[3].relay(2)
+    feed_step(2)
+    back[4].relay(0)
+    finish_rows(0)
+    back[4].relay(1)
+    finish_rows(1)
+    back[4].relay(2)
+    finish_rows(2)
+    finish_rows(3)
+    finish_rows(4)
+    key_grads()
+    input_share(0)
+    input_share(1)
+    input_share(2)
+    input_share(3)
     grad[0].forward(0)
-    put_grad(gattn, 4 * local_width, dot(tok_t[...], dkv[...]))
-    o_grad = dot(gb[...], mloc[...], 0, 1)
-    pad = gattn.shape[2] - 7 * local_width
-    put_grad(gattn, 6 * local_width, jnp.concatenate([o_grad, jnp.zeros((width, pad), wide)], axis=1))
+    feed_step(3)
     grad[0].forward(1)
-    if planar:
-        attn.start()
-        tiny[0].wait_recv()
-        small_sum[0] = small[...] + small_in[0]
-        tiny[1].start()
-        feed.step_two()
+    input_share(4)
+    attn_step(0)
+    grad[1].forward(0)
+    grad[1].forward(1)
+    attn_step(1)
+    grad[2].forward(0)
+    grad[2].forward(1)
     grad[0].settle(dr2)
-    grad[1].forward(0)
+    attn_step(2)
+    grad[3].forward(0)
+    grad[3].forward(1)
+    grad[2].settle(dr2)
+    grad[4].forward(0)
+    attn_step(3)
+    grad[4].forward(1)
+    grad[1].settle(dr2)
+    feed_step(4)
+    grad[3].settle(dr2)
     grad[0].relay(0)
     grad[0].relay(1)
-    grad[1].forward(1)
-    if planar:
-        attn.step_one()
-        tiny[1].wait_recv()
-        small_sum[1] = small_sum[0] + small_in[1]
-        tiny[2].start()
+    grad[4].settle(dr2)
+    grad[2].relay(0)
+    grad[1].relay(0)
+    grad[2].relay(1)
+    grad[1].relay(1)
+    grad[3].relay(0)
+    grad[4].relay(0)
     grad[0].relay(2)
-    grad[1].settle(dr2)
-    if planar:
-        feed_sum = feed.finish()
-        r.in_grad[...] = feed_sum[:, :hidden_width]
-        r.out_grad[...] = feed_sum[:, hidden_width:]
-        attn.step_two()
-    grad[1].relay(0)
-    grad[1].relay(1)
-    if planar:
-        tiny[2].wait_recv()
-        r.small_out[...] = small_sum[1] + small_in[2]
+    grad[3].relay(1)
+    grad[2].relay(2)
+    attn_step(4)
+    grad[4].relay(1)
     grad[1].relay(2)
+    grad[3].relay(2)
+    grad[4].relay(2)
+    feed_step(5)
     if planar:
         attn_sum = attn.finish()
         for part in range(4):
@@ -701,6 +831,7 @@
         r.k_grad[...] = both_grads[:, :local_width]
         r.v_grad[...] = both_grads[:, local_width:]
         r.o_grad[...] = attn_sum[:, 6 * local_width : 7 * local_width].T
+        r.small_out[...] = small_sum[2]
     else:
         r.small_out[...] = small[...]
         r.feed_out[...] = gfeed[...]
@@ -711,17 +842,22 @@
         line.drain()
     for gather in gathers:
         gather.drain()
-    for copy in ow_line + ow_swap:
+    for copy in ow_line + ow_plane + ow_chip:
         copy.wait_send()
     if planar:
         for copy in tiny:
             copy.wait_send()
 
 
-def hand_on(*refs):
-    count = len(refs) // 2
-    for source, target in zip(refs[:count], refs[count:]):
-        target[...] = source[...]
+def hand_on(count, vectors, small, *refs):
+    sources, targets, rows_out, sems = refs[:count], refs[count : 2 * count], refs[2 * count : -1], refs[-1]
+    copies = [pltpu.make_async_copy(sources[i], targets[i], sems.at[i]) for i in range(count)]
+    for copy in copies:
+        copy.start()
+    for i in range(vectors):
+        rows_out[i][...] = small[i, :]
+    for copy in copies:
+        copy.wait()
 
 
 def local(
@@ -797,8 +933,8 @@
     dma = pltpu.SemaphoreType.DMA
     scratch = dict(
         ow=pltpu.VMEM((LINE, local_width, width), low),
-        ow_send=dma((6,)),
-        ow_recv=dma((6,)),
+        ow_send=dma((9,)),
+        ow_recv=dma((9,)),
         wa=pltpu.VMEM((2 * local_width, width), low),
         wb=pltpu.VMEM((2 * local_width, width), low),
         wk=pltpu.VMEM((2 * local_width, width), low),
@@ -823,6 +959,10 @@
         dr2=pltpu.VMEM((rows, width), wide),
         gf=pltpu.VMEM((rows, width), low),
         il=pltpu.VMEM((rows, hidden_width), low),
+        in_w=pltpu.VMEM((width, hidden_width), low),
+        out_w=pltpu.VMEM((hidden_width, width), low),
+        cot_in=pltpu.VMEM((rows, width), low),
+        late_sem=dma((3,)),
         tmp=pltpu.VMEM((largest, width), wide),
         vec=pltpu.VMEM((8, width), wide),
         acc=pltpu.VMEM((8, 8, width), wide),
@@ -851,16 +991,16 @@
             feed=plane_scratch(per_block, 2 * hidden_width),
             attn=plane_scratch(per_block, attn_width),
             small_in=pltpu.VMEM((3, 8, width), wide),
-            small_sum=pltpu.VMEM((2, 8, width), wide),
+            small_sum=pltpu.VMEM((3, 8, width), wide),
             small_send=dma((3,)),
             small_recv=dma((3,)),
         )
     layout = jax.tree.structure((args, outs, scratch))
-    vm = pl.BlockSpec(memory_space=pltpu.VMEM)
+    vm, far = pl.BlockSpec(memory_space=pltpu.VMEM), pl.BlockSpec(memory_space=pl.ANY)
     results = pl.pallas_call(
         functools.partial(layer_kernel, planar, layout),
         out_shape=jax.tree.leaves(outs),
-        in_specs=[vm] * len(args),
+        in_specs=[far if name in ("in_weight", "out_weight", "cotangent") else vm for name in sorted(args)],
         out_specs=[vm] * len(outs),
         scratch_shapes=jax.tree.leaves(scratch),
         compiler_params=pltpu.CompilerParams(
@@ -871,16 +1011,18 @@
     if planar:
         small = results.pop("small_out")
         flat, tree = jax.tree.flatten(results)
+        vectors = small.shape[0] - 1
         flat = pl.pallas_call(
-            hand_on,
-            out_shape=[shaped(a.shape, a.dtype) for a in flat],
-            in_specs=[vm] * len(flat),
-            out_specs=[vm] * len(flat),
-            compiler_params=pltpu.CompilerParams(vmem_limit_bytes=VMEM_LIMIT),
-        )(*flat)
-        results = jax.tree.unflatten(tree, flat) | {"small_out": small}
+            functools.partial(hand_on, len(flat), vectors),
+            out_shape=[shaped(a.shape, a.dtype) for a in flat] + [shaped((width,), wide)] * vectors,
+            in_specs=[vm] * (1 + len(flat)),
+            out_specs=[far] * len(flat) + [vm] * vectors,
+            scratch_shapes=[dma((len(flat),))],
+            compiler_params=pltpu.CompilerParams(vmem_limit_bytes=16 * 1024 * 1024),
+        )(small, *flat)
+        small = flat[len(results) :]
+        results = jax.tree.unflatten(tree, flat[: len(results)])
     res = types.SimpleNamespace(**results)
-    small = res.small_out
     if planar:
         grads = (res.q_grad, res.k_grad, res.v_grad, res.o_grad, res.in_grad, res.out_grad.T)
     else:
@@ -888,7 +1030,7 @@
         attn = res.attn_out.astype(wide).reshape(width, attn_width)
         feed = lax.psum_scatter(feed, "dp", scatter_dimension=0, tiled=True)
         attn = lax.psum_scatter(attn, "dp", scatter_dimension=0, tiled=True)
-        small = lax.psum(small, "dp")
+        small = lax.psum(res.small_out, "dp")
         per = feed.shape[0]
         queries = attn[:, : 4 * local_width].reshape(per, 2, heads, 2, HD)
         queries = queries.transpose(1, 3, 0, 2, 4).reshape(4, per, local_width)

time: 168 us -> 139 us (0.83)
  Pallas kernels: 166 us -> 129 us
  local copies, waits for them, and re-layouts: 1.67 us -> 8.73 us
    pallas_call x1, Pallas kernels: 162 us -> 127 us  [local(): pl.pallas_call(functools.partial(layer_kernel, planar, layout), out_shape...]
    unnamed x0 -> x18, local copies, waits for them, and re-layouts: none -> 8.73 us
where the time goes in v4:
time: 139 us
  Pallas kernels  129 us (93%)
  local copies, waits for them, and re-layouts  8.73 us (6%)
    pallas_call x1, Pallas kernels, local(): pl.pallas_call(functools.partial(layer_kernel, planar, layout), out_shape...  127 us
    unnamed x18, local copies, waits for them, and re-layouts  8.73 us

profile of v4, /device:TPU:0, one launch (start us, length us, event | category | flops | bytes accessed | tf_op | source)
XLA Modules:
  0.0 138.7 jit_solution(1864560395198561044)
XLA Ops:
  0.7 126.8 %shard_map.280 = (f32[96,768]{1,0:T(8,128)}, f32[96,192]{1,0:T(8,128)}, bf16[640,768]{1,0:T(8,128)(2,1)}, f32[192,96]{1,0:T(8,128)}, f32[96,768]{1,0:T(8,128)}, ...) custom-call(bf16[640,768]{1,0:T(8,128)(2,1)} %refs_0_.1, ...), custom_call_target="tpu_custom_call" | custom-call | tf_op jit(solution)/shard_map/pallas_call | solution.py:1000
  127.4 0.0 copy-start
  127.4 1.2 copy-done
  128.6 0.0 copy-start.1
  128.6 1.2 copy-done.1
  129.8 0.0 copy-start.2
  129.8 1.0 copy-done.2
  130.8 0.0 copy-start.3
  130.8 1.0 copy-done.3
  131.8 0.0 copy-start.4
  131.8 1.0 copy-done.4
  132.8 0.0 copy-start.5
  132.8 0.9 copy-done.5
  133.7 0.0 copy-start.6
  133.7 0.9 copy-done.6
  134.5 0.0 copy-start.7
  134.5 0.9 copy-done.7
  135.4 0.0 copy-start.8
  135.4 0.7 copy-done.8
  136.2 2.3 %shard_map.281 = (f32[96,768]{1,0:T(8,128)}, f32[96,192]{1,0:T(8,128)}, bf16[640,768]{1,0:T(8,128)(2,1)}, f32[192,96]{1,0:T(8,128)}, f32[96,768]{1,0:T(8,128)}, ...) custom-call(f32[8,768]{1,0:T(8,128)S(1)} %copy-done.8, ...), custom_call_target="tpu_custom_call" | custom-call | tf_op jit(solution)/shard_map/pallas_call | solution.py:1015
Async XLA Ops:
  127.4 1.2 copy-start
  128.6 1.2 copy-start.1
  129.8 1.0 copy-start.2
  130.8 1.0 copy-start.3
  131.8 1.0 copy-start.4
  132.8 0.9 copy-start.5
  133.7 0.9 copy-start.6
  134.5 0.9 copy-start.7
  135.4 0.7 copy-start.8

commit v5 on v4

--- a/solution.py
+++ b/solution.py
@@ -307,7 +307,19 @@
 
 
 def layer_kernel(planar, layout, *refs):
-    r = types.SimpleNamespace(**functools.reduce(operator.or_, jax.tree.unflatten(layout, refs)))
+    given, wanted, scratch = jax.tree.unflatten(layout, refs)
+    r = types.SimpleNamespace(**scratch, **scratch["held"], **scratch["made"])
+    loads = {
+        name: pltpu.make_async_copy(given[name], r.held[name], r.load_sem.at[i]) for i, name in enumerate(given)
+    }
+    stores = {
+        name: pltpu.make_async_copy(r.made[name], wanted[name], r.store_sem.at[i]) for i, name in enumerate(wanted)
+    }
+
+    def need(*names):
+        for name in names:
+            loads[name].wait()
+
     tokens, rows, width = r.tokens, r.tokens.shape[0], r.tokens.shape[1]
     local_width = r.k_weight.shape[0]
     heads = local_width // HD
@@ -331,20 +343,12 @@
     for peer in peers:
         pl.semaphore_signal(barrier, inc=1, device_id=peer, device_id_type=pl.DeviceIdType.MESH)
 
-    late = [
-        pltpu.make_async_copy(source, target, r.late_sem.at[i])
-        for i, (source, target) in enumerate(
-            ((r.in_weight, r.in_w), (r.out_weight, r.out_w), (r.cotangent, r.cot_in))
-        )
-    ]
-    for copy in late:
-        copy.start()
-
-    vec = r.vec
-    for i, name in enumerate((r.o_bias, r.gain1, r.shift1, r.in_bias, r.out_bias, r.gain2, r.shift2)):
-        vec[i, :] = name[...]
-    o_bias, gain1, shift1, in_bias, out_bias, gain2, shift2 = (vec[i : i + 1, :] for i in range(7))
+    first = ("k_weight", "tokens", "kind_row", "seg_row", "v_weight", "q_weight", "o_weight")
+    for name in first + tuple(name for name in loads if name not in first):
+        loads[name].start()
+
     wa, wb, wk = r.wa, r.wb, r.wk
+    need("k_weight", "q_weight")
     for h in range(heads):
         cols = slice(h * HD, (h + 1) * HD)
         both = slice(h * pair, (h + 1) * pair)
@@ -352,9 +356,12 @@
         wb[both, :] = jnp.concatenate([r.q_weight[2, cols, :], r.q_weight[3, cols, :]], axis=0)
         key_part = r.k_weight[cols, :]
         wk[both, :] = jnp.concatenate([key_part, key_part], axis=0)
+    need("o_weight")
     pl.semaphore_wait(barrier, len(peers))
 
     ow, ow_send, ow_recv = r.ow, r.ow_send, r.ow_recv
+    vec = r.vec
+    o_bias, gain1, shift1, in_bias, out_bias, gain2, shift2 = (vec.at[i : i + 1] for i in range(7))
     share = local_width // 4
     quarter = pl.ds(pl.multiple_of((2 * core + near) * share, 16), share)
     pairs = pl.ds(pl.multiple_of(2 * core * share, 16), 2 * share)
@@ -373,10 +380,12 @@
     for copy in ow_line:
         copy.start()
 
+    need("kind_row", "seg_row")
     kind_wide, seg_wide = r.kind_wide, r.seg_wide
     kind_wide[...] = jnp.broadcast_to(r.kind_row[...], (pair, rows)).T
     seg_wide[...] = jnp.broadcast_to(r.seg_row[...], (pair, rows)).T
     qcat, kcat, vt = r.qcat, r.kcat, r.vt
+    need("tokens", "v_weight")
     tok = tokens[...]
     entity = kind_wide[...] == 1
     upper = lax.broadcasted_iota(jnp.int32, (rows, pair), 1) >= HD
@@ -445,8 +454,9 @@
     def own_weights():
         for copy in ow_chip:
             copy.wait_recv()
-        late[0].wait()
-        late[1].wait()
+        need("in_weight", "out_weight", "o_bias", "gain1", "shift1", "in_bias", "out_bias", "gain2", "shift2")
+        for i, name in enumerate((r.o_bias, r.gain1, r.shift1, r.in_bias, r.out_bias, r.gain2, r.shift2)):
+            vec[i, :] = name[...]
 
     tok_t, kct, vn = r.tok_t, r.kct, r.vn
 
@@ -480,25 +490,25 @@
         tmp[:size, :] = dot(mixed, ow[...].reshape(LINE * local_width, width), 0, 0)
 
         def first_norm(at_rows, inside):
-            value = tmp[inside, :] + tokens[at_rows, :].astype(wide) + o_bias
+            value = tmp[inside, :] + tokens[at_rows, :].astype(wide) + o_bias[...]
             centred = value - row_mean(value)
             scaled = lax.rsqrt(row_mean(centred * centred) + norm_epsilon)
             normal = centred * scaled
             xh1[at_rows, :] = normal
             rstd1[at_rows, :] = jnp.broadcast_to(scaled, (CHUNK, 128))
-            hl[at_rows, :] = (normal * gain1 + shift1).astype(low)
+            hl[at_rows, :] = (normal * gain1[...] + shift1[...]).astype(low)
 
         rows_loop(start, size, first_norm)
-        tmp[:size, :] = dot(hl[here, :], r.in_w[...])
+        tmp[:size, :] = dot(hl[here, :], r.in_weight[...])
 
         def activate(at_rows, inside):
-            inner = tmp[inside, :] + in_bias
+            inner = tmp[inside, :] + in_bias[...]
             gate = 0.5 + 0.5 * lax.erf(inner * root_half)
             act[at_rows, :] = (inner * gate).astype(low)
             gp[at_rows, :] = gate + inner * (density * jnp.exp(-0.5 * inner * inner))
 
         rows_loop(start, size, activate)
-        r.ffn_part[here, :] = dot(act[here, :], r.out_w[...]).astype(low)
+        r.ffn_part[here, :] = dot(act[here, :], r.out_weight[...]).astype(low)
         ffn[q].start()
 
     def backward(q):
@@ -507,23 +517,23 @@
         here = pl.ds(start, size)
 
         def second_norm(at_rows, inside):
-            value = xh1[at_rows, :] * gain1 + shift1
-            value = value + r.ffn_out[at_rows, :].astype(wide) + out_bias
+            value = xh1[at_rows, :] * gain1[...] + shift1[...]
+            value = value + r.ffn_out[at_rows, :].astype(wide) + out_bias[...]
             centred = value - row_mean(value)
             scaled = lax.rsqrt(row_mean(centred * centred) + norm_epsilon)
             normal = centred * scaled
-            r.layer_out[at_rows, :] = (normal * gain2 + shift2).astype(low)
-            cot = r.cot_in[at_rows, :].astype(wide)
+            r.layer_out[at_rows, :] = (normal * gain2[...] + shift2[...]).astype(low)
+            cot = r.cotangent[at_rows, :].astype(wide)
             acc[6] += fold(cot)
             acc[5] += fold(cot * normal)
-            grown = cot * gain2
+            grown = cot * gain2[...]
             grad_in = scaled * (grown - row_mean(grown) - normal * row_mean(grown * normal))
             acc[4] += fold(grad_in)
             dr2[at_rows, :] = grad_in
             gf[at_rows, :] = grad_in.astype(low)
 
         rows_loop(start, size, second_norm)
-        tmp[:size, :] = dot(gf[here, :], r.out_w[...], 1, 1)
+        tmp[:size, :] = dot(gf[here, :], r.out_weight[...], 1, 1)
 
         def inner_step(at_rows, inside):
             d_inner = tmp[inside, :] * gp[at_rows, :]
@@ -531,7 +541,7 @@
             il[at_rows, :] = d_inner.astype(low)
 
         rows_loop(start, size, inner_step)
-        r.back_part[here, :] = dot(il[here, :], r.in_w[...], 1, 1).astype(low)
+        r.back_part[here, :] = dot(il[here, :], r.in_weight[...], 1, 1).astype(low)
         back[q].start()
 
     dqa, dqb, dkv, dk_sum, dv_sum = r.dqa, r.dqb, r.dkv, r.dk_sum, r.dv_sum
@@ -547,7 +557,7 @@
             normal = xh1[at_rows, :]
             acc[2] += fold(d_hidden)
             acc[1] += fold(d_hidden * normal)
-            grown = d_hidden * gain1
+            grown = d_hidden * gain1[...]
             grad_in = rstd1[at_rows, 0:1] * (grown - row_mean(grown) - normal * row_mean(grown * normal))
             acc[0] += fold(grad_in)
             dr2[at_rows, :] = grad_in
@@ -633,6 +643,8 @@
             feed_sum = feed.finish()
             r.in_grad[...] = feed_sum[:, :hidden_width]
             r.out_grad[...] = feed_sum[:, hidden_width:]
+            stores["in_grad"].start()
+            stores["out_grad"].start()
 
     def key_grads():
         for i in range(8):
@@ -728,7 +740,7 @@
     ffn[4].settle()
     ffn[4].relay(0)
     ffn[2].relay(1)
-    late[2].wait()
+    need("cotangent")
     backward(0)
     back[0].forward(0)
     ffn[2].relay(2)
@@ -749,6 +761,7 @@
     back[2].forward(1)
     back[0].relay(1)
     backward(4)
+    stores["layer_out"].start()
     back[1].relay(0)
     back[3].settle()
     feed_step(0)
@@ -832,12 +845,17 @@
         r.v_grad[...] = both_grads[:, local_width:]
         r.o_grad[...] = attn_sum[:, 6 * local_width : 7 * local_width].T
         r.small_out[...] = small_sum[2]
+        for name in ("q_grad", "k_grad", "v_grad", "o_grad", "small_out"):
+            stores[name].start()
     else:
         r.small_out[...] = small[...]
         r.feed_out[...] = gfeed[...]
         r.attn_out[...] = gattn[...]
+        for name in ("small_out", "feed_out", "attn_out"):
+            stores[name].start()
     for line in grad:
         line.arrive()
+    stores["tokens_grad"].start()
     for line in ffn + back + grad:
         line.drain()
     for gather in gathers:
@@ -847,16 +865,29 @@
     if planar:
         for copy in tiny:
             copy.wait_send()
-
-
-def hand_on(count, vectors, small, *refs):
-    sources, targets, rows_out, sems = refs[:count], refs[count : 2 * count], refs[2 * count : -1], refs[-1]
-    copies = [pltpu.make_async_copy(sources[i], targets[i], sems.at[i]) for i in range(count)]
-    for copy in copies:
+    for copy in stores.values():
+        copy.wait()
+
+
+def hand_on(layout, *refs):
+    sources, targets, held, lines, sems = jax.tree.unflatten(layout, refs)
+    count = len(sources) - 1
+    small = held[0]
+    fetch = [pltpu.make_async_copy(source, kept, sems.at[0, i]) for i, (source, kept) in enumerate(zip(sources, held))]
+    store = [
+        pltpu.make_async_copy(kept, target, sems.at[1, i])
+        for i, (kept, target) in enumerate(zip(list(held[1:]) + list(lines), targets))
+    ]
+    for copy in fetch:
         copy.start()
-    for i in range(vectors):
-        rows_out[i][...] = small[i, :]
-    for copy in copies:
+    fetch[0].wait()
+    for i, line in enumerate(lines):
+        line[...] = small[i, :]
+        store[count + i].start()
+    for i in range(count):
+        fetch[1 + i].wait()
+        store[i].start()
+    for copy in store:
         copy.wait()
 
 
@@ -959,10 +990,6 @@
         dr2=pltpu.VMEM((rows, width), wide),
         gf=pltpu.VMEM((rows, width), low),
         il=pltpu.VMEM((rows, hidden_width), low),
-        in_w=pltpu.VMEM((width, hidden_width), low),
-        out_w=pltpu.VMEM((hidden_width, width), low),
-        cot_in=pltpu.VMEM((rows, width), low),
-        late_sem=dma((3,)),
         tmp=pltpu.VMEM((largest, width), wide),
         vec=pltpu.VMEM((8, width), wide),
         acc=pltpu.VMEM((8, 8, width), wide),
@@ -995,13 +1022,19 @@
             small_send=dma((3,)),
             small_recv=dma((3,)),
         )
+    scratch |= dict(
+        held={name: pltpu.VMEM(a.shape, a.dtype) for name, a in args.items()},
+        made={name: pltpu.VMEM(a.shape, a.dtype) for name, a in outs.items()},
+        load_sem=dma((len(args),)),
+        store_sem=dma((len(outs),)),
+    )
     layout = jax.tree.structure((args, outs, scratch))
     vm, far = pl.BlockSpec(memory_space=pltpu.VMEM), pl.BlockSpec(memory_space=pl.ANY)
     results = pl.pallas_call(
         functools.partial(layer_kernel, planar, layout),
         out_shape=jax.tree.leaves(outs),
-        in_specs=[far if name in ("in_weight", "out_weight", "cotangent") else vm for name in sorted(args)],
-        out_specs=[vm] * len(outs),
+        in_specs=[far] * len(args),
+        out_specs=[far] * len(outs),
         scratch_shapes=jax.tree.leaves(scratch),
         compiler_params=pltpu.CompilerParams(
             collective_id=0, has_side_effects=True, vmem_limit_bytes=VMEM_LIMIT
@@ -1012,13 +1045,19 @@
         small = results.pop("small_out")
         flat, tree = jax.tree.flatten(results)
         vectors = small.shape[0] - 1
+        line = (width,)
+        targets = [shaped(a.shape, a.dtype) for a in flat] + [shaped(line, wide)] * vectors
+        held = [pltpu.VMEM(a.shape, a.dtype) for a in [small] + flat]
+        lines = [pltpu.VMEM(line, wide)] * vectors
+        sems = dma((2, len(targets)))
+        pieces = ([small] + flat, targets, held, lines, sems)
         flat = pl.pallas_call(
-            functools.partial(hand_on, len(flat), vectors),
-            out_shape=[shaped(a.shape, a.dtype) for a in flat] + [shaped((width,), wide)] * vectors,
-            in_specs=[vm] * (1 + len(flat)),
-            out_specs=[far] * len(flat) + [vm] * vectors,
-            scratch_shapes=[dma((len(flat),))],
-            compiler_params=pltpu.CompilerParams(vmem_limit_bytes=16 * 1024 * 1024),
+            functools.partial(hand_on, jax.tree.structure(pieces)),
+            out_shape=targets,
+            in_specs=[far] * (1 + len(flat)),
+            out_specs=[far] * len(targets),
+            scratch_shapes=held + lines + [sems],
+            compiler_params=pltpu.CompilerParams(vmem_limit_bytes=VMEM_LIMIT),
         )(small, *flat)
         small = flat[len(results) :]
         results = jax.tree.unflatten(tree, flat[: len(results)])

time: 139 us -> 129 us (0.928)
  local copies, waits for them, and re-layouts: 8.73 us -> 0 us
    unnamed x18 -> x0, local copies, waits for them, and re-layouts: 8.73 us -> none
    pallas_call x1, Pallas kernels: 127 us -> 125 us  [local(): pl.pallas_call(functools.partial(layer_kernel, planar, layout), out_shape...]
where the time goes in v5:
time: 129 us
  Pallas kernels  128 us (99%)
    pallas_call x1, Pallas kernels, local(): pl.pallas_call(functools.partial(layer_kernel, planar, layout), out_shape...  125 us
    pallas_call x1, Pallas kernels, local(): pl.pallas_call(functools.partial(hand_on, jax.tree.structure(pieces)), ou...  3.19 us

profile of v5, /device:TPU:0, one launch (start us, length us, event | category | flops | bytes accessed | tf_op | source)
XLA Modules:
  0.0 128.6 jit_solution(1842772587857930496)
XLA Ops:
  0.7 124.5 %shard_map.280 = (f32[96,768]{1,0:T(8,128)}, f32[96,192]{1,0:T(8,128)}, bf16[640,768]{1,0:T(8,128)(2,1)}, f32[192,96]{1,0:T(8,128)}, f32[96,768]{1,0:T(8,128)}, ...) custom-call(bf16[640,768]{1,0:T(8,128)(2,1)} %refs_0_.1, ...), custom_call_target="tpu_custom_call" | custom-call | tf_op jit(solution)/shard_map/pallas_call | solution.py:1033
  125.2 3.2 %shard_map.281 = (f32[96,768]{1,0:T(8,128)}, f32[96,192]{1,0:T(8,128)}, bf16[640,768]{1,0:T(8,128)(2,1)}, f32[192,96]{1,0:T(8,128)}, f32[96,768]{1,0:T(8,128)}, ...) custom-call(f32[8,768]{1,0:T(8,128)} %get-tuple-element.39.refs_0_, ...), custom_call_target="tpu_custom_call" | custom-call | tf_op jit(solution)/shard_map/pallas_call | solution.py:1054

commit v6 on v5

--- a/solution.py
+++ b/solution.py
@@ -49,7 +49,7 @@
         self.at, self.send, self.recv, self.out = place, send, recv, out
 
     def copy(self, block, slot, target):
-        return remote(self.out(block), self.out(block), self.send.at[slot], self.recv.at[block], mp=target)
+        return remote(self.out(block), self.out(block), self.send, self.recv.at[block], mp=target)
 
     def spread(self):
         at = self.at
@@ -82,18 +82,6 @@
             self.copy(at.far_mid, 0, at.mid).wait_recv()
             self.copy(at.far_end, 0, at.mid).wait_recv()
 
-    def drain(self):
-        at = self.at
-
-        @pl.when(at.is_end)
-        def _():
-            self.copy(at.me, 0, at.mid).wait_send()
-
-        @pl.when(at.is_mid)
-        def _():
-            for slot in range(5):
-                self.copy(at.me, slot, at.end).wait_send()
-
 
 class LineReduce:
     def __init__(self, place, part, carry, single, summed, send, recv, start, block_rows, out):
@@ -104,7 +92,7 @@
             return pl.ds(pl.multiple_of(start + block * block_rows, 16), block_rows)
 
         self.rows_of, self.part_ref, self.out_ref = rows_of, part, out
-        self.gather = LineGather(place, send.at[1], recv.at[1], lambda block: out.at[rows_of(block)])
+        self.gather = LineGather(place, send, recv.at[1], lambda block: out.at[rows_of(block)])
 
     def part(self, block):
         return self.part_ref.at[self.rows_of(block)]
@@ -112,17 +100,17 @@
     def end_sends(self):
         at, send, recv = self.at, self.send, self.recv
         return (
-            remote(self.part(at.far_end), self.carry.at[0], send.at[0, 0], recv.at[0, 2], mp=at.mid),
-            remote(self.part(at.far_mid), self.carry.at[1], send.at[0, 1], recv.at[0, 3], mp=at.mid),
-            remote(self.part(at.mid), self.single, send.at[0, 2], recv.at[0, 0], mp=at.mid),
+            remote(self.part(at.far_end), self.carry.at[0], send, recv.at[0, 2], mp=at.mid),
+            remote(self.part(at.far_mid), self.carry.at[1], send, recv.at[0, 3], mp=at.mid),
+            remote(self.part(at.mid), self.single, send, recv.at[0, 0], mp=at.mid),
         )
 
     def mid_sends(self):
         at, send, recv = self.at, self.send, self.recv
         return (
-            remote(self.carry.at[0], self.summed, send.at[0, 1], recv.at[0, 1], mp=at.far_end),
-            remote(self.carry.at[1], self.summed, send.at[0, 2], recv.at[0, 1], mp=at.far_mid),
-            remote(self.part(at.end), self.single, send.at[0, 0], recv.at[0, 0], mp=at.end),
+            remote(self.carry.at[0], self.summed, send, recv.at[0, 1], mp=at.far_end),
+            remote(self.carry.at[1], self.summed, send, recv.at[0, 1], mp=at.far_mid),
+            remote(self.part(at.end), self.single, send, recv.at[0, 0], mp=at.end),
         )
 
     def start(self):
@@ -146,15 +134,18 @@
             self.carry[step] = total.astype(jnp.bfloat16)
             self.mid_sends()[step].start()
 
-    def settle(self, extra=None):
-        at = self.at
+    def total(self):
         self.end_sends()[2].wait_recv()
         self.mid_sends()[0].wait_recv()
-        total = (
-            self.part(at.me)[...].astype(jnp.float32)
+        return (
+            self.part(self.at.me)[...].astype(jnp.float32)
             + self.single[...].astype(jnp.float32)
             + self.summed[...].astype(jnp.float32)
         )
+
+    def settle(self, extra=None):
+        at = self.at
+        total = self.total()
         if extra is not None:
             total = total + extra[self.rows_of(at.me), :]
         self.out_ref[self.rows_of(at.me), :] = total.astype(jnp.bfloat16)
@@ -166,18 +157,38 @@
     def arrive(self):
         self.gather.arrive()
 
+
+class LineSwap:
+    def __init__(self, place, sent, got, send, recv):
+        me = place.me
+        self.me, self.sent, self.got = me, sent, got
+        targets = [lax.rem(me + step, LINE) for step in range(1, LINE)]
+        self.outward = [
+            remote(sent.at[j], got.at[me], send.at[i], recv.at[me], mp=j) for i, j in enumerate(targets)
+        ]
+        self.inward = [remote(got.at[j], got.at[j], send.at[i], recv.at[j], mp=j) for i, j in enumerate(targets)]
+
+    def start(self):
+        for copy in self.outward:
+            copy.start()
+        self.got[self.me] = self.sent[self.me]
+
+    def wait(self):
+        for copy in self.inward:
+            copy.wait_recv()
+
     def drain(self):
-        @pl.when(self.at.is_end)
-        def _():
-            for copy in self.end_sends():
-                copy.wait_send()
-
-        @pl.when(self.at.is_mid)
-        def _():
-            for copy in self.mid_sends():
-                copy.wait_send()
-
-        self.gather.drain()
+        for copy in self.outward:
+            copy.wait_send()
+
+
+def swap_scratch(rows, width, kind):
+    return [
+        pltpu.VMEM((LINE, rows, width), kind),
+        pltpu.VMEM((LINE, rows, width), kind),
+        pltpu.SemaphoreType.DMA((LINE - 1,)),
+        pltpu.SemaphoreType.DMA((LINE,)),
+    ]
 
 
 def line_scratch(rows, width):
@@ -185,7 +196,6 @@
         pltpu.VMEM((2, rows, width), jnp.bfloat16),
         pltpu.VMEM((rows, width), jnp.bfloat16),
         pltpu.VMEM((rows, width), jnp.bfloat16),
-        pltpu.SemaphoreType.DMA((2, 5)),
         pltpu.SemaphoreType.DMA((2, 4)),
     ]
 
@@ -400,10 +410,10 @@
         both = slice(h * pair, (h + 1) * pair)
         qcat[:, both] = jnp.where(entity, q_entity[:, both], q_plain[:, both]).astype(low)
 
-    pt, mx, mloc, st = r.pt, r.mx, r.mloc, r.st
+    pt, mx, st = r.pt, r.mx, r.st
     scale = HD ** (-0.5)
     gathers = [
-        LineGather(at, r.mx_send.at[q], r.mx_recv.at[q], lambda block, q=q: mx[q].at[block])
+        LineGather(at, r.line_send.at[0], r.mx_recv.at[q], lambda block, q=q: mx[q].at[block])
         for q in range(len(spans))
     ]
 
@@ -432,7 +442,6 @@
             lax.fori_loop(0, size // LANES, soften, 0)
             mixed = dot(vt[head_of(h), :], pt[h, :, here]).astype(low)
             mx[q][me, head_of(h), :] = mixed
-            mloc[head_of(h), here] = mixed
             return carry
 
         lax.fori_loop(0, heads, head_step, 0)
@@ -466,18 +475,21 @@
         for h in range(heads):
             vn[h] = vt[h * HD : (h + 1) * HD, :].T
 
-    xh1, rstd1, hl = r.xh1, r.rstd1, r.hl
-    act, gp, dr2, gf, il, gb, tmp, acc = r.act, r.gp, r.dr2, r.gf, r.il, r.gb, r.tmp, r.acc
+    xh1, rstd1, hl, mnat, mown, gbown = r.xh1, r.rstd1, r.hl, r.mnat, r.mown, r.gbown
+    act, gp, dr2, gf, il, tmp, acc = r.act, r.gp, r.dr2, r.gf, r.il, r.tmp, r.acc
     acc[...] = jnp.zeros_like(acc)
 
-    def make_lines(parts, part, out):
-        return [
-            LineReduce(at, part, *parts[q], start, size // LINE, out) for q, (start, size) in enumerate(spans)
-        ]
-
-    ffn = make_lines(r.ffn, r.ffn_part, r.ffn_out)
-    back = make_lines(r.back, r.back_part, r.back_out)
-    grad = make_lines(r.grad, r.grad_part, r.tokens_grad)
+    def make_lines(parts, send, part, out):
+        lines = []
+        for q, (start, size) in enumerate(spans):
+            carry, single, summed, recv = parts[q]
+            lines.append(LineReduce(at, part, carry, single, summed, send, recv, start, size // LINE, out))
+        return lines
+
+    ffn = make_lines(r.ffn, r.line_send.at[1], r.ffn_part, r.ffn_out)
+    back = make_lines(r.back, r.line_send.at[2], r.back_part, r.back_part)
+    swaps = [LineSwap(at, *parts) for parts in r.swap]
+    grad = make_lines(r.grad, r.line_send.at[3], r.grad_part, r.tokens_grad)
 
     root_half = math.sqrt(0.5)
     density = 1.0 / math.sqrt(2.0 * math.pi)
@@ -486,8 +498,11 @@
         gathers[q].arrive()
         start, size = spans[q]
         here = pl.ds(start, size)
-        mixed = mx[q][...].reshape(LINE * local_width, size)
-        tmp[:size, :] = dot(mixed, ow[...].reshape(LINE * local_width, width), 0, 0)
+        mnat[:size, :] = mx[q][...].reshape(LINE * local_width, size).T
+        tmp[:size, :] = dot(mnat[:size, :], ow[...].reshape(LINE * local_width, width))
+        quarter_rows = size // LINE
+        own = pl.ds(pl.multiple_of(me * quarter_rows, 16), quarter_rows)
+        mown[start // LINE : (start + size) // LINE, :] = mnat[own, :]
 
         def first_norm(at_rows, inside):
             value = tmp[inside, :] + tokens[at_rows, :].astype(wide) + o_bias[...]
@@ -547,28 +562,33 @@
     dqa, dqb, dkv, dk_sum, dv_sum = r.dqa, r.dqb, r.dkv, r.dk_sum, r.dv_sum
     dmt, ds = r.dmt, r.ds
 
+    def settle_back(q):
+        start, size = spans[q]
+        own = back[q].rows_of(me)
+        d_hidden = dr2[own, :] + back[q].total()
+        normal = xh1[own, :]
+        acc[2] += fold(d_hidden)
+        acc[1] += fold(d_hidden * normal)
+        grown = d_hidden * gain1[...]
+        grad_in = rstd1[own, 0:1] * (grown - row_mean(grown) - normal * row_mean(grown * normal))
+        acc[0] += fold(grad_in)
+        dr2[own, :] = grad_in
+        grad_low = grad_in.astype(low)
+        gbown[start // LINE : (start + size) // LINE, :] = grad_low
+        for j in range(LINE):
+            swaps[q].sent[j] = dot(grad_low, ow[j], 1, 1).astype(low)
+        swaps[q].start()
+
     def finish_rows(q):
-        back[q].arrive()
+        swaps[q].wait()
         start, size = spans[q]
         here = pl.ds(start, size)
-
-        def last_norm(at_rows, inside):
-            d_hidden = dr2[at_rows, :] + r.back_out[at_rows, :].astype(wide)
-            normal = xh1[at_rows, :]
-            acc[2] += fold(d_hidden)
-            acc[1] += fold(d_hidden * normal)
-            grown = d_hidden * gain1[...]
-            grad_in = rstd1[at_rows, 0:1] * (grown - row_mean(grown) - normal * row_mean(grown * normal))
-            acc[0] += fold(grad_in)
-            dr2[at_rows, :] = grad_in
-            gb[at_rows, :] = grad_in.astype(low)
-
-        rows_loop(start, size, last_norm)
-        dmt[:, here] = dot(r.o_weight[...], gb[here, :], 1, 1).astype(low)
+        for h in range(heads):
+            dmt[h, :size, :] = swaps[q].got[:, :, h * HD : (h + 1) * HD].reshape(size, HD)
 
         def head_step(h, carry):
-            d_mixed = dmt[head_of(h), here]
-            st[:, :size] = dot(vn[h], d_mixed)
+            d_mixed = dmt[h, :size, :]
+            st[:, :size] = dot(vn[h], d_mixed, 1, 1)
 
             def harden(i, carry):
                 cols = pl.ds(pl.multiple_of(i * LANES, LANES), LANES)
@@ -581,7 +601,7 @@
 
             lax.fori_loop(0, size // LANES, harden, 0)
             d_score = ds[:, :size]
-            d_value = dot(pt[h, :, here], d_mixed, 1, 1)
+            d_value = dot(pt[h, :, here], d_mixed)
             d_key = dot(d_score, qcat[here, pair_of(h)])
             if q == 0:
                 dv_sum[h] = d_value
@@ -627,6 +647,10 @@
             small_sum[s] = (small if s == 0 else small_sum.at[s - 1])[...] + r.small_in[s]
             if s < 2:
                 tiny[s + 1].start()
+
+    norms = LineSwap(at, *r.norms)
+    if planar:
+        o_swap = LineSwap(at, *r.o_swap)
 
     def feed_step(i):
         if i == 0:
@@ -642,13 +666,26 @@
         elif planar and i == 5:
             feed_sum = feed.finish()
             r.in_grad[...] = feed_sum[:, :hidden_width]
-            r.out_grad[...] = feed_sum[:, hidden_width:]
+            r.out_grad[...] = feed_sum[:, hidden_width : 2 * hidden_width]
+            for j in range(LINE):
+                begin = 2 * hidden_width + j * local_width
+                o_swap.sent[j] = feed_sum[:, begin : begin + local_width].astype(low)
+            o_swap.start()
             stores["in_grad"].start()
             stores["out_grad"].start()
 
+    def share_norms():
+        for i in range(8):
+            norms.sent[0, i : i + 1, :] = jnp.sum(acc[i], axis=0, keepdims=True)
+        for j in range(1, LINE):
+            norms.sent[j] = norms.sent[0]
+        norms.start()
+        put_grad(gfeed, 2 * hidden_width, dot(gbown[...], mown[...], 0, 0))
+
     def key_grads():
-        for i in range(8):
-            small[i : i + 1, :] = jnp.sum(acc[i], axis=0, keepdims=True)
+        norms.wait()
+        small[...] = norms.sent[0]
+        small[0:3, :] = norms.got[0, 0:3] + norms.got[1, 0:3] + norms.got[2, 0:3] + norms.got[3, 0:3]
         if planar:
             tiny[0].start()
         d_keys = [
@@ -672,9 +709,6 @@
             put_grad(gattn, 2 * local_width, dot(tok_t[...], dqb[...]))
         elif i == 1:
             put_grad(gattn, 4 * local_width, dot(tok_t[...], dkv[...]))
-            o_grad = dot(gb[...], mloc[...], 0, 1)
-            pad = gattn.shape[2] - 7 * local_width
-            put_grad(gattn, 6 * local_width, jnp.concatenate([o_grad, jnp.zeros((width, pad), wide)], axis=1))
         elif planar and i == 2:
             attn.start()
             tiny_step(0)
@@ -687,152 +721,138 @@
 
     attend(0)
     attend(1)
+    attend(2)
+    attend(3)
     gathers[0].relay(0)
+    swap_plane()
     gathers[0].relay(1)
-    swap_plane()
-    attend(2)
+    attend(4)
+    gathers[3].relay(0)
+    gathers[2].relay(0)
+    gathers[3].relay(1)
+    gathers[4].relay(0)
+    gathers[0].relay(2)
     gathers[1].relay(0)
-    gathers[0].relay(2)
-    attend(3)
-    gathers[3].relay(0)
+    gathers[3].relay(2)
+    gathers[2].relay(1)
     gathers[1].relay(1)
+    gathers[4].relay(1)
+    turn()
+    swap_chip()
+    own_weights()
     gathers[1].relay(2)
-    attend(4)
-    gathers[4].relay(0)
-    swap_chip()
-    gathers[3].relay(1)
-    gathers[3].relay(2)
-    gathers[2].relay(0)
-    gathers[4].relay(1)
-    gathers[4].relay(2)
-    gathers[2].relay(1)
-    own_weights()
     forward(0)
     ffn[0].forward(0)
+    gathers[2].relay(2)
+    forward(3)
+    gathers[4].relay(2)
     ffn[0].forward(1)
-    gathers[2].relay(2)
+    ffn[3].forward(0)
     forward(1)
+    ffn[3].forward(1)
+    ffn[0].settle()
     ffn[1].forward(0)
-    forward(3)
-    ffn[3].forward(0)
+    forward(2)
     ffn[1].forward(1)
-    forward(4)
-    ffn[0].settle()
-    ffn[3].forward(1)
-    ffn[4].forward(0)
-    forward(2)
     ffn[0].relay(0)
-    ffn[1].settle()
     ffn[2].forward(0)
+    ffn[3].settle()
     ffn[2].forward(1)
     ffn[0].relay(1)
+    forward(4)
+    ffn[3].relay(0)
+    ffn[4].forward(0)
     ffn[0].relay(2)
-    ffn[1].relay(0)
-    ffn[3].settle()
-    ffn[1].relay(1)
     ffn[4].forward(1)
-    ffn[3].relay(0)
-    ffn[1].relay(2)
+    ffn[1].settle()
     ffn[2].settle()
-    ffn[2].relay(0)
     ffn[3].relay(1)
     ffn[3].relay(2)
+    ffn[1].relay(0)
+    ffn[2].relay(0)
+    ffn[1].relay(1)
     ffn[4].settle()
     ffn[4].relay(0)
+    ffn[1].relay(2)
     ffn[2].relay(1)
     need("cotangent")
     backward(0)
+    ffn[2].relay(2)
+    ffn[4].relay(1)
+    backward(3)
     back[0].forward(0)
-    ffn[2].relay(2)
     back[0].forward(1)
+    ffn[4].relay(2)
     backward(1)
-    ffn[4].relay(1)
+    back[3].forward(0)
+    backward(2)
     back[1].forward(0)
-    backward(3)
+    settle_back(0)
+    back[2].forward(0)
     back[1].forward(1)
-    ffn[4].relay(2)
-    back[3].forward(0)
-    back[0].settle()
-    backward(2)
-    back[0].relay(0)
     back[3].forward(1)
-    back[1].settle()
-    back[2].forward(0)
-    back[2].forward(1)
-    back[0].relay(1)
     backward(4)
     stores["layer_out"].start()
-    back[1].relay(0)
-    back[3].settle()
+    back[2].forward(1)
     feed_step(0)
     back[4].forward(0)
-    back[1].relay(1)
+    settle_back(1)
     back[4].forward(1)
-    back[0].relay(2)
-    back[2].settle()
-    turn()
-    back[1].relay(2)
-    back[3].relay(0)
-    back[2].relay(0)
-    back[4].settle()
-    back[2].relay(1)
     feed_step(1)
-    back[2].relay(2)
-    back[3].relay(1)
-    back[3].relay(2)
+    settle_back(2)
+    settle_back(3)
+    finish_rows(0)
+    settle_back(4)
+    share_norms()
     feed_step(2)
-    back[4].relay(0)
-    finish_rows(0)
-    back[4].relay(1)
     finish_rows(1)
-    back[4].relay(2)
     finish_rows(2)
     finish_rows(3)
     finish_rows(4)
     key_grads()
     input_share(0)
+    feed_step(3)
     input_share(1)
     input_share(2)
+    grad[0].forward(0)
     input_share(3)
-    grad[0].forward(0)
-    feed_step(3)
+    input_share(4)
     grad[0].forward(1)
-    input_share(4)
     attn_step(0)
     grad[1].forward(0)
     grad[1].forward(1)
     attn_step(1)
     grad[2].forward(0)
     grad[2].forward(1)
-    grad[0].settle(dr2)
     attn_step(2)
     grad[3].forward(0)
     grad[3].forward(1)
     grad[2].settle(dr2)
     grad[4].forward(0)
+    grad[0].settle(dr2)
+    feed_step(4)
+    grad[4].forward(1)
     attn_step(3)
-    grad[4].forward(1)
+    grad[3].settle(dr2)
+    grad[2].relay(0)
+    grad[2].relay(1)
     grad[1].settle(dr2)
-    feed_step(4)
-    grad[3].settle(dr2)
     grad[0].relay(0)
     grad[0].relay(1)
     grad[4].settle(dr2)
-    grad[2].relay(0)
     grad[1].relay(0)
-    grad[2].relay(1)
-    grad[1].relay(1)
     grad[3].relay(0)
-    grad[4].relay(0)
-    grad[0].relay(2)
     grad[3].relay(1)
     grad[2].relay(2)
+    grad[4].relay(0)
+    grad[1].relay(1)
+    feed_step(5)
+    grad[4].relay(1)
     attn_step(4)
-    grad[4].relay(1)
     grad[1].relay(2)
     grad[3].relay(2)
     grad[4].relay(2)
-    feed_step(5)
+    grad[0].relay(2)
     if planar:
         attn_sum = attn.finish()
         for part in range(4):
@@ -843,7 +863,10 @@
         both_grads = attn_sum[:, 4 * local_width : 6 * local_width]
         r.k_grad[...] = both_grads[:, :local_width]
         r.v_grad[...] = both_grads[:, local_width:]
-        r.o_grad[...] = attn_sum[:, 6 * local_width : 7 * local_width].T
+        o_swap.wait()
+        o_sum = o_swap.got[0].astype(wide) + o_swap.got[1].astype(wide)
+        r.o_grad[...] = (o_sum + o_swap.got[2].astype(wide) + o_swap.got[3].astype(wide)).T
+        o_swap.drain()
         r.small_out[...] = small_sum[2]
         for name in ("q_grad", "k_grad", "v_grad", "o_grad", "small_out"):
             stores[name].start()
@@ -856,10 +879,28 @@
     for line in grad:
         line.arrive()
     stores["tokens_grad"].start()
-    for line in ffn + back + grad:
-        line.drain()
-    for gather in gathers:
-        gather.drain()
+
+    def sent_all(i, held):
+        remote(held, held, r.line_send.at[i], r.mx_recv.at[0, 0], mp=at.mid).wait_send()
+
+    blocks_out = rows // LINE * 3
+
+    @pl.when(at.is_end)
+    def _():
+        sent_all(0, vt)
+        sent_all(1, hl)
+        sent_all(2, hl.at[:blocks_out])
+        sent_all(3, hl)
+
+    @pl.when(at.is_mid)
+    def _():
+        sent_all(0, xh1.at[: 5 * rows * local_width // (2 * width)])
+        sent_all(1, xh1)
+        sent_all(2, hl.at[:blocks_out])
+        sent_all(3, xh1)
+
+    for swap in swaps + [norms]:
+        swap.drain()
     for copy in ow_line + ow_plane + ow_chip:
         copy.wait_send()
     if planar:
@@ -921,7 +962,8 @@
     spans = portions_of(rows)
     largest = max(size for _, size in spans)
     low, wide = jnp.bfloat16, jnp.float32
-    attn_width = -(-7 * local_width // 128) * 128
+    attn_width = 6 * local_width
+    feed_width = 2 * hidden_width + LINE * local_width
     args = dict(
         tokens=tokens,
         seg_row=segment_ids,
@@ -958,7 +1000,7 @@
         )
     else:
         outs |= dict(
-            feed_out=shaped((blocks, per_block, 2 * hidden_width), low),
+            feed_out=shaped((blocks, per_block, feed_width), low),
             attn_out=shaped((blocks, per_block, attn_width), low),
         )
     dma = pltpu.SemaphoreType.DMA
@@ -978,8 +1020,7 @@
         mx=[pltpu.VMEM((LINE, local_width, size), low) for _, size in spans],
         st=pltpu.VMEM((rows, largest), wide),
         ds=pltpu.VMEM((rows, largest), low),
-        mloc=pltpu.VMEM((local_width, rows), low),
-        mx_send=dma((len(spans), 5)),
+        line_send=dma((4,)),
         mx_recv=dma((len(spans), LINE)),
         tok_t=pltpu.VMEM((width, rows), low),
         xh1=pltpu.VMEM((rows, width), wide),
@@ -993,18 +1034,21 @@
         tmp=pltpu.VMEM((largest, width), wide),
         vec=pltpu.VMEM((8, width), wide),
         acc=pltpu.VMEM((8, 8, width), wide),
-        gb=pltpu.VMEM((rows, width), low),
+        mnat=pltpu.VMEM((largest, LINE * local_width), low),
+        mown=pltpu.VMEM((rows // LINE, LINE * local_width), low),
+        gbown=pltpu.VMEM((rows // LINE, width), low),
+        swap=[swap_scratch(size // LINE, local_width, low) for _, size in spans],
+        norms=swap_scratch(8, width, wide),
         ffn_part=pltpu.VMEM((rows, width), low),
         back_part=pltpu.VMEM((rows, width), low),
         grad_part=pltpu.VMEM((rows, width), low),
         ffn_out=pltpu.VMEM((rows, width), low),
-        back_out=pltpu.VMEM((rows, width), low),
-        gfeed=pltpu.VMEM((blocks, per_block, 2 * hidden_width), low),
+        gfeed=pltpu.VMEM((blocks, per_block, feed_width), low),
         gattn=pltpu.VMEM((blocks, per_block, attn_width), low),
         small=pltpu.VMEM((8, width), wide),
         kct=pltpu.VMEM((2 * local_width, rows), low),
         vn=pltpu.VMEM((heads, rows, HD), low),
-        dmt=pltpu.VMEM((local_width, rows), low),
+        dmt=pltpu.VMEM((heads, largest, HD), low),
         dk_sum=pltpu.VMEM((heads, rows, 2 * HD), wide),
         dv_sum=pltpu.VMEM((heads, rows, HD), wide),
         dqa=pltpu.VMEM((rows, 2 * local_width), low),
@@ -1015,7 +1059,8 @@
         scratch[name] = [line_scratch(size // LINE, width) for _, size in spans]
     if planar:
         scratch |= dict(
-            feed=plane_scratch(per_block, 2 * hidden_width),
+            feed=plane_scratch(per_block, feed_width),
+            o_swap=swap_scratch(per_block, local_width, low),
             attn=plane_scratch(per_block, attn_width),
             small_in=pltpu.VMEM((3, 8, width), wide),
             small_sum=pltpu.VMEM((3, 8, width), wide),
@@ -1065,21 +1110,22 @@
     if planar:
         grads = (res.q_grad, res.k_grad, res.v_grad, res.o_grad, res.in_grad, res.out_grad.T)
     else:
-        feed = res.feed_out.astype(wide).reshape(width, 2 * hidden_width)
+        feed = res.feed_out.astype(wide).reshape(width, feed_width)
         attn = res.attn_out.astype(wide).reshape(width, attn_width)
         feed = lax.psum_scatter(feed, "dp", scatter_dimension=0, tiled=True)
         attn = lax.psum_scatter(attn, "dp", scatter_dimension=0, tiled=True)
         small = lax.psum(res.small_out, "dp")
         per = feed.shape[0]
+        o_part = lax.psum_scatter(feed[:, 2 * hidden_width :], "mp", scatter_dimension=1, tiled=True)
         queries = attn[:, : 4 * local_width].reshape(per, 2, heads, 2, HD)
         queries = queries.transpose(1, 3, 0, 2, 4).reshape(4, per, local_width)
         grads = (
             queries,
             attn[:, 4 * local_width : 5 * local_width],
             attn[:, 5 * local_width : 6 * local_width],
-            attn[:, 6 * local_width : 7 * local_width].T,
+            o_part.T,
             feed[:, :hidden_width],
-            feed[:, hidden_width:].T,
+            feed[:, hidden_width : 2 * hidden_width].T,
         )
     d_q, d_k, d_v, d_o, d_in, d_out = grads
     return (

time: 129 us -> 126 us (0.977)
  Pallas kernels: 128 us -> 125 us
    pallas_call x1, Pallas kernels: 125 us -> 122 us  [local(): pl.pallas_call(functools.partial(layer_kernel, planar, layout), out_shape...]
where the time goes in v6:
time: 126 us
  Pallas kernels  125 us (99%)
    pallas_call x1, Pallas kernels, local(): pl.pallas_call(functools.partial(layer_kernel, planar, layout), out_shape...  122 us
    pallas_call x1, Pallas kernels, local(): pl.pallas_call(functools.partial(hand_on, jax.tree.structure(pieces)), ou...  3.19 us

profile of v6, /device:TPU:0, one launch (start us, length us, event | category | flops | bytes accessed | tf_op | source)
XLA Modules:
  0.0 125.8 jit_solution(11252810888569353785)
XLA Ops:
  0.7 121.8 %shard_map.280 = (f32[96,768]{1,0:T(8,128)}, f32[96,192]{1,0:T(8,128)}, bf16[640,768]{1,0:T(8,128)(2,1)}, f32[192,96]{1,0:T(8,128)}, f32[96,768]{1,0:T(8,128)}, ...) custom-call(bf16[640,768]{1,0:T(8,128)(2,1)} %refs_0_.1, ...), custom_call_target="tpu_custom_call" | custom-call | tf_op jit(solution)/shard_map/pallas_call | solution.py:1078
  122.5 3.2 %shard_map.281 = (f32[96,768]{1,0:T(8,128)}, f32[96,192]{1,0:T(8,128)}, bf16[640,768]{1,0:T(8,128)(2,1)}, f32[192,96]{1,0:T(8,128)}, f32[96,768]{1,0:T(8,128)}, ...) custom-call(f32[8,768]{1,0:T(8,128)} %get-tuple-element.39.refs_0_, ...), custom_call_target="tpu_custom_call" | custom-call | tf_op jit(solution)/shard_map/pallas_call | solution.py:1099

commit v7 on v6

--- a/solution.py
+++ b/solution.py
@@ -300,7 +300,7 @@
         body(pl.ds(pl.multiple_of(start + i * CHUNK, CHUNK), CHUNK), inside)
         return carry
 
-    lax.fori_loop(0, count // CHUNK, step, 0)
+    lax.fori_loop(0, count // CHUNK, step, 0, unroll=True)
 
 
 def fold(value):
@@ -439,12 +439,12 @@
                 pt[h, :, span] = (shifted * (1.0 / total)).astype(low)
                 return carry
 
-            lax.fori_loop(0, size // LANES, soften, 0)
+            lax.fori_loop(0, size // LANES, soften, 0, unroll=True)
             mixed = dot(vt[head_of(h), :], pt[h, :, here]).astype(low)
             mx[q][me, head_of(h), :] = mixed
             return carry
 
-        lax.fori_loop(0, heads, head_step, 0)
+        lax.fori_loop(0, heads, head_step, 0, unroll=True)
         gathers[q].spread()
 
     def swap_plane():
@@ -599,7 +599,7 @@
                 ds[:, cols] = (prob * (d_prob - delta) * scale).astype(low)
                 return carry
 
-            lax.fori_loop(0, size // LANES, harden, 0)
+            lax.fori_loop(0, size // LANES, harden, 0, unroll=True)
             d_score = ds[:, :size]
             d_value = dot(pt[h, :, here], d_mixed)
             d_key = dot(d_score, qcat[here, pair_of(h)])
@@ -615,7 +615,7 @@
             dqb[here, pair_of(h)] = jnp.where(row_entity, d_query, 0.0).astype(low)
             return carry
 
-        lax.fori_loop(0, heads, head_step, 0)
+        lax.fori_loop(0, heads, head_step, 0, unroll=True)
 
     gfeed, gattn = r.gfeed, r.gattn
     blocks, per_block = gfeed.shape[0], gfeed.shape[1]

time: 126 us -> 124 us (0.984)
  Pallas kernels: 125 us -> 123 us
    pallas_call x1, Pallas kernels: 122 us -> 119 us  [local(): pl.pallas_call(functools.partial(layer_kernel, planar, layout), out_shape...]
where the time goes in v7:
time: 124 us; the launch traced here: 123 us
  Pallas kernels  123 us (99%)
    pallas_call x1, Pallas kernels, local(): pl.pallas_call(functools.partial(layer_kernel, planar, layout), out_shape...  119 us
    pallas_call x1, Pallas kernels, local(): pl.pallas_call(functools.partial(hand_on, jax.tree.structure(pieces)), ou...  3.19 us

profile of v7, /device:TPU:0, one launch (start us, length us, event | category | flops | bytes accessed | tf_op | source)
XLA Modules:
  0.0 123.4 jit_solution(6011121992382133244)
XLA Ops:
  0.7 119.4 %shard_map.280 = (f32[96,768]{1,0:T(8,128)}, f32[96,192]{1,0:T(8,128)}, bf16[640,768]{1,0:T(8,128)(2,1)}, f32[192,96]{1,0:T(8,128)}, f32[96,768]{1,0:T(8,128)}, ...) custom-call(bf16[640,768]{1,0:T(8,128)(2,1)} %refs_0_.1, ...), custom_call_target="tpu_custom_call" | custom-call | tf_op jit(solution)/shard_map/pallas_call | solution.py:1078
  120.0 3.2 %shard_map.281 = (f32[96,768]{1,0:T(8,128)}, f32[96,192]{1,0:T(8,128)}, bf16[640,768]{1,0:T(8,128)(2,1)}, f32[192,96]{1,0:T(8,128)}, f32[96,768]{1,0:T(8,128)}, ...) custom-call(f32[8,768]{1,0:T(8,128)} %get-tuple-element.39.refs_0_, ...), custom_call_target="tpu_custom_call" | custom-call | tf_op jit(solution)/shard_map/pallas_call | solution.py:1099

commit v8 on v7

--- a/solution.py
+++ b/solution.py
@@ -724,84 +724,84 @@
     attend(2)
     attend(3)
     gathers[0].relay(0)
+    gathers[2].relay(0)
+    gathers[0].relay(1)
+    gathers[1].relay(0)
     swap_plane()
-    gathers[0].relay(1)
     attend(4)
+    gathers[1].relay(1)
+    gathers[4].relay(0)
     gathers[3].relay(0)
-    gathers[2].relay(0)
+    gathers[0].relay(2)
+    gathers[2].relay(1)
+    gathers[1].relay(2)
+    swap_chip()
+    gathers[2].relay(2)
+    gathers[4].relay(1)
+    gathers[4].relay(2)
+    own_weights()
+    forward(0)
     gathers[3].relay(1)
-    gathers[4].relay(0)
-    gathers[0].relay(2)
-    gathers[1].relay(0)
+    ffn[0].forward(0)
     gathers[3].relay(2)
-    gathers[2].relay(1)
-    gathers[1].relay(1)
-    gathers[4].relay(1)
-    turn()
-    swap_chip()
-    own_weights()
-    gathers[1].relay(2)
-    forward(0)
-    ffn[0].forward(0)
-    gathers[2].relay(2)
-    forward(3)
-    gathers[4].relay(2)
+    forward(2)
     ffn[0].forward(1)
-    ffn[3].forward(0)
+    ffn[2].forward(0)
     forward(1)
-    ffn[3].forward(1)
     ffn[0].settle()
     ffn[1].forward(0)
-    forward(2)
+    forward(4)
+    ffn[2].forward(1)
     ffn[1].forward(1)
+    forward(3)
     ffn[0].relay(0)
-    ffn[2].forward(0)
-    ffn[3].settle()
-    ffn[2].forward(1)
+    ffn[4].forward(0)
+    ffn[4].forward(1)
     ffn[0].relay(1)
-    forward(4)
-    ffn[3].relay(0)
-    ffn[4].forward(0)
+    ffn[1].settle()
+    ffn[3].forward(0)
+    ffn[3].forward(1)
     ffn[0].relay(2)
-    ffn[4].forward(1)
-    ffn[1].settle()
-    ffn[2].settle()
-    ffn[3].relay(1)
-    ffn[3].relay(2)
     ffn[1].relay(0)
-    ffn[2].relay(0)
     ffn[1].relay(1)
     ffn[4].settle()
+    ffn[2].settle()
+    turn()
     ffn[4].relay(0)
     ffn[1].relay(2)
-    ffn[2].relay(1)
+    ffn[3].settle()
+    ffn[2].relay(0)
+    ffn[4].relay(1)
     need("cotangent")
     backward(0)
+    ffn[3].relay(0)
+    ffn[4].relay(2)
+    ffn[2].relay(1)
     ffn[2].relay(2)
-    ffn[4].relay(1)
-    backward(3)
+    ffn[3].relay(1)
+    backward(1)
     back[0].forward(0)
     back[0].forward(1)
-    ffn[4].relay(2)
-    backward(1)
+    ffn[3].relay(2)
+    backward(4)
+    back[1].forward(0)
+    backward(2)
+    back[1].forward(1)
+    settle_back(0)
+    backward(3)
+    stores["layer_out"].start()
+    back[4].forward(0)
+    feed_step(0)
+    back[2].forward(0)
+    back[2].forward(1)
+    settle_back(1)
     back[3].forward(0)
-    backward(2)
-    back[1].forward(0)
-    settle_back(0)
-    back[2].forward(0)
-    back[1].forward(1)
+    feed_step(1)
     back[3].forward(1)
-    backward(4)
-    stores["layer_out"].start()
-    back[2].forward(1)
-    feed_step(0)
-    back[4].forward(0)
-    settle_back(1)
     back[4].forward(1)
-    feed_step(1)
+    finish_rows(0)
     settle_back(2)
     settle_back(3)
-    finish_rows(0)
     settle_back(4)
     share_norms()
     feed_step(2)
@@ -822,37 +822,37 @@
     grad[1].forward(0)
     grad[1].forward(1)
     attn_step(1)
+    attn_step(2)
+    grad[0].settle(dr2)
     grad[2].forward(0)
     grad[2].forward(1)
-    attn_step(2)
+    feed_step(4)
     grad[3].forward(0)
     grad[3].forward(1)
+    grad[1].settle(dr2)
+    attn_step(3)
+    grad[4].forward(0)
     grad[2].settle(dr2)
-    grad[4].forward(0)
-    grad[0].settle(dr2)
-    feed_step(4)
     grad[4].forward(1)
-    attn_step(3)
     grad[3].settle(dr2)
+    feed_step(5)
+    grad[1].relay(0)
+    grad[1].relay(1)
+    grad[0].relay(0)
     grad[2].relay(0)
+    grad[0].relay(1)
     grad[2].relay(1)
-    grad[1].settle(dr2)
-    grad[0].relay(0)
-    grad[0].relay(1)
+    grad[3].relay(0)
     grad[4].settle(dr2)
-    grad[1].relay(0)
-    grad[3].relay(0)
+    grad[1].relay(2)
+    grad[4].relay(0)
     grad[3].relay(1)
+    grad[0].relay(2)
+    attn_step(4)
+    grad[3].relay(2)
+    grad[4].relay(1)
+    grad[4].relay(2)
     grad[2].relay(2)
-    grad[4].relay(0)
-    grad[1].relay(1)
-    feed_step(5)
-    grad[4].relay(1)
-    attn_step(4)
-    grad[1].relay(2)
-    grad[3].relay(2)
-    grad[4].relay(2)
-    grad[0].relay(2)
     if planar:
         attn_sum = attn.finish()
         for part in range(4):

time: 124 us -> 123 us (level)
  no operation moved by 1% of the time
where the time goes in v8:
time: 123 us; the launch traced here: 122 us
  Pallas kernels  122 us (99%)
    pallas_call x1, Pallas kernels, local(): pl.pallas_call(functools.partial(layer_kernel, planar, layout), out_shape...  118 us
    pallas_call x1, Pallas kernels, local(): pl.pallas_call(functools.partial(hand_on, jax.tree.structure(pieces)), ou...  3.19 us

profile of v8, /device:TPU:0, one launch (start us, length us, event | category | flops | bytes accessed | tf_op | source)
XLA Modules:
  0.0 122.5 jit_solution(5385553592975222103)
XLA Ops:
  0.7 118.4 %shard_map.280 = (f32[96,768]{1,0:T(8,128)}, f32[96,192]{1,0:T(8,128)}, bf16[640,768]{1,0:T(8,128)(2,1)}, f32[192,96]{1,0:T(8,128)}, f32[96,768]{1,0:T(8,128)}, ...) custom-call(bf16[640,768]{1,0:T(8,128)(2,1)} %refs_0_.1, ...), custom_call_target="tpu_custom_call" | custom-call | tf_op jit(solution)/shard_map/pallas_call | solution.py:1078
  119.1 3.2 %shard_map.281 = (f32[96,768]{1,0:T(8,128)}, f32[96,192]{1,0:T(8,128)}, bf16[640,768]{1,0:T(8,128)(2,1)}, f32[192,96]{1,0:T(8,128)}, f32[96,768]{1,0:T(8,128)}, ...) custom-call(f32[8,768]{1,0:T(8,128)} %get-tuple-element.39.refs_0_, ...), custom_call_target="tpu_custom_call" | custom-call | tf_op jit(solution)/shard_map/pallas_call | solution.py:1099
